TPU v7x, 256 devices: a whole 4x4x8 slice. The times are simulated.
256 devices in a mesh: fsdp: 32 (over z, y), rep: 8 (over x, core).
Axes of the slice: x: 4, y: 4, z: 8, core: 2. Of those that a mesh axis runs over, the one named last changes fastest.
Arguments:
- hidden: bfloat16 [65536, 2048], P(('fsdp', 'rep')), may hold values from -6 to 6
- attn_gain: bfloat16 [2048], P(('fsdp', 'rep')), may hold values from 0.25 to 1.75
- w_query: bfloat16 [2048, 2048], P(('fsdp', 'rep')), as said below
- w_key: bfloat16 [2048, 512], P(('fsdp', 'rep')), as said below
- w_value: bfloat16 [2048, 512], P(('fsdp', 'rep')), may hold values from -0.125 to 0.125
- w_out: bfloat16 [2048, 2048], P(None, ('fsdp', 'rep')), may hold values from -0.125 to 0.125
Outputs:
- mixed: bfloat16 [65536, 2048], P(('fsdp', 'rep'))
Inputs may be any that keep to these rules, and one draw needn't show every extreme that they name: `w_query`: entries of order 2048^(-1/2). `w_key`: entries of order 2048^(-1/2) times a factor up to twenty.
All inputs are finite; a program needn't handle non-finite values.
Results may differ from a plain program's by a relative error of at most 0.012.
The roundings to bfloat16 on the way count: a program that leaves them out, or rounds other values in their place, can miss the bound.
Values may be sent and summed in bfloat16 or wider, within the bound.
No kernel may reach another device: no remote copies, remote signals or barrier semaphores. Data moves between devices by JAX's collectives and lax.ppermute only.
A program may use at most 64 MiB of HBM per device.

v0:
```python
import jax
import jax.numpy as jnp
from jax import lax
from jax.sharding import PartitionSpec as P

HD = 64


rope_base = 500000.0
norm_eps = 1e-05


def sent_together(arrays, axis, dim, along):
    columns = [a.reshape(*a.shape[:along], -1) for a in arrays]
    both = jnp.concatenate(columns, axis=along)
    filled, at, gathered = (lax.all_gather(both, axis, axis=dim, tiled=True), 0, [])
    for a, column in zip(arrays, columns):
        piece = filled[..., at : at + column.shape[along]]
        gathered.append(piece.reshape(*piece.shape[:along], *a.shape[along:]))
        at += column.shape[along]
    return tuple(gathered)


def copy_for_each(array, axis):
    copies = jnp.broadcast_to(array, (lax.axis_size(axis), *array.shape))
    return lax.all_to_all(copies, axis, split_axis=0, concat_axis=0, tiled=True)


def laid_out(blocks, dim):
    blocks = jnp.moveaxis(blocks, 0, dim)
    dims = blocks.shape
    return blocks.reshape(*dims[:dim], dims[dim] * dims[dim + 1], *dims[dim + 2 :])


def gather_directly(array, axis, dim):
    blocks = copy_for_each(array, axis)
    return laid_out(blocks, dim)


def rope_tables(tokens, head_dim):
    position = jnp.arange(tokens, dtype=jnp.float32)
    freq = rope_base ** (-(jnp.arange(head_dim // 2, dtype=jnp.float32) * 2.0) / head_dim)
    angle = position[:, None] * freq[None, :]
    cos_table = jnp.concatenate([jnp.cos(angle), jnp.cos(angle)], axis=-1)
    sin_table = jnp.concatenate([jnp.sin(angle), jnp.sin(angle)], axis=-1)
    return (cos_table, sin_table)


def rotate(tensor, cos_table, sin_table):
    half = tensor.shape[-1] // 2
    turned = jnp.concatenate([-tensor[..., half:], tensor[..., :half]], axis=-1)
    return tensor * cos_table + turned * sin_table


def body(hidden, attn_gain, w_query, w_key, w_value, w_out):
    tokens = hidden.shape[0]
    head_dim = HD
    width_query = w_query.shape[1]
    width_kv = w_key.shape[1]
    kv_count = width_kv // head_dim
    group = width_query // width_kv
    x_float = hidden.astype(jnp.float32)
    inv_rms = lax.rsqrt(jnp.mean(x_float * x_float, axis=-1, keepdims=True) + norm_eps)
    grouped = sent_together((attn_gain, w_query, w_key, w_value), "rep", 0, 1)
    gain_piece, query_piece, key_piece, value_piece = sent_together(
        (grouped[0], grouped[1], grouped[2], grouped[3]), "fsdp", 0, 1
    )
    normed = (x_float * inv_rms * gain_piece.astype(jnp.float32)[None, :]).astype(jnp.bfloat16)
    queries = jnp.dot(normed, query_piece, preferred_element_type=jnp.float32)
    keys_raw = jnp.dot(normed, key_piece, preferred_element_type=jnp.float32)
    values_raw = jnp.dot(normed, value_piece, preferred_element_type=jnp.float32)
    cos_table, sin_table = rope_tables(tokens, head_dim)
    queries = queries.reshape(tokens, kv_count, group, head_dim)
    keys_raw = keys_raw.reshape(tokens, kv_count, head_dim)
    values_bf = values_raw.reshape(tokens, kv_count, head_dim).astype(jnp.bfloat16)
    rope_queries = rotate(queries, cos_table[:, None, None, :], sin_table[:, None, None, :]).astype(
        jnp.bfloat16
    )
    rope_keys = rotate(keys_raw, cos_table[:, None, :], sin_table[:, None, :]).astype(jnp.bfloat16)
    scores = jnp.einsum(
        "qkgd,skd->kgqs", rope_queries, rope_keys, preferred_element_type=jnp.float32
    ) * head_dim ** (-0.5)
    causal = jnp.arange(tokens)[:, None] >= jnp.arange(tokens)[None, :]
    scores = jnp.where(causal[None, None, :, :], scores, -1e30)
    top = jnp.max(scores, axis=-1, keepdims=True)
    expo = jnp.exp(scores - top)
    probs = (expo / jnp.sum(expo, axis=-1, keepdims=True)).astype(jnp.bfloat16)
    context = jnp.einsum("kgqs,skd->qkgd", probs, values_bf, preferred_element_type=jnp.float32)
    context = context.reshape(tokens, width_query).astype(jnp.bfloat16)
    grouped_cols = gather_directly(w_out, "rep", 1)
    branch = jnp.dot(
        context,
        lax.all_gather(grouped_cols, "fsdp", axis=1, tiled=True),
        preferred_element_type=jnp.float32,
    )
    return (x_float + branch).astype(jnp.bfloat16)


def solution(mesh):
    placed = (
        P(("fsdp", "rep"), None),
        P(("fsdp", "rep")),
        P(("fsdp", "rep"), None),
        P(("fsdp", "rep"), None),
        P(("fsdp", "rep"), None),
        P(None, ("fsdp", "rep")),
    )
    return jax.shard_map(
        body, mesh=mesh, in_specs=placed, out_specs=P(("fsdp", "rep"), None), check_vma=False
    )
```

profile of v0, /device:TPU:1, one launch (start us, length us, event | category | flops | bytes accessed | tf_op | source)
XLA Modules:
  0.0 258.1 jit_solution(10988606192208036558)
XLA Ops:
  6.5 0.0 copy-start
  6.5 0.0 all-gather.3.cloned.1.call-start
  6.5 0.8 copy.17
  7.4 0.9 concatenate.17
  8.2 17.1 %all_gather.9 = bf16[64,3073]{1,0:T(8,128)(2,1)} all-gather(bf16[8,3073]{1,0:T(8,128)(2,1)S(1)} %concatenate.17), channel_id=1, replica_groups=mesh['fsdp'=32,'rep'=8] {'rep'}, dimensions={0}, use_global_device_ids=true | all-gather | bytes 442512 | tf_op jit(solution)/shard_map/all_gather | solution.py:16
  25.4 0.0 all-gather.3.cloned.1.call-update
  25.4 0.0 all-gather.5.cloned.1.call-start
  25.4 0.8 broadcast_in_dim.12
  26.2 9.7 %all_to_all.5 = bf16[8,2048,8]{1,2,0:T(8,128)(2,1)} all-to-all(bf16[8,2048,8]{1,2,0:T(8,128)(2,1)S(1)} %broadcast_in_dim.12), channel_id=1, replica_groups=mesh['fsdp'=32,'rep'=8] {'rep'}, dimensions={0} | all-to-all | bytes 524288 | tf_op jit(solution)/shard_map/all_to_all | solution.py:26
  35.9 0.0 all-gather.5.cloned.1.call-update
  36.0 0.2 fusion.33
  36.2 0.0 copy-done
  36.2 0.3 fusion.9
  36.5 110.4 %all-gather.3.cloned.1.call-done = bf16[2048,3073]{1,0:T(8,128)(2,1)} async-done(((bf16[64,3073]{1,0:T(8,128)(2,1)}), bf16[2048,3073]{1,0:T(8,128)(2,1)}) %all-gather.3.cloned.1.call-update) | async-done | bytes 12587024 | tf_op jit(solution)/shard_map/all_gather | solution.py:16
  146.9 1.3 convert_reduce_fusion
  148.2 2.9 %fusion.19 = bf16[256,512]{1,0:T(8,128)(2,1)S(1)} fusion(bf16[2048,3073]{1,0:T(8,128)(2,1)} %all-gather.3.cloned.1.call-done, bf16[256,2048]{1,0:T(8,128)(2,1)S(1)} %copy-done, f32[2048]{0:T(1024)S(1)} %convert_reduce_fusion, f32[256]{0:T(256)S(1)} %add_rsqrt_fusion), kind=kOutput, calls=%fused_computation.26 | convolution fusion | flops 539099136 | bytes 3417088 | tf_op jit(solution)/shard_map/dot_general | solution.py:71
  151.0 0.1 copy.18
  151.2 3.7 %fusion.12 = f32[256,512]{0,1:T(8,128)S(1)} fusion(bf16[2048,3073]{1,0:T(8,128)(2,1)} %all-gather.3.cloned.1.call-done, bf16[256,2048]{1,0:T(8,128)(2,1)S(1)} %copy-done, f32[2048]{0:T(1024)S(1)} %convert_reduce_fusion, f32[256]{0:T(256)S(1)} %add_rsqrt_fusion), kind=kOutput, calls=%fused_computation.18 | convolution fusion | flops 538968064 | bytes 3679232 | tf_op jit(solution)/shard_map/dot_general | solution.py:70
  154.9 10.6 %fusion.1 = f32[256,2048]{0,1:T(8,128)S(1)} fusion(bf16[2048,3073]{1,0:T(8,128)(2,1)} %all-gather.3.cloned.1.call-done, bf16[256,2048]{1,0:T(8,128)(2,1)S(1)} %copy-done, f32[2048]{0:T(1024)S(1)} %convert_reduce_fusion, f32[256]{0:T(256)S(1)} %add_rsqrt_fusion), kind=kOutput, calls=%fused_computation.1 | convolution fusion | flops 2149580800 | bytes 11543552 | tf_op jit(solution)/shard_map/dot_general | solution.py:69
  165.5 0.2 slice_negate_fusion
  165.7 1.5 fusion.22
  167.2 2.3 fusion.40
  169.5 0.9 fusion.18
  170.4 74.1 %all-gather.5.cloned.1.call-done = bf16[2048,2048]{0,1:T(8,128)(2,1)} async-done(((bf16[2048,64]{0,1:T(8,128)(2,1)}), bf16[2048,2048]{0,1:T(8,128)(2,1)}) %all-gather.5.cloned.1.call-update) | async-done | bytes 8388624 | tf_op jit(solution)/shard_map/all_gather | solution.py:93
  244.5 6.7 %fusion.8 = bf16[256,2048]{1,0:T(8,128)(2,1)} fusion(bf16[256,2048]{0,1:T(8,128)(2,1)S(1)} %bitcast.40, bf16[2048,2048]{0,1:T(8,128)(2,1)} %all-gather.5.cloned.1.call-done, bf16[256,2048]{1,0:T(8,128)(2,1)S(1)} %copy-done), kind=kOutput, calls=%fused_computation.14 | convolution fusion | flops 2149056512 | bytes 11534336 | tf_op jit(solution)/shard_map/dot_general | solution.py:91
  (5 shorter events, 0.1 us)
Async XLA Ops:
  6.5 29.7 %copy-start = (bf16[256,2048]{1,0:T(8,128)(2,1)S(1)}, bf16[256,2048]{1,0:T(8,128)(2,1)}, u32[]{:S(2)}) copy-start(bf16[256,2048]{1,0:T(8,128)(2,1)} %param.6) | copy-start | bytes 3145732
  6.5 140.4 %all-gather.3.cloned.1.call-start = ((), (), s32[]{:S(2)}) async-start(), calls=%async_computation.1 | async-start | bytes 13516800 | tf_op jit(solution)/shard_map/all_gather | solution.py:16
  25.4 219.1 %all-gather.5.cloned.1.call-start = ((), (), s32[]{:S(2)}) async-start(), calls=%async_computation.2 | async-start | bytes 8650752 | tf_op jit(solution)/shard_map/all_gather | solution.py:93
Sparse Core Ops, SparseCore 0:
  25.5 121.3 all-gather.2
  149.5 94.9 all-gather.4
where the time goes:
time: 258 us
  waiting for transfers between devices  184 us (71%)
  blocking collectives  26.8 us (10%)
  matrix products  26.3 us (10%)
  between operations  13.5 us (5%)
  other arithmetic  4.28 us (2%)
  local copies, waits for them, and re-layouts  2.62 us (1%)
    all_gather x1, waiting for transfers between devices, sent_together(): lax.all_gather(both, axis, axis=dim, tiled=True)  110 us
    all_gather x1, waiting for transfers between devices, body(): lax.all_gather(grouped_cols, 'fsdp', axis=1, tiled=True)  74.1 us
    all_gather x1, blocking collectives, sent_together(): lax.all_gather(both, axis, axis=dim, tiled=True)  17.1 us
    dot_general x1, matrix products, body(): queries = jnp.dot(normed, query_piece, preferred_element_type=jnp.float32)  10.6 us
    all_to_all x1, blocking collectives, copy_for_each(): return lax.all_to_all(copies, axis, split_axis=0, concat_axis=0, tiled=True)  9.7 us
    dot_general x1, matrix products, body(): jnp.dot(context, lax.all_gather(grouped_cols, 'fsdp', axis=1, tiled=True)...  6.74 us
  transfers between devices with their start and end apart: 2, of which 2 were waited for; matrix products, arithmetic and copies ran while one was open for 10% of the time, Pallas kernels for 0%

commit v1 on v0

--- a/solution.py
+++ b/solution.py
@@ -4,37 +4,10 @@
 from jax.sharding import PartitionSpec as P
 
 HD = 64
-
+PAD = 128
 
 rope_base = 500000.0
 norm_eps = 1e-05
-
-
-def sent_together(arrays, axis, dim, along):
-    columns = [a.reshape(*a.shape[:along], -1) for a in arrays]
-    both = jnp.concatenate(columns, axis=along)
-    filled, at, gathered = (lax.all_gather(both, axis, axis=dim, tiled=True), 0, [])
-    for a, column in zip(arrays, columns):
-        piece = filled[..., at : at + column.shape[along]]
-        gathered.append(piece.reshape(*piece.shape[:along], *a.shape[along:]))
-        at += column.shape[along]
-    return tuple(gathered)
-
-
-def copy_for_each(array, axis):
-    copies = jnp.broadcast_to(array, (lax.axis_size(axis), *array.shape))
-    return lax.all_to_all(copies, axis, split_axis=0, concat_axis=0, tiled=True)
-
-
-def laid_out(blocks, dim):
-    blocks = jnp.moveaxis(blocks, 0, dim)
-    dims = blocks.shape
-    return blocks.reshape(*dims[:dim], dims[dim] * dims[dim + 1], *dims[dim + 2 :])
-
-
-def gather_directly(array, axis, dim):
-    blocks = copy_for_each(array, axis)
-    return laid_out(blocks, dim)
 
 
 def rope_tables(tokens, head_dim):
@@ -61,10 +34,16 @@
     group = width_query // width_kv
     x_float = hidden.astype(jnp.float32)
     inv_rms = lax.rsqrt(jnp.mean(x_float * x_float, axis=-1, keepdims=True) + norm_eps)
-    grouped = sent_together((attn_gain, w_query, w_key, w_value), "rep", 0, 1)
-    gain_piece, query_piece, key_piece, value_piece = sent_together(
-        (grouped[0], grouped[1], grouped[2], grouped[3]), "fsdp", 0, 1
-    )
+    gain_column = jnp.broadcast_to(attn_gain[:, None], (attn_gain.shape[0], PAD))
+    rows = jnp.concatenate([w_query, w_key, w_value, w_out.T, gain_column], axis=1)
+    every = lax.all_gather(rows, ("fsdp", "rep"), axis=0, tiled=True)
+    at = 0
+    pieces = []
+    for width in (width_query, width_kv, width_kv, w_out.shape[0]):
+        pieces.append(every[:, at : at + width])
+        at += width
+    query_piece, key_piece, value_piece, out_piece = pieces
+    gain_piece = every[:, at]
     normed = (x_float * inv_rms * gain_piece.astype(jnp.float32)[None, :]).astype(jnp.bfloat16)
     queries = jnp.dot(normed, query_piece, preferred_element_type=jnp.float32)
     keys_raw = jnp.dot(normed, key_piece, preferred_element_type=jnp.float32)
@@ -87,11 +66,8 @@
     probs = (expo / jnp.sum(expo, axis=-1, keepdims=True)).astype(jnp.bfloat16)
     context = jnp.einsum("kgqs,skd->qkgd", probs, values_bf, preferred_element_type=jnp.float32)
     context = context.reshape(tokens, width_query).astype(jnp.bfloat16)
-    grouped_cols = gather_directly(w_out, "rep", 1)
-    branch = jnp.dot(
-        context,
-        lax.all_gather(grouped_cols, "fsdp", axis=1, tiled=True),
-        preferred_element_type=jnp.float32,
+    branch = lax.dot_general(
+        context, out_piece, (((1,), (1,)), ((), ())), preferred_element_type=jnp.float32
     )
     return (x_float + branch).astype(jnp.bfloat16)
 

time: 258 us -> 186 us (0.72)
  waiting for transfers between devices: 184 us -> 134 us
  blocking collectives: 26.8 us -> 0 us
  local copies, waits for them, and re-layouts: 2.62 us -> 7.53 us
  other arithmetic: 4.28 us -> 7.87 us
  matrix products: 26.3 us -> 22.9 us
    all_gather x2 -> x1, waiting for transfers between devices: 184 us -> 134 us  [body(): every = lax.all_gather(rows, ('fsdp', 'rep'), axis=0, tiled=True)]
    all_gather x1 -> x0, blocking collectives: 17.1 us -> none  [sent_together(): lax.all_gather(both, axis, axis=dim, tiled=True)]
    all_to_all x1 -> x0, blocking collectives: 9.7 us -> none  [copy_for_each(): return lax.all_to_all(copies, axis, split_axis=0, concat_axis=0, tiled=True)]
    unnamed x2 -> x18, local copies, waits for them, and re-layouts: 0.01 us -> 5.02 us
    dot_general x1, matrix products: 10.6 us -> 6.84 us  [body(): queries = jnp.dot(normed, query_piece, preferred_element_type=jnp.float32)]
  transfers between devices with their start and end apart: 2 -> 1, of which waited for: 2 -> 1; matrix products, arithmetic and copies ran while one was open for 10% -> 1% of each run, Pallas kernels for 0% -> 0%
where the time goes in v1:
time: 186 us
  waiting for transfers between devices  134 us (72%)
  matrix products  22.9 us (12%)
  between operations  13.5 us (7%)
  other arithmetic  7.87 us (4%)
  local copies, waits for them, and re-layouts  7.53 us (4%)
    all_gather x1, waiting for transfers between devices, body(): every = lax.all_gather(rows, ('fsdp', 'rep'), axis=0, tiled=True)  134 us
    dot_general x1, matrix products, body(): queries = jnp.dot(normed, query_piece, preferred_element_type=jnp.float32)  6.84 us
    dot_general x1, matrix products, body(): lax.dot_general(context, out_piece, (((1,), (1,)), ((), ())), preferred_e...  6.74 us
    unnamed x18, local copies, waits for them, and re-layouts  5.02 us
  transfers between devices with their start and end apart: 1, of which 1 were waited for; matrix products, arithmetic and copies ran while one was open for 1% of the time, Pallas kernels for 0%

profile of v1, /device:TPU:1, one launch (start us, length us, event | category | flops | bytes accessed | tf_op | source)
XLA Modules:
  0.0 185.7 jit_solution(11780577300669882799)
XLA Ops:
  6.5 0.0 copy-start.1
  6.5 0.0 all-gather.2.cloned.1.call-start
  6.5 0.8 constant_dynamic-update-slice_fusion.3
  7.4 0.7 constant_dynamic-update-slice_fusion.2
  8.1 0.7 constant_dynamic-update-slice_fusion.1
  8.8 0.8 bitcast_dynamic-update-slice_fusion
  9.5 0.7 constant_dynamic-update-slice_fusion
  10.3 0.0 copy-start.5
  10.3 0.6 copy-done.5
  10.9 0.0 all-gather.2.cloned.1.call-update
  11.0 0.6 iota_compare_fusion
  11.6 0.2 fusion.39
  11.8 1.5 fusion.15
  13.3 133.9 %all-gather.2.cloned.1.call-done = bf16[2048,5248]{1,0:T(8,128)(2,1)} async-done(((bf16[8,5248]{1,0:T(8,128)(2,1)}), bf16[2048,5248]{1,0:T(8,128)(2,1)}) %all-gather.2.cloned.1.call-update) | async-done | bytes 21495824 | tf_op jit(solution)/shard_map/all_gather | solution.py:39
  147.2 1.3 convert_reduce_fusion
  148.5 0.0 copy-done.1
  148.5 6.8 %fusion.3 = f32[256,2048]{0,1:T(8,128)S(1)} fusion(bf16[2048,5248]{1,0:T(8,128)(2,1)} %all-gather.2.cloned.1.call-done, bf16[256,2048]{1,0:T(8,128)(2,1)S(1)} %copy-done.1, f32[2048]{0:T(1024)S(1)} %convert_reduce_fusion, f32[256]{0:T(256)S(1)} %add_rsqrt_fusion), kind=kOutput, calls=%fused_computation.3 | convolution fusion | flops 2149580800 | bytes 11543552 | tf_op jit(solution)/shard_map/dot_general | solution.py:48
  155.3 0.0 copy-start.2
  155.3 1.2 slice_negate_fusion
  156.5 0.2 copy-done.2
  156.7 2.6 %fusion.18 = f32[256,512]{0,1:T(8,128)S(1)} fusion(bf16[2048,5248]{1,0:T(8,128)(2,1)} %all-gather.2.cloned.1.call-done, bf16[256,2048]{1,0:T(8,128)(2,1)S(1)} %copy-done.2, f32[2048]{0:T(1024)S(1)} %convert_reduce_fusion, f32[256]{0:T(256)S(1)} %add_rsqrt_fusion), kind=kOutput, calls=%fused_computation.20 | convolution fusion | flops 538968064 | bytes 3679232 | tf_op jit(solution)/shard_map/dot_general | solution.py:49
  159.4 0.0 copy-start
  159.4 0.8 copy-done
  160.2 0.8 slice_negate_fusion.1
  160.9 3.0 %fusion.25 = bf16[256,512]{1,0:T(8,128)(2,1)} fusion(bf16[2048,5248]{1,0:T(8,128)(2,1)} %all-gather.2.cloned.1.call-done, bf16[256,2048]{1,0:T(8,128)(2,1)S(1)} %copy-done.2, f32[2048]{0:T(1024)S(1)} %convert_reduce_fusion, f32[256]{0:T(256)S(1)} %add_rsqrt_fusion), kind=kOutput, calls=%fused_computation.28 | convolution fusion | flops 539099136 | bytes 3417088 | tf_op jit(solution)/shard_map/dot_general | solution.py:50
  164.0 1.8 copy.15
  165.8 0.0 copy-start.6
  165.8 2.8 %fusion.28 = f32[8,256,256,4]{2,1,3,0:T(8,128)S(1)} fusion(f32[256,8,4,32]{0,3,2,1:T(8,128)} %get-tuple-element.6, f32[256,8,4,32]{0,3,2,1:T(8,128)S(1)} %get-tuple-element.5, f32[256,8,4,64]{0,3,2,1:T(8,128)S(1)} %bitcast.31, f32[256,64]{0,1:T(8,128)S(1)} %get-tuple-element.14, f32[256,64]{0,1:T(8,128)S(1)} %get-tuple-element.13, ...), kind=kOutput, calls=%fused_computation.29 | convolution fusion | flops 271712256 | bytes 13762560 | tf_op jit(solution)/shard_map/qkgd,skd->kgqs/dot_general | solution.py:59
  168.6 0.0 copy-done.6
  168.6 0.0 copy-start.4
  168.6 2.3 %fusion.46 = (f32[8,4,256]{2,1,0:T(4,128)S(1)}, f32[8,4,256,256]{2,3,1,0:T(8,128)S(1)}) fusion(f32[8,256,256,4]{2,1,3,0:T(8,128)S(1)} %fusion.28, pred[256,256]{0,1:T(8,128)(4,1)S(1)} %copy-done.6), kind=kOutput, calls=%fused_computation.57 | output fusion | flops 12583167 | bytes 16875520 | tf_op jit(solution)/shard_map/sub | solution.py:65
  170.9 0.0 copy-done.4
  170.9 0.0 copy-start.3
  170.9 0.8 fusion.24
  171.8 0.4 copy-done.3
  172.1 6.7 %fusion.12 = bf16[256,2048]{1,0:T(8,128)(2,1)} fusion(bf16[256,2048]{0,1:T(8,128)(2,1)S(1)} %bitcast.35, bf16[2048,5248]{1,0:T(8,128)(2,1)} %all-gather.2.cloned.1.call-done, bf16[256,2048]{1,0:T(8,128)(2,1)S(1)} %copy-done.3), kind=kOutput, calls=%fused_computation.16 | convolution fusion | flops 2149056512 | bytes 11534336 | tf_op jit(solution)/shard_map/dot_general | solution.py:69
  (3 shorter events, 0.0 us)
Async XLA Ops:
  6.5 141.9 %copy-start.1 = (bf16[256,2048]{1,0:T(8,128)(2,1)S(1)}, bf16[256,2048]{1,0:T(8,128)(2,1)}, u32[]{:S(2)}) copy-start(bf16[256,2048]{1,0:T(8,128)(2,1)} %param.6) | copy-start | bytes 3145732
  6.5 140.7 %all-gather.2.cloned.1.call-start = ((), (), s32[]{:S(2)}) async-start(), calls=%async_computation | async-start | bytes 21579776 | tf_op jit(solution)/shard_map/all_gather | solution.py:39
  10.3 0.6 copy-start.5
  155.3 1.4 copy-start.2
  159.4 0.8 copy-start
  165.8 2.8 %copy-start.6 = (pred[256,256]{0,1:T(8,128)(4,1)S(1)}, pred[256,256]{0,1:T(8,128)(4,1)}, u32[]{:S(2)}) copy-start(pred[256,256]{0,1:T(8,128)(4,1)} %iota_compare_fusion) | copy-start | bytes 196612
  168.6 2.3 %copy-start.4 = (bf16[256,512]{0,1:T(8,128)(2,1)S(1)}, bf16[256,512]{0,1:T(8,128)(2,1)}, u32[]{:S(2)}) copy-start(bf16[256,512]{0,1:T(8,128)(2,1)} %copy.15) | copy-start | bytes 786436
  170.9 1.2 copy-start.3
Sparse Core Ops, SparseCore 0:
  11.1 136.0 all-gather.1

commit v2 on v1

v2 whole, which is shorter than its diff:
```python
import functools

import jax
import jax.numpy as jnp
from jax import lax
from jax.experimental import pallas as pl
from jax.experimental.pallas import tpu as pltpu
from jax.sharding import Mesh
from jax.sharding import PartitionSpec as P


HD = 64
PAD = 128
AXES = ("z", "y", "x", "c")
VMEM = pl.BlockSpec(memory_space=pltpu.VMEM)
SMEM = pl.BlockSpec(memory_space=pltpu.SMEM)
ANY = pl.BlockSpec(memory_space=pl.ANY)
F32 = jnp.float32
BF16 = jnp.bfloat16

rope_base = 500000.0
norm_eps = 1e-05


def shape_of(dims, dtype=BF16):
    return jax.ShapeDtypeStruct(tuple(dims), dtype)


def shift(array, axis, by):
    n = lax.axis_size(axis)
    return lax.ppermute(array, axis, [(i, (i + by) % n) for i in range(n)])


def halves_kernel(at, wq, wk, wv, gain, wo, mine, theirs):
    core = at[0]
    for out, which in ((mine, core), (theirs, 1 - core)):
        to = 0
        for ref, dtype_cols in ((wk, 2), (wv, 2), (gain, 1), (wq, 2), (wo, 2)):
            n = ref.shape[1] // dtype_cols
            start = 0 if dtype_cols == 1 else pl.multiple_of(which * n, 128)
            out[:, to : to + n] = ref[:, pl.ds(start, n)]
            to += n


def order_kernel(cols, at, mine, got, copies, outs):
    core = at[0]
    rows = mine.shape[0]
    for k in range(2):
        piece = jnp.where(core == k, mine[...], got[...])
        for z in range(copies.shape[0]):
            copies[z, k * rows : (k + 1) * rows, :] = piece[:, :cols]
        outs[k * rows : (k + 1) * rows, :] = piece[:, cols:]


def beside_kernel(dim, n, slot, at, *refs):
    *pieces, out = refs
    me = at[slot]
    for by, ref in zip((0, n - 1, 1, 2, 2), pieces):
        index = lax.rem(me + by, n)
        if dim == 0:
            out[index] = ref[...]
        elif ref.shape[0] == out.shape[0]:
            out[:, pl.ds(index, 1)] = ref[...][:, None]
    if dim == 1:
        low, high = pieces[3], pieces[4]
        half = low.shape[0]
        index = lax.rem(me + 2, n)
        out[0:half, pl.ds(index, 1)] = low[...][:, None]
        out[half : 2 * half, pl.ds(index, 1)] = high[...][:, None]


def beside(at, slot, pieces, dim):
    dims = list(pieces[0].shape)
    dims.insert(dim, 4)
    return pl.pallas_call(
        functools.partial(beside_kernel, dim, 4, slot),
        out_shape=shape_of(dims),
        in_specs=[SMEM] + [VMEM] * len(pieces),
        out_specs=VMEM,
        name="beside",
    )(at, *pieces)


def ring4(block, axis):
    half = block.shape[0] // 2
    back = shift(block, axis, 1)
    ahead = shift(block, axis, -1)
    low = shift(back[:half], axis, 1)
    high = shift(ahead[half:], axis, -1)
    return block, back, ahead, low, high


def direct4(at, slot, block, axis):
    back = shift(block, axis, 1)
    ahead = shift(block, axis, -1)
    far = shift(block, axis, 2)
    return beside(at, slot, (block, back, ahead, far), 0)


def ring8(block, axis):
    half = block.shape[0] // 2
    back = ahead = block
    pieces = [block]
    for _ in range(3):
        back = shift(back, axis, 1)
        ahead = shift(ahead, axis, -1)
        pieces += [back, ahead]
    return (*pieces, shift(back[:half], axis, 1), shift(ahead[half:], axis, -1))


def attend_kernel(tokens, at, own, other, cos_ref, sin_ref, *refs):
    a_pieces, b_pieces = refs[0:5], refs[5:10]
    ctx, w_a, w_b, normed, q_s, k_s, v_s, sems = refs[10:]
    width = own.shape[1]
    x_at, y_at = at[1], at[2]
    copies = []
    for i, (by, z0, zn) in enumerate(((0, 0, 8), (3, 0, 8), (1, 0, 8), (2, 0, 4), (2, 4, 4))):
        y_from = lax.rem(y_at + by, 4)
        x_from = lax.rem(x_at + by, 4)
        copies.append(pltpu.make_async_copy(a_pieces[i], w_a.at[pl.ds(z0, zn), y_from], sems.at[i]))
        copies.append(
            pltpu.make_async_copy(b_pieces[i], w_b.at[pl.ds(z0, zn), :, x_from], sems.at[5 + i])
        )
    for c in copies:
        c.start()
    kv_cols = k_s.shape[1]
    for c in copies:
        c.wait()
    gain = w_a[:, :, :, :, 2 * kv_cols : 2 * kv_cols + PAD].reshape(width // PAD, PAD, PAD).astype(F32)
    eye = lax.broadcasted_iota(jnp.int32, (PAD, PAD), 0) == lax.broadcasted_iota(jnp.int32, (PAD, PAD), 1)
    lanes = jnp.concatenate(
        [jnp.sum(jnp.where(eye, gain[i], 0.0), axis=0, keepdims=True) for i in range(width // PAD)], axis=1
    )
    step = 64

    def norm(i, _):
        for s, ref in enumerate((own, other)):
            start = pl.multiple_of(i * step, step)
            x = ref[pl.ds(start, step), :].astype(F32)
            inv = lax.rsqrt(jnp.sum(x * x, axis=1, keepdims=True) * (1.0 / width) + norm_eps)
            normed[pl.ds(s * tokens + start, step), :] = (x * inv * lanes).astype(BF16)
        return 0

    lax.fori_loop(0, tokens // step, norm, 0)

    low_half = (lax.broadcasted_iota(jnp.int32, (tokens, 2 * HD), 1) % HD) < HD // 2

    def rope(t):
        turned = jnp.where(low_half, -pltpu.roll(t, 2 * HD - HD // 2, 1), pltpu.roll(t, HD // 2, 1))
        return t * cos_ref[...] + turned * sin_ref[...]

    def product(s, weights):
        start = pl.multiple_of(s * tokens, tokens)
        return jnp.dot(normed[pl.ds(start, tokens), :], weights, preferred_element_type=F32)

    def keys_values(s, _):
        start = pl.multiple_of(s * tokens, tokens)
        t = product(s, w_a[:, :, :, :, 0:kv_cols].reshape(width, kv_cols))
        for j in range(kv_cols // (2 * HD)):
            cols = slice(j * 2 * HD, (j + 1) * 2 * HD)
            k_s[pl.ds(start, tokens), cols] = rope(t[:, cols]).astype(BF16)
        t = product(s, w_a[:, :, :, :, kv_cols : 2 * kv_cols].reshape(width, kv_cols))
        v_s[s] = t.T.astype(BF16)
        return 0

    lax.fori_loop(0, 2, keys_values, 0)

    def queries(s, _):
        start = pl.multiple_of(s * tokens, tokens)
        base = 2 * kv_cols + PAD
        for n in range(4):
            if n == 0:
                weights = w_a[:, :, :, :, base : base + kv_cols]
            else:
                weights = w_b[:, :, :, :, (n - 1) * kv_cols : n * kv_cols]
            t = product(s, weights.reshape(width, kv_cols))
            for j in range(kv_cols // (2 * HD)):
                cols = slice(j * 2 * HD, (j + 1) * 2 * HD)
                to = n * kv_cols + j * 2 * HD
                q_s[pl.ds(start, tokens), to : to + 2 * HD] = rope(t[:, cols]).astype(BF16)
        return 0

    lax.fori_loop(0, 2, queries, 0)

    seen = lax.broadcasted_iota(jnp.int32, (tokens, tokens), 0) <= lax.broadcasted_iota(
        jnp.int32, (tokens, tokens), 1
    )
    left = lax.broadcasted_iota(jnp.int32, (tokens, 2 * HD), 1) < HD

    def attend(s, _):
        start = pl.multiple_of(s * tokens, tokens)
        for kv in range(4):
            tile = k_s[pl.ds(start, tokens), (kv // 2) * 2 * HD : (kv // 2 + 1) * 2 * HD].astype(F32)
            in_left = jnp.where(left, tile if kv % 2 == 0 else pltpu.roll(tile, HD, 1), 0.0)
            sides = (in_left.astype(BF16), pltpu.roll(in_left, HD, 1).astype(BF16))
            parts = []
            for g in range(4):
                h = kv * 4 + g
                q = q_s[pl.ds(start, tokens), (h // 2) * 2 * HD : (h // 2 + 1) * 2 * HD]
                scores = lax.dot_general(
                    sides[h % 2], q, (((1,), (1,)), ((), ())), preferred_element_type=F32
                )
                scores = jnp.where(seen, scores * HD**-0.5, -1e30)
                expo = jnp.exp(scores - jnp.max(scores, axis=0, keepdims=True))
                probs = (expo * (1.0 / jnp.sum(expo, axis=0, keepdims=True))).astype(BF16)
                parts.append(
                    jnp.dot(v_s[s, kv * HD : (kv + 1) * HD, :], probs, preferred_element_type=F32)
                )
            ctx[pl.ds(start, tokens), kv * 4 * HD : (kv + 1) * 4 * HD] = (
                jnp.concatenate(parts, axis=0).T.astype(BF16)
            )
        return 0

    lax.fori_loop(0, 2, attend, 0)


def project_kernel(seq, tokens, at, ctx, *refs):
    pieces = refs[0:9]
    out, w_o, sems = refs[9:]
    z_at = at[3]
    rows = w_o.shape[1]
    half = rows // 2
    copies = []
    for i, by in enumerate((0, 7, 1, 6, 2, 5, 3, 4, 4)):
        z_from = lax.rem(z_at + by, 8)
        to = w_o.at[z_from]
        if i == 7:
            to = w_o.at[z_from, 0:half]
        if i == 8:
            to = w_o.at[z_from, half:rows]
        copies.append(pltpu.make_async_copy(pieces[i], to, sems.at[i]))
    for c in copies:
        c.start()
    for c in copies:
        c.wait()

    def one(z, _):
        out[:, pl.ds(pl.multiple_of(z * rows, rows), rows)] = lax.dot_general(
            ctx[seq * tokens : (seq + 1) * tokens, :],
            w_o[z],
            (((1,), (1,)), ((), ())),
            preferred_element_type=F32,
        )
        return 0

    lax.fori_loop(0, 8, one, 0)


def inner(hidden, attn_gain, w_query, w_key, w_value, w_out):
    tokens, width = hidden.shape
    wq, wkv = w_query.shape[1] // 2, w_key.shape[1] // 2
    rows = w_query.shape[0]
    cols = wq + 2 * wkv + PAD
    cols_a = 3 * wkv + PAD
    at = jnp.stack([lax.axis_index(a) for a in ("c", "x", "y", "z")]).astype(jnp.int32)

    gain = jnp.broadcast_to(attn_gain[:, None], (rows, PAD))
    mine, theirs = pl.pallas_call(
        halves_kernel,
        out_shape=(shape_of((rows, cols + wq)),) * 2,
        in_specs=[SMEM] + [VMEM] * 5,
        out_specs=(VMEM, VMEM),
        name="halves",
    )(at, w_query, w_key, w_value, gain, w_out.T)
    got = shift(theirs, "c", 1)
    copies, out_rows = pl.pallas_call(
        functools.partial(order_kernel, cols),
        out_shape=(shape_of((8, 2 * rows, cols)), shape_of((2 * rows, wq))),
        in_specs=[SMEM, VMEM, VMEM],
        out_specs=(VMEM, VMEM),
        name="order",
    )(at, mine, got)
    by_z = lax.all_to_all(copies, "z", split_axis=0, concat_axis=0, tiled=True)
    other = shift(hidden, "c", 1)
    out_x = direct4(at, 1, out_rows, "x")
    out_xy = direct4(at, 2, out_x, "y").reshape(-1, wq)
    out_pieces = ring8(out_xy, "z")
    block_a = beside(at, 1, ring4(by_z[:, :, :cols_a], "x"), 1)
    block_b = beside(at, 2, ring4(by_z[:, :, cols_a:], "y"), 1)
    a_pieces = ring4(block_a, "y")
    b_pieces = ring4(block_b, "x")

    position = jnp.arange(tokens, dtype=F32)
    freq = rope_base ** (-(jnp.arange(HD // 2, dtype=F32) * 2.0) / HD)
    angle = position[:, None] * freq[None, :]
    cos_table = jnp.concatenate([jnp.cos(angle)] * 4, axis=-1)
    sin_table = jnp.concatenate([jnp.sin(angle)] * 4, axis=-1)

    context = pl.pallas_call(
        functools.partial(attend_kernel, tokens),
        out_shape=shape_of((2 * tokens, wq)),
        in_specs=[SMEM] + [VMEM] * 4 + [ANY] * 10,
        out_specs=VMEM,
        scratch_shapes=[
            pltpu.VMEM((8, 4, 4, 2 * rows, cols_a), BF16),
            pltpu.VMEM((8, 4, 4, 2 * rows, cols - cols_a), BF16),
            pltpu.VMEM((2 * tokens, width), BF16),
            pltpu.VMEM((2 * tokens, wq), BF16),
            pltpu.VMEM((2 * tokens, wkv), BF16),
            pltpu.VMEM((2, wkv, tokens), BF16),
            pltpu.SemaphoreType.DMA((10,)),
        ],
        cost_estimate=pl.CostEstimate(flops=4_000_000_000, bytes_accessed=10_000_000, transcendentals=0),
        compiler_params=pltpu.CompilerParams(vmem_limit_bytes=40 * 1024 * 1024),
        name="attend",
    )(at, hidden, other, cos_table, sin_table, *a_pieces, *b_pieces)

    def project(seq):
        return pl.pallas_call(
            functools.partial(project_kernel, seq, tokens),
            out_shape=shape_of((tokens, width), F32),
            in_specs=[SMEM, VMEM] + [ANY] * 9,
            out_specs=VMEM,
            scratch_shapes=[pltpu.VMEM((8, width // 8, wq), BF16), pltpu.SemaphoreType.DMA((9,))],
            cost_estimate=pl.CostEstimate(flops=1_000_000_000, bytes_accessed=8_000_000, transcendentals=0),
            compiler_params=pltpu.CompilerParams(vmem_limit_bytes=24 * 1024 * 1024),
            name="project",
        )(at, context, *out_pieces)

    from_them = shift(project(1), "c", 1)
    return (hidden.astype(F32) + (project(0) + from_them)).astype(BF16)


def solution(mesh):
    torus = Mesh(mesh.devices.reshape(8, 4, 4, 2), AXES)
    placed = (P(AXES, None), P(AXES), P(AXES, None), P(AXES, None), P(AXES, None), P(None, AXES))
    return jax.shard_map(inner, mesh=torus, in_specs=placed, out_specs=P(AXES, None), check_vma=False)
```

time: 186 us -> 150 us (0.81)
  waiting for transfers between devices: 134 us -> 42.8 us
  starting transfers between devices: 0.01 us -> 59.1 us
  Pallas kernels: 0 us -> 37.1 us
  matrix products: 22.9 us -> 0 us
  between operations: 13.5 us -> 0.33 us
  other arithmetic: 7.87 us -> 2.88 us
    all_gather x1 -> x0, waiting for transfers between devices: 134 us -> none  [body(): every = lax.all_gather(rows, ('fsdp', 'rep'), axis=0, tiled=True)]
    ppermute x0 -> x33, starting transfers between devices: none -> 52.6 us  [shift(): return lax.ppermute(array, axis, [(i, (i + by) % n) for i in range(n)])]
    ppermute x0 -> x33, waiting for transfers between devices: none -> 42.8 us  [shift(): return lax.ppermute(array, axis, [(i, (i + by) % n) for i in range(n)])]
    pallas_call x0 -> x9, Pallas kernels: none -> 37.1 us  [the longest x1 18.8 us: inner(): pl.pallas_call(functools.partial(attend_kernel, tokens), out_shape=shape_...]
    dot_general x6 -> x0, matrix products: 22.9 us -> none  [the longest x1 6.84 us: body(): queries = jnp.dot(normed, query_piece, preferred_element_type=jnp.float32)]
    all_to_all x0 -> x1, starting transfers between devices: none -> 6.48 us  [inner(): by_z = lax.all_to_all(copies, 'z', split_axis=0, concat_axis=0, tiled=True)]
    slice x0 -> x12, local copies, waits for them, and re-layouts: none -> 3.24 us  [the longest x4 2.1 us: ring4(): high = shift(ahead[half:], axis, -1)]
    unnamed x18 -> x40, local copies, waits for them, and re-layouts: 5.02 us -> 2.58 us
  transfers between devices with their start and end apart: 1 -> 34, of which waited for: 1 -> 13; matrix products, arithmetic and copies ran while one was open for 1% -> 3% of each run, Pallas kernels for 0% -> 20%
where the time goes in v2:
time: 150 us; the launch traced here: 149 us
  starting transfers between devices  59.1 us (39%)
  waiting for transfers between devices  42.8 us (29%)
  Pallas kernels  37.1 us (25%)
  local copies, waits for them, and re-layouts  7.13 us (5%)
  other arithmetic  2.88 us (2%)
    ppermute x33, starting transfers between devices, shift(): return lax.ppermute(array, axis, [(i, (i + by) % n) for i in range(n)])  52.6 us
    ppermute x33, waiting for transfers between devices, shift(): return lax.ppermute(array, axis, [(i, (i + by) % n) for i in range(n)])  42.8 us
    pallas_call x1, Pallas kernels, inner(): pl.pallas_call(functools.partial(attend_kernel, tokens), out_shape=shape_...  18.8 us
    pallas_call x4, Pallas kernels, beside(): pl.pallas_call(functools.partial(beside_kernel, dim, 4, slot), out_shape=...  7.92 us
    pallas_call x2, Pallas kernels, project(): pl.pallas_call(functools.partial(project_kernel, seq, tokens), out_shape=...  7.27 us
    all_to_all x1, starting transfers between devices, inner(): by_z = lax.all_to_all(copies, 'z', split_axis=0, concat_axis=0, tiled=True)  6.48 us
  transfers between devices with their start and end apart: 34, of which 13 were waited for; matrix products, arithmetic and copies ran while one was open for 3% of the time, Pallas kernels for 20%

profile of v2, /device:TPU:1, one launch (start us, length us, event | category | flops | bytes accessed | tf_op | source)
XLA Modules:
  0.0 149.3 jit_solution(2454782512698058518)
XLA Ops:
  0.6 1.3 broadcast_in_dim.2.gain
  1.9 1.5 halves.1
  3.3 3.2 %collective-permute-start.1 = (bf16[8,2688]{1,0:T(8,128)(2,1)}, bf16[8,2688]{1,0:T(8,128)(2,1)S(1)}, u32[]{:S(2)}, u32[]{:S(2)}) collective-permute-start(bf16[8,2688]{1,0:T(8,128)(2,1)} %get-tuple-element.10), channel_id=1, source_target_pairs={{0,1},{1,0},{2,3},{3,2},{4,5},{5,4},{6,7},{7,6},{8,9},{9,8},{10,11... | collective-permute-start | bytes 129032 | tf_op jit(solution)/shard_map/ppermute | solution.py:31
  6.6 1.1 collective-permute-done.1.got
  8.2 1.6 %order.1 = (bf16[8,16,1664]{2,1,0:T(8,128)(2,1)}, bf16[16,1024]{1,0:T(8,128)(2,1)}) custom-call(s32[4]{0:T(128)} %pad_add_fusion.at, bf16[8,2688]{1,0:T(8,128)(2,1)} %get-tuple-element.9.mine, bf16[8,2688]{1,0:T(8,128)(2,1)} %copy-done.16), custom_call_target="tpu_custom_call" | custom-call | tf_op jit(solution)/shard_map/order/pallas_call | solution.py:266
  9.8 6.5 %all-to-all-start = ((bf16[8,16,1664]{2,1,0:T(8,128)(2,1)}), bf16[8,16,1664]{2,1,0:T(8,128)(2,1)S(1)}, u32[]{:S(2)}, u32[]{:S(2)}) async-start(bf16[8,16,1664]{2,1,0:T(8,128)(2,1)} %get-tuple-element.11), calls=%async_computation | async-start | bytes 851968 | tf_op jit(solution)/shard_map/all_to_all | solution.py:273
  16.3 1.2 collective-permute-start.18
  17.5 1.5 collective-permute-start.19
  19.0 1.5 %collective-permute-start.20 = (bf16[16,1024]{1,0:T(8,128)(2,1)}, bf16[16,1024]{1,0:T(8,128)(2,1)S(1)}, u32[]{:S(2)}, u32[]{:S(2)}) collective-permute-start(bf16[16,1024]{1,0:T(8,128)(2,1)} %get-tuple-element.12.refs_0_), channel_id=1, source_target_pairs={{0,4},{2,6},{4,0},{6,2},{1,5},{3,7},{5,1},{7,3},{8,12},{10,14},{12... | collective-permute-start | bytes 98312 | tf_op jit(solution)/shard_map/ppermute | solution.py:31
  20.8 3.0 %collective-permute-done.20.refs_3_ = bf16[16,1024]{1,0:T(8,128)(2,1)S(1)} collective-permute-done((bf16[16,1024]{1,0:T(8,128)(2,1)}, bf16[16,1024]{1,0:T(8,128)(2,1)S(1)}, u32[]{:S(2)}, u32[]{:S(2)}) %collective-permute-start.20) | collective-permute-done | bytes 32800 | tf_op jit(solution)/shard_map/ppermute | solution.py:31
  24.4 1.5 beside.6.refs_0_
  25.9 1.3 collective-permute-start.21
  27.2 1.4 collective-permute-start.22
  28.6 1.6 %collective-permute-start.23 = (bf16[4,16,1024]{2,1,0:T(8,128)(2,1)}, bf16[4,16,1024]{2,1,0:T(8,128)(2,1)S(1)}, u32[]{:S(2)}, u32[]{:S(2)}) collective-permute-start(bf16[4,16,1024]{2,1,0:T(8,128)(2,1)} %beside.6.refs_0_), channel_id=1, source_target_pairs={{0,16},{8,24},{16,0},{24,8},{1,17},{9,25},{17,1},{25,9},{2,18},{10... | collective-permute-start | bytes 393224 | tf_op jit(solution)/shard_map/ppermute | solution.py:31
  30.3 1.2 collective-permute-done.21.refs_1_
  31.5 3.3 %collective-permute-done.23.refs_3_ = bf16[4,16,1024]{2,1,0:T(8,128)(2,1)S(1)} collective-permute-done((bf16[4,16,1024]{2,1,0:T(8,128)(2,1)}, bf16[4,16,1024]{2,1,0:T(8,128)(2,1)S(1)}, u32[]{:S(2)}, u32[]{:S(2)}) %collective-permute-start.23) | collective-permute-done | bytes 131104 | tf_op jit(solution)/shard_map/ppermute | solution.py:31
  35.5 2.0 %beside.7 = bf16[4,4,16,1024]{3,2,1,0:T(8,128)(2,1)} custom-call(s32[4]{0:T(128)} %pad_add_fusion.at, bf16[4,16,1024]{2,1,0:T(8,128)(2,1)} %beside.6.refs_0_, bf16[4,16,1024]{2,1,0:T(8,128)(2,1)} %copy-done.10, bf16[4,16,1024]{2,1,0:T(8,128)(2,1)} %copy-done.11, bf16[4,16,1024]{2,1,0:T(8,128)(2,1)} %copy-done.12), custom_call_target="tpu_custom_call" | custom-call | tf_op jit(solution)/shard_map/beside/pallas_call | solution.py:75
  37.5 1.2 collective-permute-start.24
  38.7 1.4 collective-permute-start.25
  40.3 2.7 %collective-permute-start.11 = (bf16[8,16,768]{2,1,0:T(8,128)(2,1)S(1)}, bf16[8,16,768]{2,1,0:T(8,128)(2,1)S(1)}, u32[]{:S(2)}, u32[]{:S(2)}) collective-permute-start(bf16[8,16,768]{2,1,0:T(8,128)(2,1)S(1)} %slice.53.refs_0_), channel_id=1, source_target_pairs={{0,24},{8,0},{16,8},{24,16},{1,25},{9,1},{17,9},{25,17},{2,26},{10... | collective-permute-start | bytes 589832 | tf_op jit(solution)/shard_map/ppermute | solution.py:31
  43.1 6.3 %collective-permute-done.24.refs_1_ = bf16[256,1024]{1,0:T(8,128)(2,1)S(1)} collective-permute-done((bf16[256,1024]{1,0:T(8,128)(2,1)}, bf16[256,1024]{1,0:T(8,128)(2,1)S(1)}, u32[]{:S(2)}, u32[]{:S(2)}) %collective-permute-start.24) | collective-permute-done | bytes 524320 | tf_op jit(solution)/shard_map/ppermute | solution.py:31
  49.5 2.7 %collective-permute-start.13 = (bf16[4,16,768]{2,1,0:T(8,128)(2,1)S(1)}, bf16[4,16,768]{2,1,0:T(8,128)(2,1)S(1)}, u32[]{:S(2)}, u32[]{:S(2)}) collective-permute-start(bf16[4,16,768]{2,1,0:T(8,128)(2,1)S(1)} %slice.55), channel_id=1, source_target_pairs={{0,24},{8,0},{16,8},{24,16},{1,25},{9,1},{17,9},{25,17},{2,26},{10... | collective-permute-start | bytes 294920 | tf_op jit(solution)/shard_map/ppermute | solution.py:31
  52.3 1.9 %collective-permute-done.12.refs_3_ = bf16[4,16,768]{2,1,0:T(8,128)(2,1)S(1)} collective-permute-done((bf16[4,16,768]{2,1,0:T(8,128)(2,1)S(1)}, bf16[4,16,768]{2,1,0:T(8,128)(2,1)S(1)}, u32[]{:S(2)}, u32[]{:S(2)}) %collective-permute-start.12) | collective-permute-done | bytes 98336 | tf_op jit(solution)/shard_map/ppermute | solution.py:31
  54.2 1.3 collective-permute-start.3
  56.1 2.2 %beside.5.refs_5_ = bf16[8,4,16,768]{3,2,1,0:T(8,128)(2,1)} custom-call(s32[4]{0:T(128)} %pad_add_fusion.at, bf16[8,16,768]{2,1,0:T(8,128)(2,1)} %copy-done.6, bf16[8,16,768]{2,1,0:T(8,128)(2,1)} %copy-done.8, bf16[8,16,768]{2,1,0:T(8,128)(2,1)} %copy-done.9, bf16[4,16,768]{2,1,0:T(8,128)(2,1)} %copy-done.14, bf16[4,16,768]{2,1,0:T(8,128)(2,1)} %copy-done.15), custom_call_target="tpu_custom_call" | custom-call | tf_op jit(solution)/shard_map/beside/pallas_call | solution.py:75
  58.5 2.5 %collective-permute-start.15 = (bf16[8,4,16,768]{3,2,1,0:T(8,128)(2,1)}, bf16[8,4,16,768]{3,2,1,0:T(8,128)(2,1)}, u32[]{:S(2)}, u32[]{:S(2)}) collective-permute-start(bf16[8,4,16,768]{3,2,1,0:T(8,128)(2,1)} %beside.5.refs_5_), channel_id=1, source_target_pairs={{0,6},{2,0},{4,2},{6,4},{1,7},{3,1},{5,3},{7,5},{8,14},{10,8},{12,... | collective-permute-start | bytes 2359304 | tf_op jit(solution)/shard_map/ppermute | solution.py:31
  61.2 2.7 %collective-permute-start.27 = (bf16[256,1024]{1,0:T(8,128)(2,1)S(1)}, bf16[256,1024]{1,0:T(8,128)(2,1)S(1)}, u32[]{:S(2)}, u32[]{:S(2)}) collective-permute-start(bf16[256,1024]{1,0:T(8,128)(2,1)S(1)} %collective-permute-done.25.refs_2_), channel_id=1, source_target_pairs={{0,224},{32,0},{64,32},{96,64},{128,96},{160,128},{192,160},{224,1... | collective-permute-start | bytes 1572872 | tf_op jit(solution)/shard_map/ppermute | solution.py:31
  63.9 0.9 slice.50
  64.8 10.5 %collective-permute-done.4.refs_3_ = bf16[4,16,896]{2,1,0:T(8,128)(2,1)S(1)} collective-permute-done((bf16[4,16,896]{2,1,0:T(8,128)(2,1)S(1)}, bf16[4,16,896]{2,1,0:T(8,128)(2,1)S(1)}, u32[]{:S(2)}, u32[]{:S(2)}) %collective-permute-start.4) | collective-permute-done | bytes 114720 | tf_op jit(solution)/shard_map/ppermute | solution.py:31
  75.3 5.3 %collective-permute-done.5.refs_4_ = bf16[4,16,896]{2,1,0:T(8,128)(2,1)} collective-permute-done((bf16[4,16,896]{2,1,0:T(8,128)(2,1)S(1)}, bf16[4,16,896]{2,1,0:T(8,128)(2,1)}, u32[]{:S(2)}, u32[]{:S(2)}) %collective-permute-start.5) | collective-permute-done | bytes 114720 | tf_op jit(solution)/shard_map/ppermute | solution.py:31
  80.6 2.3 %beside.4.refs_0_ = bf16[8,4,16,896]{3,2,1,0:T(8,128)(2,1)} custom-call(s32[4]{0:T(128)} %pad_add_fusion.at, bf16[8,16,896]{2,1,0:T(8,128)(2,1)} %copy-done.5, bf16[8,16,896]{2,1,0:T(8,128)(2,1)} %copy-done.7, bf16[8,16,896]{2,1,0:T(8,128)(2,1)} %collective-permute-done.3.refs_2_, bf16[4,16,896]{2,1,0:T(8,128)(2,1)} %copy-done.13, ...), custom_call_target="tpu_custom_call" | custom-call | tf_op jit(solution)/shard_map/beside/pallas_call | solution.py:75
  82.9 2.6 %collective-permute-start.7 = (bf16[8,4,16,896]{3,2,1,0:T(8,128)(2,1)}, bf16[8,4,16,896]{3,2,1,0:T(8,128)(2,1)S(1)}, u32[]{:S(2)}, u32[]{:S(2)}) collective-permute-start(bf16[8,4,16,896]{3,2,1,0:T(8,128)(2,1)} %beside.4.refs_0_), channel_id=1, source_target_pairs={{0,24},{8,0},{16,8},{24,16},{1,25},{9,1},{17,9},{25,17},{2,26},{10... | collective-permute-start | bytes 2752520 | tf_op jit(solution)/shard_map/ppermute | solution.py:31
  85.5 7.1 %collective-permute-start = (bf16[256,2048]{1,0:T(8,128)(2,1)S(1)}, bf16[256,2048]{1,0:T(8,128)(2,1)S(1)}, u32[]{:S(2)}, u32[]{:S(2)}) collective-permute-start(bf16[256,2048]{1,0:T(8,128)(2,1)S(1)} %copy-done.1), channel_id=1, source_target_pairs={{0,1},{1,0},{2,3},{3,2},{4,5},{5,4},{6,7},{7,6},{8,9},{9,8},{10,11... | collective-permute-start | bytes 3145736 | tf_op jit(solution)/shard_map/ppermute | solution.py:31
  93.2 2.2 %collective-permute-start.29 = (bf16[256,1024]{1,0:T(8,128)(2,1)S(1)}, bf16[256,1024]{1,0:T(8,128)(2,1)S(1)}, u32[]{:S(2)}, u32[]{:S(2)}) collective-permute-start(bf16[256,1024]{1,0:T(8,128)(2,1)S(1)} %collective-permute-done.27.refs_4_), channel_id=1, source_target_pairs={{0,224},{32,0},{64,32},{96,64},{128,96},{160,128},{192,160},{224,1... | collective-permute-start | bytes 1572872 | tf_op jit(solution)/shard_map/ppermute | solution.py:31
  95.4 1.0 slice.56
  96.4 1.1 slice.57
  97.6 2.0 %collective-permute-done.6.refs_1_ = bf16[8,4,16,896]{3,2,1,0:T(8,128)(2,1)S(1)} collective-permute-done((bf16[8,4,16,896]{3,2,1,0:T(8,128)(2,1)}, bf16[8,4,16,896]{3,2,1,0:T(8,128)(2,1)S(1)}, u32[]{:S(2)}, u32[]{:S(2)}) %collective-permute-start.6) | collective-permute-done | bytes 917536 | tf_op jit(solution)/shard_map/ppermute | solution.py:31
  99.7 3.2 %collective-permute-start.17 = (bf16[4,4,16,768]{3,2,1,0:T(8,128)(2,1)S(1)}, bf16[4,4,16,768]{3,2,1,0:T(8,128)(2,1)S(1)}, u32[]{:S(2)}, u32[]{:S(2)}) collective-permute-start(bf16[4,4,16,768]{3,2,1,0:T(8,128)(2,1)S(1)} %slice.57), channel_id=1, source_target_pairs={{0,6},{2,0},{4,2},{6,4},{1,7},{3,1},{5,3},{7,5},{8,14},{10,8},{12,... | collective-permute-start | bytes 1179656 | tf_op jit(solution)/shard_map/ppermute | solution.py:31
  103.0 4.3 %collective-permute-done.28.refs_5_ = bf16[256,1024]{1,0:T(8,128)(2,1)S(1)} collective-permute-done((bf16[256,1024]{1,0:T(8,128)(2,1)S(1)}, bf16[256,1024]{1,0:T(8,128)(2,1)S(1)}, u32[]{:S(2)}, u32[]{:S(2)}) %collective-permute-start.28) | collective-permute-done | bytes 524320 | tf_op jit(solution)/shard_map/ppermute | solution.py:31
  107.2 2.7 %collective-permute-start.9 = (bf16[4,4,16,896]{3,2,1,0:T(8,128)(2,1)S(1)}, bf16[4,4,16,896]{3,2,1,0:T(8,128)(2,1)S(1)}, u32[]{:S(2)}, u32[]{:S(2)}) collective-permute-start(bf16[4,4,16,896]{3,2,1,0:T(8,128)(2,1)S(1)} %slice.52), channel_id=1, source_target_pairs={{0,24},{8,0},{16,8},{24,16},{1,25},{9,1},{17,9},{25,17},{2,26},{10... | collective-permute-start | bytes 1376264 | tf_op jit(solution)/shard_map/ppermute | solution.py:31
  110.8 0.9 collective-permute-start.30
  111.7 2.1 %collective-permute-start.31 = (bf16[128,1024]{1,0:T(8,128)(2,1)S(1)}, bf16[128,1024]{1,0:T(8,128)(2,1)S(1)}, u32[]{:S(2)}, u32[]{:S(2)}) collective-permute-start(bf16[128,1024]{1,0:T(8,128)(2,1)S(1)} %slice.59), channel_id=1, source_target_pairs={{0,224},{32,0},{64,32},{96,64},{128,96},{160,128},{192,160},{224,1... | collective-permute-start | bytes 786440 | tf_op jit(solution)/shard_map/ppermute | solution.py:31
  113.7 3.5 %collective-permute-done.8.refs_3_ = bf16[4,4,16,896]{3,2,1,0:T(8,128)(2,1)S(1)} collective-permute-done((bf16[4,4,16,896]{3,2,1,0:T(8,128)(2,1)S(1)}, bf16[4,4,16,896]{3,2,1,0:T(8,128)(2,1)S(1)}, u32[]{:S(2)}, u32[]{:S(2)}) %collective-permute-start.8) | collective-permute-done | bytes 458784 | tf_op jit(solution)/shard_map/ppermute | solution.py:31
  117.2 18.8 %attend.1.ctx = bf16[512,1024]{1,0:T(8,128)(2,1)S(1)} custom-call(s32[4]{0:T(128)S(1)} %copy-done.4, bf16[256,2048]{1,0:T(8,128)(2,1)S(1)} %copy-done.1, bf16[256,2048]{1,0:T(8,128)(2,1)S(1)} %collective-permute-done.other, f32[256,128]{1,0:T(8,128)S(1)} %get-tuple-element.15.cos_ref, f32[256,128]{1,0:T(8,128)S(1)} %get-tuple-element.16.sin_ref, ...), custom_call_target="tpu_custom_call" | custom-call | flops 4000000000 | bytes 10000000 | tf_op jit(solution)/shard_map/attend/pallas_call | solution.py:289
  136.1 3.7 %project.3 = f32[256,2048]{1,0:T(8,128)S(1)} custom-call(s32[4]{0:T(128)S(1)} %copy-done.4, bf16[512,1024]{1,0:T(8,128)(2,1)S(1)} %attend.1.ctx, bf16[256,1024]{1,0:T(8,128)(2,1)S(1)} %bitcast.8, bf16[256,1024]{1,0:T(8,128)(2,1)S(1)} %collective-permute-done.24.refs_1_, bf16[256,1024]{1,0:T(8,128)(2,1)S(1)} %collective-permute-done.25.refs_2_, ...), custom_call_target="tpu_custom_call" | custom-call | flops 1000000000 | bytes 8000000 | tf_op jit(solution)/shard_map/project/pallas_call | solution.py:309
  139.8 4.2 %collective-permute-start.32 = (f32[256,2048]{1,0:T(8,128)S(1)}, f32[256,2048]{1,0:T(8,128)S(1)}, u32[]{:S(2)}, u32[]{:S(2)}) collective-permute-start(f32[256,2048]{1,0:T(8,128)S(1)} %project.3), channel_id=1, source_target_pairs={{0,1},{1,0},{2,3},{3,2},{4,5},{5,4},{6,7},{7,6},{8,9},{9,8},{10,11... | collective-permute-start | bytes 6291464 | tf_op jit(solution)/shard_map/ppermute | solution.py:31
  144.0 3.6 %project.2 = f32[256,2048]{1,0:T(8,128)S(1)} custom-call(s32[4]{0:T(128)S(1)} %copy-done.4, bf16[512,1024]{1,0:T(8,128)(2,1)S(1)} %attend.1.ctx, bf16[256,1024]{1,0:T(8,128)(2,1)S(1)} %bitcast.9, bf16[256,1024]{1,0:T(8,128)(2,1)S(1)} %collective-permute-done.24.refs_1_, bf16[256,1024]{1,0:T(8,128)(2,1)S(1)} %collective-permute-done.25.refs_2_, ...), custom_call_target="tpu_custom_call" | custom-call | flops 1000000000 | bytes 8000000 | tf_op jit(solution)/shard_map/project/pallas_call | solution.py:309
  147.8 1.5 %add_convert_fusion = bf16[256,2048]{1,0:T(8,128)(2,1)} fusion(f32[256,2048]{1,0:T(8,128)S(1)} %project.2, f32[256,2048]{1,0:T(8,128)S(1)} %collective-permute-done.32, bf16[256,2048]{1,0:T(8,128)(2,1)S(1)} %copy-done.1), kind=kLoop, calls=%fused_computation | loop fusion | flops 2097152 | bytes 6291456 | tf_op jit(solution)/shard_map/convert_element_type | solution.py:321
  (87 shorter events, 5.7 us)
Async XLA Ops:
  3.3 4.3 %collective-permute-start.1 = (bf16[8,2688]{1,0:T(8,128)(2,1)}, bf16[8,2688]{1,0:T(8,128)(2,1)S(1)}, u32[]{:S(2)}, u32[]{:S(2)}) collective-permute-start(bf16[8,2688]{1,0:T(8,128)(2,1)} %get-tuple-element.10), channel_id=1, source_target_pairs={{0,1},{1,0},{2,3},{3,2},{4,5},{5,4},{6,7},{7,6},{8,9},{9,8},{10,11... | collective-permute-start | bytes 129032 | tf_op jit(solution)/shard_map/ppermute | solution.py:31
  9.8 30.3 %all-to-all-start = ((bf16[8,16,1664]{2,1,0:T(8,128)(2,1)}), bf16[8,16,1664]{2,1,0:T(8,128)(2,1)S(1)}, u32[]{:S(2)}, u32[]{:S(2)}) async-start(bf16[8,16,1664]{2,1,0:T(8,128)(2,1)} %get-tuple-element.11), calls=%async_computation | async-start | bytes 851968 | tf_op jit(solution)/shard_map/all_to_all | solution.py:273
  16.3 4.2 %collective-permute-start.18 = (bf16[16,1024]{1,0:T(8,128)(2,1)}, bf16[16,1024]{1,0:T(8,128)(2,1)S(1)}, u32[]{:S(2)}, u32[]{:S(2)}) collective-permute-start(bf16[16,1024]{1,0:T(8,128)(2,1)} %get-tuple-element.12.refs_0_), channel_id=1, source_target_pairs={{0,2},{2,4},{4,6},{6,0},{1,3},{3,5},{5,7},{7,1},{8,10},{10,12},{12... | collective-permute-start | bytes 98312 | tf_op jit(solution)/shard_map/ppermute | solution.py:31
  17.5 3.3 %collective-permute-start.19 = (bf16[16,1024]{1,0:T(8,128)(2,1)}, bf16[16,1024]{1,0:T(8,128)(2,1)S(1)}, u32[]{:S(2)}, u32[]{:S(2)}) collective-permute-start(bf16[16,1024]{1,0:T(8,128)(2,1)} %get-tuple-element.12.refs_0_), channel_id=1, source_target_pairs={{0,6},{2,0},{4,2},{6,4},{1,7},{3,1},{5,3},{7,5},{8,14},{10,8},{12,... | collective-permute-start | bytes 98312 | tf_op jit(solution)/shard_map/ppermute | solution.py:31
  19.0 4.8 %collective-permute-start.20 = (bf16[16,1024]{1,0:T(8,128)(2,1)}, bf16[16,1024]{1,0:T(8,128)(2,1)S(1)}, u32[]{:S(2)}, u32[]{:S(2)}) collective-permute-start(bf16[16,1024]{1,0:T(8,128)(2,1)} %get-tuple-element.12.refs_0_), channel_id=1, source_target_pairs={{0,4},{2,6},{4,0},{6,2},{1,5},{3,7},{5,1},{7,3},{8,12},{10,14},{12... | collective-permute-start | bytes 98312 | tf_op jit(solution)/shard_map/ppermute | solution.py:31
  20.5 3.2 %copy-start.17 = (bf16[16,1024]{1,0:T(8,128)(2,1)}, bf16[16,1024]{1,0:T(8,128)(2,1)S(1)}, u32[]{:S(2)}) copy-start(bf16[16,1024]{1,0:T(8,128)(2,1)S(1)} %collective-permute-done.18.refs_1_) | copy-start | bytes 98308
  20.8 3.0 %copy-start.18 = (bf16[16,1024]{1,0:T(8,128)(2,1)}, bf16[16,1024]{1,0:T(8,128)(2,1)S(1)}, u32[]{:S(2)}) copy-start(bf16[16,1024]{1,0:T(8,128)(2,1)S(1)} %collective-permute-done.19.refs_2_) | copy-start | bytes 98308
  25.9 5.6 %collective-permute-start.21 = (bf16[4,16,1024]{2,1,0:T(8,128)(2,1)}, bf16[4,16,1024]{2,1,0:T(8,128)(2,1)S(1)}, u32[]{:S(2)}, u32[]{:S(2)}) collective-permute-start(bf16[4,16,1024]{2,1,0:T(8,128)(2,1)} %beside.6.refs_0_), channel_id=1, source_target_pairs={{0,8},{8,16},{16,24},{24,0},{1,9},{9,17},{17,25},{25,1},{2,10},{10... | collective-permute-start | bytes 393224 | tf_op jit(solution)/shard_map/ppermute | solution.py:31
  27.2 4.3 %collective-permute-start.22 = (bf16[4,16,1024]{2,1,0:T(8,128)(2,1)}, bf16[4,16,1024]{2,1,0:T(8,128)(2,1)S(1)}, u32[]{:S(2)}, u32[]{:S(2)}) collective-permute-start(bf16[4,16,1024]{2,1,0:T(8,128)(2,1)} %beside.6.refs_0_), channel_id=1, source_target_pairs={{0,24},{8,0},{16,8},{24,16},{1,25},{9,1},{17,9},{25,17},{2,26},{10... | collective-permute-start | bytes 393224 | tf_op jit(solution)/shard_map/ppermute | solution.py:31
  28.6 6.2 %collective-permute-start.23 = (bf16[4,16,1024]{2,1,0:T(8,128)(2,1)}, bf16[4,16,1024]{2,1,0:T(8,128)(2,1)S(1)}, u32[]{:S(2)}, u32[]{:S(2)}) collective-permute-start(bf16[4,16,1024]{2,1,0:T(8,128)(2,1)} %beside.6.refs_0_), channel_id=1, source_target_pairs={{0,16},{8,24},{16,0},{24,8},{1,17},{9,25},{17,1},{25,9},{2,18},{10... | collective-permute-start | bytes 393224 | tf_op jit(solution)/shard_map/ppermute | solution.py:31
  31.5 3.4 %copy-start.10 = (bf16[4,16,1024]{2,1,0:T(8,128)(2,1)}, bf16[4,16,1024]{2,1,0:T(8,128)(2,1)S(1)}, u32[]{:S(2)}) copy-start(bf16[4,16,1024]{2,1,0:T(8,128)(2,1)S(1)} %collective-permute-done.21.refs_1_) | copy-start | bytes 393220
  31.5 3.4 %copy-start.11 = (bf16[4,16,1024]{2,1,0:T(8,128)(2,1)}, bf16[4,16,1024]{2,1,0:T(8,128)(2,1)S(1)}, u32[]{:S(2)}) copy-start(bf16[4,16,1024]{2,1,0:T(8,128)(2,1)S(1)} %collective-permute-done.22.refs_2_) | copy-start | bytes 393220
  37.5 11.9 %collective-permute-start.24 = (bf16[256,1024]{1,0:T(8,128)(2,1)}, bf16[256,1024]{1,0:T(8,128)(2,1)S(1)}, u32[]{:S(2)}, u32[]{:S(2)}) collective-permute-start(bf16[256,1024]{1,0:T(8,128)(2,1)} %bitcast.6), channel_id=1, source_target_pairs={{0,32},{32,64},{64,96},{96,128},{128,160},{160,192},{192,224},{224... | collective-permute-start | bytes 1572872 | tf_op jit(solution)/shard_map/ppermute | solution.py:31
  38.7 22.3 %collective-permute-start.25 = (bf16[256,1024]{1,0:T(8,128)(2,1)}, bf16[256,1024]{1,0:T(8,128)(2,1)S(1)}, u32[]{:S(2)}, u32[]{:S(2)}) collective-permute-start(bf16[256,1024]{1,0:T(8,128)(2,1)} %bitcast.7), channel_id=1, source_target_pairs={{0,224},{32,0},{64,32},{96,64},{128,96},{160,128},{192,160},{224,1... | collective-permute-start | bytes 1572872 | tf_op jit(solution)/shard_map/ppermute | solution.py:31
  40.2 15.3 %copy-start.6 = (bf16[8,16,768]{2,1,0:T(8,128)(2,1)}, bf16[8,16,768]{2,1,0:T(8,128)(2,1)S(1)}, u32[]{:S(2)}) copy-start(bf16[8,16,768]{2,1,0:T(8,128)(2,1)S(1)} %slice.53.refs_0_) | copy-start | bytes 589828
  40.2 9.2 %collective-permute-start.10 = (bf16[8,16,768]{2,1,0:T(8,128)(2,1)S(1)}, bf16[8,16,768]{2,1,0:T(8,128)(2,1)S(1)}, u32[]{:S(2)}, u32[]{:S(2)}) collective-permute-start(bf16[8,16,768]{2,1,0:T(8,128)(2,1)S(1)} %slice.53.refs_0_), channel_id=1, source_target_pairs={{0,8},{8,16},{16,24},{24,0},{1,9},{9,17},{17,25},{25,1},{2,10},{10... | collective-permute-start | bytes 589832 | tf_op jit(solution)/shard_map/ppermute | solution.py:31
  40.3 9.2 %collective-permute-start.11 = (bf16[8,16,768]{2,1,0:T(8,128)(2,1)S(1)}, bf16[8,16,768]{2,1,0:T(8,128)(2,1)S(1)}, u32[]{:S(2)}, u32[]{:S(2)}) collective-permute-start(bf16[8,16,768]{2,1,0:T(8,128)(2,1)S(1)} %slice.53.refs_0_), channel_id=1, source_target_pairs={{0,24},{8,0},{16,8},{24,16},{1,25},{9,1},{17,9},{25,17},{2,26},{10... | collective-permute-start | bytes 589832 | tf_op jit(solution)/shard_map/ppermute | solution.py:31
  43.0 37.6 %copy-start.5 = (bf16[8,16,896]{2,1,0:T(8,128)(2,1)}, bf16[8,16,896]{2,1,0:T(8,128)(2,1)S(1)}, u32[]{:S(2)}) copy-start(bf16[8,16,896]{2,1,0:T(8,128)(2,1)S(1)} %slice.48.refs_0_) | copy-start | bytes 688132
  43.0 42.5 %copy-start.1 = (bf16[256,2048]{1,0:T(8,128)(2,1)S(1)}, bf16[256,2048]{1,0:T(8,128)(2,1)}, u32[]{:S(2)}) copy-start(bf16[256,2048]{1,0:T(8,128)(2,1)} %own.1) | copy-start | bytes 3145732
  43.0 15.5 %collective-permute-start.2 = (bf16[8,16,896]{2,1,0:T(8,128)(2,1)S(1)}, bf16[8,16,896]{2,1,0:T(8,128)(2,1)S(1)}, u32[]{:S(2)}, u32[]{:S(2)}) collective-permute-start(bf16[8,16,896]{2,1,0:T(8,128)(2,1)S(1)} %slice.48.refs_0_), channel_id=1, source_target_pairs={{0,2},{2,4},{4,6},{6,0},{1,3},{3,5},{5,7},{7,1},{8,10},{10,12},{12... | collective-permute-start | bytes 688136 | tf_op jit(solution)/shard_map/ppermute | solution.py:31
  49.4 33.5 %collective-permute-start.26 = (bf16[256,1024]{1,0:T(8,128)(2,1)S(1)}, bf16[256,1024]{1,0:T(8,128)(2,1)S(1)}, u32[]{:S(2)}, u32[]{:S(2)}) collective-permute-start(bf16[256,1024]{1,0:T(8,128)(2,1)S(1)} %collective-permute-done.24.refs_1_), channel_id=1, source_target_pairs={{0,32},{32,64},{64,96},{96,128},{128,160},{160,192},{192,224},{224... | collective-permute-start | bytes 1572872 | tf_op jit(solution)/shard_map/ppermute | solution.py:31
  49.4 2.9 %copy-start.8 = (bf16[8,16,768]{2,1,0:T(8,128)(2,1)}, bf16[8,16,768]{2,1,0:T(8,128)(2,1)S(1)}, u32[]{:S(2)}) copy-start(bf16[8,16,768]{2,1,0:T(8,128)(2,1)S(1)} %collective-permute-done.10.refs_1_) | copy-start | bytes 589828
  49.4 4.8 %collective-permute-start.12 = (bf16[4,16,768]{2,1,0:T(8,128)(2,1)S(1)}, bf16[4,16,768]{2,1,0:T(8,128)(2,1)S(1)}, u32[]{:S(2)}, u32[]{:S(2)}) collective-permute-start(bf16[4,16,768]{2,1,0:T(8,128)(2,1)S(1)} %slice.54), channel_id=1, source_target_pairs={{0,8},{8,16},{16,24},{24,0},{1,9},{9,17},{17,25},{25,1},{2,10},{10... | collective-permute-start | bytes 294920 | tf_op jit(solution)/shard_map/ppermute | solution.py:31
  49.5 4.7 %copy-start.9 = (bf16[8,16,768]{2,1,0:T(8,128)(2,1)}, bf16[8,16,768]{2,1,0:T(8,128)(2,1)S(1)}, u32[]{:S(2)}) copy-start(bf16[8,16,768]{2,1,0:T(8,128)(2,1)S(1)} %collective-permute-done.11.refs_2_) | copy-start | bytes 589828
  49.5 6.0 %collective-permute-start.13 = (bf16[4,16,768]{2,1,0:T(8,128)(2,1)S(1)}, bf16[4,16,768]{2,1,0:T(8,128)(2,1)S(1)}, u32[]{:S(2)}, u32[]{:S(2)}) collective-permute-start(bf16[4,16,768]{2,1,0:T(8,128)(2,1)S(1)} %slice.55), channel_id=1, source_target_pairs={{0,24},{8,0},{16,8},{24,16},{1,25},{9,1},{17,9},{25,17},{2,26},{10... | collective-permute-start | bytes 294920 | tf_op jit(solution)/shard_map/ppermute | solution.py:31
  54.2 7.0 %collective-permute-start.3 = (bf16[8,16,896]{2,1,0:T(8,128)(2,1)S(1)}, bf16[8,16,896]{2,1,0:T(8,128)(2,1)}, u32[]{:S(2)}, u32[]{:S(2)}) collective-permute-start(bf16[8,16,896]{2,1,0:T(8,128)(2,1)S(1)} %slice.48.refs_0_), channel_id=1, source_target_pairs={{0,6},{2,0},{4,2},{6,4},{1,7},{3,1},{5,3},{7,5},{8,14},{10,8},{12,... | collective-permute-start | bytes 688136 | tf_op jit(solution)/shard_map/ppermute | solution.py:31
  58.4 34.3 %collective-permute-start.14 = (bf16[8,4,16,768]{3,2,1,0:T(8,128)(2,1)}, bf16[8,4,16,768]{3,2,1,0:T(8,128)(2,1)}, u32[]{:S(2)}, u32[]{:S(2)}) collective-permute-start(bf16[8,4,16,768]{3,2,1,0:T(8,128)(2,1)} %beside.5.refs_5_), channel_id=1, source_target_pairs={{0,2},{2,4},{4,6},{6,0},{1,3},{3,5},{5,7},{7,1},{8,10},{10,12},{12... | collective-permute-start | bytes 2359304 | tf_op jit(solution)/shard_map/ppermute | solution.py:31
  58.5 34.7 %collective-permute-start.15 = (bf16[8,4,16,768]{3,2,1,0:T(8,128)(2,1)}, bf16[8,4,16,768]{3,2,1,0:T(8,128)(2,1)}, u32[]{:S(2)}, u32[]{:S(2)}) collective-permute-start(bf16[8,4,16,768]{3,2,1,0:T(8,128)(2,1)} %beside.5.refs_5_), channel_id=1, source_target_pairs={{0,6},{2,0},{4,2},{6,4},{1,7},{3,1},{5,3},{7,5},{8,14},{10,8},{12,... | collective-permute-start | bytes 2359304 | tf_op jit(solution)/shard_map/ppermute | solution.py:31
  61.1 14.2 %collective-permute-start.4 = (bf16[4,16,896]{2,1,0:T(8,128)(2,1)S(1)}, bf16[4,16,896]{2,1,0:T(8,128)(2,1)S(1)}, u32[]{:S(2)}, u32[]{:S(2)}) collective-permute-start(bf16[4,16,896]{2,1,0:T(8,128)(2,1)S(1)} %slice.49), channel_id=1, source_target_pairs={{0,2},{2,4},{4,6},{6,0},{1,3},{3,5},{5,7},{7,1},{8,10},{10,12},{12... | collective-permute-start | bytes 344072 | tf_op jit(solution)/shard_map/ppermute | solution.py:31
  61.2 24.3 %collective-permute-start.27 = (bf16[256,1024]{1,0:T(8,128)(2,1)S(1)}, bf16[256,1024]{1,0:T(8,128)(2,1)S(1)}, u32[]{:S(2)}, u32[]{:S(2)}) collective-permute-start(bf16[256,1024]{1,0:T(8,128)(2,1)S(1)} %collective-permute-done.25.refs_2_), channel_id=1, source_target_pairs={{0,224},{32,0},{64,32},{96,64},{128,96},{160,128},{192,160},{224,1... | collective-permute-start | bytes 1572872 | tf_op jit(solution)/shard_map/ppermute | solution.py:31
  75.3 5.3 %copy-start.13 = (bf16[4,16,896]{2,1,0:T(8,128)(2,1)}, bf16[4,16,896]{2,1,0:T(8,128)(2,1)S(1)}, u32[]{:S(2)}) copy-start(bf16[4,16,896]{2,1,0:T(8,128)(2,1)S(1)} %collective-permute-done.4.refs_3_) | copy-start | bytes 344068
  75.3 5.3 %collective-permute-start.5 = (bf16[4,16,896]{2,1,0:T(8,128)(2,1)S(1)}, bf16[4,16,896]{2,1,0:T(8,128)(2,1)}, u32[]{:S(2)}, u32[]{:S(2)}) collective-permute-start(bf16[4,16,896]{2,1,0:T(8,128)(2,1)S(1)} %slice.50), channel_id=1, source_target_pairs={{0,6},{2,0},{4,2},{6,4},{1,7},{3,1},{5,3},{7,5},{8,14},{10,8},{12,... | collective-permute-start | bytes 344072 | tf_op jit(solution)/shard_map/ppermute | solution.py:31
  82.8 16.8 %collective-permute-start.6 = (bf16[8,4,16,896]{3,2,1,0:T(8,128)(2,1)}, bf16[8,4,16,896]{3,2,1,0:T(8,128)(2,1)S(1)}, u32[]{:S(2)}, u32[]{:S(2)}) collective-permute-start(bf16[8,4,16,896]{3,2,1,0:T(8,128)(2,1)} %beside.4.refs_0_), channel_id=1, source_target_pairs={{0,8},{8,16},{16,24},{24,0},{1,9},{9,17},{17,25},{25,1},{2,10},{10... | collective-permute-start | bytes 2752520 | tf_op jit(solution)/shard_map/ppermute | solution.py:31
  82.9 16.8 %collective-permute-start.7 = (bf16[8,4,16,896]{3,2,1,0:T(8,128)(2,1)}, bf16[8,4,16,896]{3,2,1,0:T(8,128)(2,1)S(1)}, u32[]{:S(2)}, u32[]{:S(2)}) collective-permute-start(bf16[8,4,16,896]{3,2,1,0:T(8,128)(2,1)} %beside.4.refs_0_), channel_id=1, source_target_pairs={{0,24},{8,0},{16,8},{24,16},{1,25},{9,1},{17,9},{25,17},{2,26},{10... | collective-permute-start | bytes 2752520 | tf_op jit(solution)/shard_map/ppermute | solution.py:31
  85.5 25.2 %collective-permute-start = (bf16[256,2048]{1,0:T(8,128)(2,1)S(1)}, bf16[256,2048]{1,0:T(8,128)(2,1)S(1)}, u32[]{:S(2)}, u32[]{:S(2)}) collective-permute-start(bf16[256,2048]{1,0:T(8,128)(2,1)S(1)} %copy-done.1), channel_id=1, source_target_pairs={{0,1},{1,0},{2,3},{3,2},{4,5},{5,4},{6,7},{7,6},{8,9},{9,8},{10,11... | collective-permute-start | bytes 3145736 | tf_op jit(solution)/shard_map/ppermute | solution.py:31
  92.6 14.6 %collective-permute-start.28 = (bf16[256,1024]{1,0:T(8,128)(2,1)S(1)}, bf16[256,1024]{1,0:T(8,128)(2,1)S(1)}, u32[]{:S(2)}, u32[]{:S(2)}) collective-permute-start(bf16[256,1024]{1,0:T(8,128)(2,1)S(1)} %collective-permute-done.26.refs_3_), channel_id=1, source_target_pairs={{0,32},{32,64},{64,96},{96,128},{128,160},{160,192},{192,224},{224... | collective-permute-start | bytes 1572872 | tf_op jit(solution)/shard_map/ppermute | solution.py:31
  93.2 14.1 %collective-permute-start.29 = (bf16[256,1024]{1,0:T(8,128)(2,1)S(1)}, bf16[256,1024]{1,0:T(8,128)(2,1)S(1)}, u32[]{:S(2)}, u32[]{:S(2)}) collective-permute-start(bf16[256,1024]{1,0:T(8,128)(2,1)S(1)} %collective-permute-done.27.refs_4_), channel_id=1, source_target_pairs={{0,224},{32,0},{64,32},{96,64},{128,96},{160,128},{192,160},{224,1... | collective-permute-start | bytes 1572872 | tf_op jit(solution)/shard_map/ppermute | solution.py:31
  96.4 20.8 %copy-start.2 = (bf16[8,4,16,896]{3,2,1,0:T(8,128)(2,1)S(1)}, bf16[8,4,16,896]{3,2,1,0:T(8,128)(2,1)}, u32[]{:S(2)}) copy-start(bf16[8,4,16,896]{3,2,1,0:T(8,128)(2,1)} %beside.4.refs_0_) | copy-start | bytes 2752516
  96.4 20.8 %copy-start.3 = (bf16[8,4,16,768]{3,2,1,0:T(8,128)(2,1)S(1)}, bf16[8,4,16,768]{3,2,1,0:T(8,128)(2,1)}, u32[]{:S(2)}) copy-start(bf16[8,4,16,768]{3,2,1,0:T(8,128)(2,1)} %beside.5.refs_5_) | copy-start | bytes 2359300
  96.4 20.8 %copy-start.4 = (s32[4]{0:T(128)S(1)}, s32[4]{0:T(128)}, u32[]{:S(2)}) copy-start(s32[4]{0:T(128)} %pad_add_fusion.at) | copy-start | bytes 52
  99.6 12.0 %collective-permute-start.16 = (bf16[4,4,16,768]{3,2,1,0:T(8,128)(2,1)S(1)}, bf16[4,4,16,768]{3,2,1,0:T(8,128)(2,1)S(1)}, u32[]{:S(2)}, u32[]{:S(2)}) collective-permute-start(bf16[4,4,16,768]{3,2,1,0:T(8,128)(2,1)S(1)} %slice.56), channel_id=1, source_target_pairs={{0,2},{2,4},{4,6},{6,0},{1,3},{3,5},{5,7},{7,1},{8,10},{10,12},{12... | collective-permute-start | bytes 1179656 | tf_op jit(solution)/shard_map/ppermute | solution.py:31
  99.7 14.1 %collective-permute-start.17 = (bf16[4,4,16,768]{3,2,1,0:T(8,128)(2,1)S(1)}, bf16[4,4,16,768]{3,2,1,0:T(8,128)(2,1)S(1)}, u32[]{:S(2)}, u32[]{:S(2)}) collective-permute-start(bf16[4,4,16,768]{3,2,1,0:T(8,128)(2,1)S(1)} %slice.57), channel_id=1, source_target_pairs={{0,6},{2,0},{4,2},{6,4},{1,7},{3,1},{5,3},{7,5},{8,14},{10,8},{12,... | collective-permute-start | bytes 1179656 | tf_op jit(solution)/shard_map/ppermute | solution.py:31
  107.2 10.0 %collective-permute-start.8 = (bf16[4,4,16,896]{3,2,1,0:T(8,128)(2,1)S(1)}, bf16[4,4,16,896]{3,2,1,0:T(8,128)(2,1)S(1)}, u32[]{:S(2)}, u32[]{:S(2)}) collective-permute-start(bf16[4,4,16,896]{3,2,1,0:T(8,128)(2,1)S(1)} %slice.51), channel_id=1, source_target_pairs={{0,8},{8,16},{16,24},{24,0},{1,9},{9,17},{17,25},{25,1},{2,10},{10... | collective-permute-start | bytes 1376264 | tf_op jit(solution)/shard_map/ppermute | solution.py:31
  107.2 10.0 %collective-permute-start.9 = (bf16[4,4,16,896]{3,2,1,0:T(8,128)(2,1)S(1)}, bf16[4,4,16,896]{3,2,1,0:T(8,128)(2,1)S(1)}, u32[]{:S(2)}, u32[]{:S(2)}) collective-permute-start(bf16[4,4,16,896]{3,2,1,0:T(8,128)(2,1)S(1)} %slice.52), channel_id=1, source_target_pairs={{0,24},{8,0},{16,8},{24,16},{1,25},{9,1},{17,9},{25,17},{2,26},{10... | collective-permute-start | bytes 1376264 | tf_op jit(solution)/shard_map/ppermute | solution.py:31
  110.8 25.3 %collective-permute-start.30 = (bf16[128,1024]{1,0:T(8,128)(2,1)S(1)}, bf16[128,1024]{1,0:T(8,128)(2,1)S(1)}, u32[]{:S(2)}, u32[]{:S(2)}) collective-permute-start(bf16[128,1024]{1,0:T(8,128)(2,1)S(1)} %slice.58), channel_id=1, source_target_pairs={{0,32},{32,64},{64,96},{96,128},{128,160},{160,192},{192,224},{224... | collective-permute-start | bytes 786440 | tf_op jit(solution)/shard_map/ppermute | solution.py:31
  111.7 24.4 %collective-permute-start.31 = (bf16[128,1024]{1,0:T(8,128)(2,1)S(1)}, bf16[128,1024]{1,0:T(8,128)(2,1)S(1)}, u32[]{:S(2)}, u32[]{:S(2)}) collective-permute-start(bf16[128,1024]{1,0:T(8,128)(2,1)S(1)} %slice.59), channel_id=1, source_target_pairs={{0,224},{32,0},{64,32},{96,64},{128,96},{160,128},{192,160},{224,1... | collective-permute-start | bytes 786440 | tf_op jit(solution)/shard_map/ppermute | solution.py:31
  117.2 18.9 %copy-start = (bf16[4,4,16,1024]{3,2,1,0:T(8,128)(2,1)S(1)}, bf16[4,4,16,1024]{3,2,1,0:T(8,128)(2,1)}, u32[]{:S(2)}) copy-start(bf16[4,4,16,1024]{3,2,1,0:T(8,128)(2,1)} %beside.7) | copy-start | bytes 1572868
  139.8 8.0 %collective-permute-start.32 = (f32[256,2048]{1,0:T(8,128)S(1)}, f32[256,2048]{1,0:T(8,128)S(1)}, u32[]{:S(2)}, u32[]{:S(2)}) collective-permute-start(f32[256,2048]{1,0:T(8,128)S(1)} %project.3), channel_id=1, source_target_pairs={{0,1},{1,0},{2,3},{3,2},{4,5},{5,4},{6,7},{7,6},{8,9},{9,8},{10,11... | collective-permute-start | bytes 6291464 | tf_op jit(solution)/shard_map/ppermute | solution.py:31
  (6 other events, 6.5 us)

commit v3 on v2

v3 whole, which is shorter than its diff:
```python
import functools

import jax
import jax.numpy as jnp
from jax import lax
from jax.experimental import pallas as pl
from jax.experimental.pallas import tpu as pltpu
from jax.sharding import Mesh
from jax.sharding import PartitionSpec as P


HD = 64
PAD = 128
AXES = ("z", "y", "x", "c")
VMEM = pl.BlockSpec(memory_space=pltpu.VMEM)
SMEM = pl.BlockSpec(memory_space=pltpu.SMEM)
ANY = pl.BlockSpec(memory_space=pl.ANY)
F32 = jnp.float32
BF16 = jnp.bfloat16

rope_base = 500000.0
norm_eps = 1e-05


def shape_of(dims, dtype=BF16):
    return jax.ShapeDtypeStruct(tuple(dims), dtype)


def shift(array, axis, by):
    n = lax.axis_size(axis)
    return lax.ppermute(array, axis, [(i, (i + by) % n) for i in range(n)])


def halves_kernel(at, gain, wk, wv, wq, wo, copies, mine, theirs):
    core = at[0]
    rows = wq.shape[0]
    eye = lax.broadcasted_iota(jnp.int32, (rows, rows), 0) == lax.broadcasted_iota(jnp.int32, (rows, rows), 1)
    column = jnp.sum(jnp.where(eye, gain[...].astype(F32), 0.0), axis=1, keepdims=True)
    wide = jnp.broadcast_to(column, (rows, PAD)).astype(BF16)
    for which in range(2):
        pieces = []
        for ref in (wk, wv, wq):
            n = ref.shape[1] // 2
            pieces.append(ref[:, which * n : (which + 1) * n])
        row = jnp.concatenate(pieces[:2] + [wide] + pieces[2:], axis=1)
        for z in range(copies.shape[0] // 2):
            copies[2 * z + which] = row
    n = wo.shape[1] // 2
    mine[...] = wo[:, pl.ds(pl.multiple_of(core * n, 128), n)]
    theirs[...] = wo[:, pl.ds(pl.multiple_of((1 - core) * n, 128), n)]


def order_kernel(at, mine, got, out):
    rows = mine.shape[0]
    for k in range(2):
        out[k * rows : (k + 1) * rows, :] = jnp.where(at[0] == k, mine[...], got[...])


def split_kernel(by_z, a, b):
    n, m = a.shape[3], b.shape[2]
    for k in range(a.shape[0]):
        a[k] = by_z[:, :, 0:n]
    b[...] = by_z[:, :, n : n + m]


def to_all(array, axes):
    return lax.all_to_all(array, axes, split_axis=0, concat_axis=0, tiled=True)


def beside_kernel(dim, n, slot, at, *refs):
    *pieces, out = refs
    me = at[slot]
    for by, ref in zip((0, n - 1, 1, 2, 2), pieces):
        index = lax.rem(me + by, n)
        if dim == 0:
            out[index] = ref[...]
        elif ref.shape[0] == out.shape[0]:
            out[:, pl.ds(index, 1)] = ref[...][:, None]
    if dim == 1:
        low, high = pieces[3], pieces[4]
        half = low.shape[0]
        index = lax.rem(me + 2, n)
        out[0:half, pl.ds(index, 1)] = low[...][:, None]
        out[half : 2 * half, pl.ds(index, 1)] = high[...][:, None]


def beside(at, slot, pieces, dim):
    dims = list(pieces[0].shape)
    dims.insert(dim, 4)
    return pl.pallas_call(
        functools.partial(beside_kernel, dim, 4, slot),
        out_shape=shape_of(dims),
        in_specs=[SMEM] + [VMEM] * len(pieces),
        out_specs=VMEM,
        name="beside",
    )(at, *pieces)


def ring4(block, axis):
    half = block.shape[0] // 2
    back = shift(block, axis, 1)
    ahead = shift(block, axis, -1)
    low = shift(back[:half], axis, 1)
    high = shift(ahead[half:], axis, -1)
    return block, back, ahead, low, high


def direct4(at, slot, block, axis):
    back = shift(block, axis, 1)
    ahead = shift(block, axis, -1)
    far = shift(block, axis, 2)
    return beside(at, slot, (block, back, ahead, far), 0)


def ring8(block, axis):
    half = block.shape[0] // 2
    back = ahead = block
    pieces = [block]
    for _ in range(3):
        back = shift(back, axis, 1)
        ahead = shift(ahead, axis, -1)
        pieces += [back, ahead]
    return (*pieces, shift(back[:half], axis, 1), shift(ahead[half:], axis, -1))


def attend_kernel(tokens, at, own, other, cos_ref, sin_ref, *refs):
    a_pieces, b_pieces = refs[0:5], refs[5:10]
    ctx, w_a, w_b, normed, q_s, k_s, v_s, sems = refs[10:]
    width = own.shape[1]
    x_at, y_at = at[1], at[2]
    a_copies, b_copies = [], []
    for i, (by, start, size) in enumerate(((0, 0, 1), (3, 0, 1), (1, 0, 1), (2, 0, 2), (2, 1, 2))):
        y_from = lax.rem(y_at + by, 4)
        x_from = lax.rem(x_at + by, 4)
        for j in range(4 // size):
            a_copies.append(
                pltpu.make_async_copy(
                    a_pieces[i].at[j], w_a.at[:, y_from, j + start * 2], sems.at[4 * i + j]
                )
            )
        z = pl.ds(start * 4, 8 // size)
        b_copies.append(pltpu.make_async_copy(b_pieces[i], w_b.at[z, :, x_from], sems.at[20 + i]))
    for c in a_copies:
        c.start()
    n = k_s.shape[1]
    for c in a_copies:
        c.wait()
    for c in b_copies:
        c.start()
    gain = w_a[:, :, :, :, 2 * n : 2 * n + PAD].reshape(width // PAD, PAD, PAD).astype(F32)
    eye = lax.broadcasted_iota(jnp.int32, (PAD, PAD), 0) == lax.broadcasted_iota(jnp.int32, (PAD, PAD), 1)
    lanes = jnp.concatenate(
        [jnp.sum(jnp.where(eye, gain[i], 0.0), axis=0, keepdims=True) for i in range(width // PAD)], axis=1
    )
    step = 32

    def norm(i, _):
        for s, ref in enumerate((own, other)):
            start = pl.multiple_of(i * step, step)
            x = ref[pl.ds(start, step), :].astype(F32)
            inv = lax.rsqrt(jnp.sum(x * x, axis=1, keepdims=True) * (1.0 / width) + norm_eps)
            normed[pl.ds(s * tokens + start, step), :] = (x * inv * lanes).astype(BF16)
        return 0

    lax.fori_loop(0, tokens // step, norm, 0)

    low_half = (lax.broadcasted_iota(jnp.int32, (2 * tokens, 2 * HD), 1) % HD) < HD // 2

    def rope(t):
        turned = jnp.where(low_half, -pltpu.roll(t, 2 * HD - HD // 2, 1), pltpu.roll(t, HD // 2, 1))
        both = lambda ref: jnp.concatenate([ref[...], ref[...]], axis=0)
        return t * both(cos_ref) + turned * both(sin_ref)

    def product(ref, start):
        weights = ref[:, :, :, :, start : start + n].reshape(width, n)
        return jnp.dot(normed[...], weights, preferred_element_type=F32)

    def store(t, to, start):
        for j in range(n // (2 * HD)):
            cols = slice(j * 2 * HD, (j + 1) * 2 * HD)
            to[:, start + j * 2 * HD : start + (j + 1) * 2 * HD] = rope(t[:, cols]).astype(BF16)

    store(product(w_a, 0), k_s, 0)
    v_s[...] = product(w_a, n).astype(BF16)
    store(product(w_a, 2 * n + PAD), q_s, 0)
    for c in b_copies:
        c.wait()
    for k in range(3):
        store(product(w_b, k * n), q_s, (k + 1) * n)

    seen = lax.broadcasted_iota(jnp.int32, (tokens, tokens), 0) >= lax.broadcasted_iota(
        jnp.int32, (tokens, tokens), 1
    )
    left = lax.broadcasted_iota(jnp.int32, (tokens, 2 * HD), 1) < HD

    def softmax(scores):
        scores = jnp.where(seen, scores, -1e30)
        expo = jnp.exp(scores - jnp.max(scores, axis=1, keepdims=True))
        return (expo * (1.0 / jnp.sum(expo, axis=1, keepdims=True))).astype(BF16)

    def attend(s, _):
        rows = pl.ds(pl.multiple_of(s * tokens, tokens), tokens)
        for kv in range(4):

            def sides(ref, scale):
                tile = ref[rows, (kv // 2) * 2 * HD : (kv // 2 + 1) * 2 * HD].astype(F32) * scale
                a = jnp.where(left, tile if kv % 2 == 0 else pltpu.roll(tile, HD, 1), 0.0)
                return jnp.concatenate([a, pltpu.roll(a, HD, 1)], axis=0).astype(BF16)

            pairs = [slice((kv * 2 + p) * 2 * HD, (kv * 2 + p + 1) * 2 * HD) for p in range(2)]
            scores = lax.dot_general(
                jnp.concatenate([q_s[rows, cols] for cols in pairs], axis=0),
                sides(k_s, HD**-0.5),
                (((1,), (1,)), ((), ())),
                preferred_element_type=F32,
            )
            block = lambda i, j: scores[i * tokens : (i + 1) * tokens, j * tokens : (j + 1) * tokens]
            probs = jnp.concatenate(
                [jnp.concatenate([softmax(block(i, j)) for j in range(2)], axis=1) for i in range(2)], axis=0
            )
            out = jnp.dot(probs, sides(v_s, 1.0), preferred_element_type=F32).astype(BF16)
            for p, cols in enumerate(pairs):
                ctx[rows, cols] = out[p * tokens : (p + 1) * tokens]
        return 0

    lax.fori_loop(0, 2, attend, 0)


def project_kernel(seq, tokens, at, ctx, *refs):
    pieces = refs[0:9]
    out, w_o, sems = refs[9:]
    z_at = at[3]
    rows = w_o.shape[1]
    half = rows // 2
    copies = []
    for i, by in enumerate((0, 7, 1, 6, 2, 5, 3, 4, 4)):
        z_from = lax.rem(z_at + by, 8)
        to = w_o.at[z_from]
        if i == 7:
            to = w_o.at[z_from, 0:half]
        if i == 8:
            to = w_o.at[z_from, half:rows]
        copies.append(pltpu.make_async_copy(pieces[i], to, sems.at[i]))
    for c in copies:
        c.start()
    for c in copies:
        c.wait()

    def one(z, _):
        out[:, pl.ds(pl.multiple_of(z * rows, rows), rows)] = lax.dot_general(
            ctx[seq * tokens : (seq + 1) * tokens, :],
            w_o[z],
            (((1,), (1,)), ((), ())),
            preferred_element_type=F32,
        )
        return 0

    lax.fori_loop(0, 8, one, 0)


def inner(hidden, attn_gain, w_query, w_key, w_value, w_out):
    tokens, width = hidden.shape
    wq, wkv = w_query.shape[1] // 2, w_key.shape[1] // 2
    rows = w_query.shape[0]
    cols = wq + 2 * wkv + PAD
    cols_a = 3 * wkv + PAD
    cols_b = cols - cols_a
    at = jnp.stack([lax.axis_index(a) for a in ("c", "x", "y", "z")]).astype(jnp.int32)

    gain = attn_gain[None]
    copies, mine, theirs = pl.pallas_call(
        halves_kernel,
        out_shape=(shape_of((16, rows, cols)), shape_of((rows, wq)), shape_of((rows, wq))),
        in_specs=[SMEM] + [VMEM] * 5,
        out_specs=(VMEM,) * 3,
        name="halves",
    )(at, gain, w_key, w_value, w_query, w_out.T)
    by_z = to_all(copies, ("z", "c")).reshape(8, 2 * rows, cols)
    got = shift(theirs, "c", 1)
    out_rows = pl.pallas_call(
        order_kernel,
        out_shape=shape_of((2 * rows, wq)),
        in_specs=[SMEM, VMEM, VMEM],
        out_specs=VMEM,
        name="order",
    )(at, mine, got)
    other = shift(hidden, "c", 1)
    side_a, side_b = pl.pallas_call(
        split_kernel,
        out_shape=(shape_of((4, 8, 2 * rows, cols_a)), shape_of((8, 2 * rows, cols_b))),
        in_specs=[VMEM],
        out_specs=(VMEM,) * 2,
        name="split",
    )(by_z)
    out_x = direct4(at, 1, out_rows, "x")
    out_xy = direct4(at, 2, out_x, "y").reshape(-1, wq)
    out_pieces = ring8(out_xy, "z")
    block_a = to_all(side_a, "x")
    block_b = beside(at, 2, ring4(side_b, "y"), 1)
    a_pieces = ring4(block_a, "y")
    b_pieces = ring4(block_b, "x")

    position = jnp.arange(tokens, dtype=F32)
    freq = rope_base ** (-(jnp.arange(HD // 2, dtype=F32) * 2.0) / HD)
    angle = position[:, None] * freq[None, :]
    cos_table = jnp.concatenate([jnp.cos(angle)] * 4, axis=-1)
    sin_table = jnp.concatenate([jnp.sin(angle)] * 4, axis=-1)

    context = pl.pallas_call(
        functools.partial(attend_kernel, tokens),
        out_shape=shape_of((2 * tokens, wq)),
        in_specs=[SMEM] + [VMEM] * 4 + [ANY] * 10,
        out_specs=VMEM,
        scratch_shapes=[
            pltpu.VMEM((8, 4, 4, 2 * rows, cols_a), BF16),
            pltpu.VMEM((8, 4, 4, 2 * rows, cols_b), BF16),
            pltpu.VMEM((2 * tokens, width), BF16),
            pltpu.VMEM((2 * tokens, wq), BF16),
            pltpu.VMEM((2 * tokens, wkv), BF16),
            pltpu.VMEM((2 * tokens, wkv), BF16),
            pltpu.SemaphoreType.DMA((25,)),
        ],
        cost_estimate=pl.CostEstimate(
            flops=4_000_000_000, bytes_accessed=10_000_000, transcendentals=0
        ),
        compiler_params=pltpu.CompilerParams(vmem_limit_bytes=40 * 1024 * 1024),
        name="att",
    )(at, hidden, other, cos_table, sin_table, *a_pieces, *b_pieces)

    def project(seq):
        return pl.pallas_call(
            functools.partial(project_kernel, seq, tokens),
            out_shape=shape_of((tokens, width), F32),
            in_specs=[SMEM, VMEM] + [ANY] * 9,
            out_specs=VMEM,
            scratch_shapes=[pltpu.VMEM((8, width // 8, wq), BF16), pltpu.SemaphoreType.DMA((9,))],
            cost_estimate=pl.CostEstimate(flops=1_000_000_000, bytes_accessed=8_000_000, transcendentals=0),
            compiler_params=pltpu.CompilerParams(vmem_limit_bytes=24 * 1024 * 1024),
            name="project",
        )(at, context, *out_pieces)

    from_them = shift(project(1), "c", 1)
    return (hidden.astype(F32) + (project(0) + from_them)).astype(BF16)


def solution(mesh):
    torus = Mesh(mesh.devices.reshape(8, 4, 4, 2), AXES)
    placed = (P(AXES, None), P(AXES), P(AXES, None), P(AXES, None), P(AXES, None), P(None, AXES))
    return jax.shard_map(inner, mesh=torus, in_specs=placed, out_specs=P(AXES, None), check_vma=False)
```

time: 150 us -> 130 us (0.87); the launches traced: 149 us -> 128 us
  waiting for transfers between devices: 42.8 us -> 21.7 us
  starting transfers between devices: 59.1 us -> 64.3 us
  Pallas kernels: 37.1 us -> 33 us
  local copies, waits for them, and re-layouts: 7.13 us -> 5.57 us
    ppermute x33 -> x29, waiting for transfers between devices: 42.8 us -> 21.7 us  [shift(): return lax.ppermute(array, axis, [(i, (i + by) % n) for i in range(n)])]
    all_to_all x1 -> x2, starting transfers between devices: 6.48 us -> 14.2 us  [to_all(): return lax.all_to_all(array, axes, split_axis=0, concat_axis=0, tiled=True)]
    pallas_call x1, Pallas kernels: 18.8 us -> 15 us  [inner(): pl.pallas_call(functools.partial(attend_kernel, tokens), out_shape=shape_...]
    ppermute x33 -> x29, starting transfers between devices: 52.6 us -> 50.1 us  [shift(): return lax.ppermute(array, axis, [(i, (i + by) % n) for i in range(n)])]
    pallas_call x4 -> x3, Pallas kernels: 7.92 us -> 5.58 us  [beside(): pl.pallas_call(functools.partial(beside_kernel, dim, 4, slot), out_shape=...]
    pallas_call x2 -> x3, Pallas kernels: 3.07 us -> 5.17 us  [the longest x1 2.13 us: inner(): pl.pallas_call(split_kernel, out_shape=(shape_of((4, 8, 2 * rows, cols_a)...]
    unnamed x40 -> x32, local copies, waits for them, and re-layouts: 2.58 us -> 3.33 us
  transfers between devices with their start and end apart: 34 -> 31, of which waited for: 13 -> 11; matrix products, arithmetic and copies ran while one was open for 3% -> 2% of each run, Pallas kernels for 20% -> 22%
where the time goes in v3:
time: 130 us; the launch traced here: 128 us
  starting transfers between devices  64.3 us (49%)
  Pallas kernels  33 us (25%)
  waiting for transfers between devices  21.7 us (17%)
  local copies, waits for them, and re-layouts  5.57 us (4%)
  other arithmetic  2.9 us (2%)
    ppermute x29, starting transfers between devices, shift(): return lax.ppermute(array, axis, [(i, (i + by) % n) for i in range(n)])  50.1 us
    ppermute x29, waiting for transfers between devices, shift(): return lax.ppermute(array, axis, [(i, (i + by) % n) for i in range(n)])  21.7 us
    pallas_call x1, Pallas kernels, inner(): pl.pallas_call(functools.partial(attend_kernel, tokens), out_shape=shape_...  15 us
    all_to_all x2, starting transfers between devices, to_all(): return lax.all_to_all(array, axes, split_axis=0, concat_axis=0, tiled=True)  14.2 us
    pallas_call x2, Pallas kernels, project(): pl.pallas_call(functools.partial(project_kernel, seq, tokens), out_shape=...  7.28 us
    pallas_call x3, Pallas kernels, beside(): pl.pallas_call(functools.partial(beside_kernel, dim, 4, slot), out_shape=...  5.58 us
    unnamed x32, local copies, waits for them, and re-layouts  3.33 us
  transfers between devices with their start and end apart: 31, of which 11 were waited for; matrix products, arithmetic and copies ran while one was open for 2% of the time, Pallas kernels for 22%

profile of v3, /device:TPU:1, one launch (start us, length us, event | category | flops | bytes accessed | tf_op | source)
XLA Modules:
  0.0 127.8 jit_solution(3796909678742122533)
XLA Ops:
  0.6 1.7 %halves.1 = (bf16[16,8,1664]{2,1,0:T(8,128)(2,1)}, bf16[8,1024]{1,0:T(8,128)(2,1)}, bf16[8,1024]{1,0:T(8,128)(2,1)}) custom-call(s32[4]{0:T(128)} %pad_add_fusion.at, bf16[1,8]{1,0:T(2,128)(2,1)} %bitcast.14, bf16[8,512]{1,0:T(8,128)(2,1)} %wk.1, bf16[8,512]{1,0:T(8,128)(2,1)} %wv.1, bf16[8,2048]{1,0:T(8,128)(2,1)} %wq.1, bf16[8,2048]{1,0:T(8,128)(2,1)} %bitcast.13), custom_call_target="tpu_custom_call" | custom-call | tf_op jit(solution)/shard_map/halves/pallas_call | solution.py:271
  2.3 10.0 %all-to-all-start = ((bf16[16,8,1664]{2,1,0:T(8,128)(2,1)}), bf16[16,8,1664]{2,1,0:T(8,128)(2,1)S(1)}, u32[]{:S(2)}, u32[]{:S(2)}) async-start(bf16[16,8,1664]{2,1,0:T(8,128)(2,1)} %get-tuple-element.10), calls=%async_computation | async-start | bytes 851968 | tf_op jit(solution)/shard_map/all_to_all | solution.py:67
  12.4 1.2 collective-permute-done.13.got
  14.2 1.4 %order.1.refs_0_ = bf16[16,1024]{1,0:T(8,128)(2,1)} custom-call(s32[4]{0:T(128)} %pad_add_fusion.at, bf16[8,1024]{1,0:T(8,128)(2,1)} %get-tuple-element.13.mine, bf16[8,1024]{1,0:T(8,128)(2,1)} %copy-done.15), custom_call_target="tpu_custom_call" | custom-call | tf_op jit(solution)/shard_map/order/pallas_call | solution.py:280
  15.6 1.2 collective-permute-start.14
  16.8 1.5 %collective-permute-start.15 = (bf16[16,1024]{1,0:T(8,128)(2,1)}, bf16[16,1024]{1,0:T(8,128)(2,1)S(1)}, u32[]{:S(2)}, u32[]{:S(2)}) collective-permute-start(bf16[16,1024]{1,0:T(8,128)(2,1)} %order.1.refs_0_), channel_id=1, source_target_pairs={{0,6},{2,0},{4,2},{6,4},{1,7},{3,1},{5,3},{7,5},{8,14},{10,8},{12,... | collective-permute-start | bytes 98312 | tf_op jit(solution)/shard_map/ppermute | solution.py:31
  18.3 1.5 %collective-permute-start.16 = (bf16[16,1024]{1,0:T(8,128)(2,1)}, bf16[16,1024]{1,0:T(8,128)(2,1)S(1)}, u32[]{:S(2)}, u32[]{:S(2)}) collective-permute-start(bf16[16,1024]{1,0:T(8,128)(2,1)} %order.1.refs_0_), channel_id=1, source_target_pairs={{0,4},{2,6},{4,0},{6,2},{1,5},{3,7},{5,1},{7,3},{8,12},{10,14},{12... | collective-permute-start | bytes 98312 | tf_op jit(solution)/shard_map/ppermute | solution.py:31
  20.1 3.0 %collective-permute-done.16.refs_3_ = bf16[16,1024]{1,0:T(8,128)(2,1)S(1)} collective-permute-done((bf16[16,1024]{1,0:T(8,128)(2,1)}, bf16[16,1024]{1,0:T(8,128)(2,1)S(1)}, u32[]{:S(2)}, u32[]{:S(2)}) %collective-permute-start.16) | collective-permute-done | bytes 32800 | tf_op jit(solution)/shard_map/ppermute | solution.py:31
  23.1 0.6 copy-done.14
  23.7 1.5 %beside.4.refs_0_ = bf16[4,16,1024]{2,1,0:T(8,128)(2,1)} custom-call(s32[4]{0:T(128)} %pad_add_fusion.at, bf16[16,1024]{1,0:T(8,128)(2,1)} %order.1.refs_0_, bf16[16,1024]{1,0:T(8,128)(2,1)} %copy-done.12, bf16[16,1024]{1,0:T(8,128)(2,1)} %copy-done.13, bf16[16,1024]{1,0:T(8,128)(2,1)} %copy-done.14), custom_call_target="tpu_custom_call" | custom-call | tf_op jit(solution)/shard_map/beside/pallas_call | solution.py:90
  25.2 1.3 %collective-permute-start.17 = (bf16[4,16,1024]{2,1,0:T(8,128)(2,1)}, bf16[4,16,1024]{2,1,0:T(8,128)(2,1)S(1)}, u32[]{:S(2)}, u32[]{:S(2)}) collective-permute-start(bf16[4,16,1024]{2,1,0:T(8,128)(2,1)} %beside.4.refs_0_), channel_id=1, source_target_pairs={{0,8},{8,16},{16,24},{24,0},{1,9},{9,17},{17,25},{25,1},{2,10},{10... | collective-permute-start | bytes 393224 | tf_op jit(solution)/shard_map/ppermute | solution.py:31
  26.5 1.4 %collective-permute-start.18 = (bf16[4,16,1024]{2,1,0:T(8,128)(2,1)}, bf16[4,16,1024]{2,1,0:T(8,128)(2,1)S(1)}, u32[]{:S(2)}, u32[]{:S(2)}) collective-permute-start(bf16[4,16,1024]{2,1,0:T(8,128)(2,1)} %beside.4.refs_0_), channel_id=1, source_target_pairs={{0,24},{8,0},{16,8},{24,16},{1,25},{9,1},{17,9},{25,17},{2,26},{10... | collective-permute-start | bytes 393224 | tf_op jit(solution)/shard_map/ppermute | solution.py:31
  27.9 1.6 %collective-permute-start.19 = (bf16[4,16,1024]{2,1,0:T(8,128)(2,1)}, bf16[4,16,1024]{2,1,0:T(8,128)(2,1)S(1)}, u32[]{:S(2)}, u32[]{:S(2)}) collective-permute-start(bf16[4,16,1024]{2,1,0:T(8,128)(2,1)} %beside.4.refs_0_), channel_id=1, source_target_pairs={{0,16},{8,24},{16,0},{24,8},{1,17},{9,25},{17,1},{25,9},{2,18},{10... | collective-permute-start | bytes 393224 | tf_op jit(solution)/shard_map/ppermute | solution.py:31
  29.6 0.9 collective-permute-done.17.refs_1_
  30.5 4.1 %collective-permute-done.19.refs_3_ = bf16[4,16,1024]{2,1,0:T(8,128)(2,1)S(1)} collective-permute-done((bf16[4,16,1024]{2,1,0:T(8,128)(2,1)}, bf16[4,16,1024]{2,1,0:T(8,128)(2,1)S(1)}, u32[]{:S(2)}, u32[]{:S(2)}) %collective-permute-start.19) | collective-permute-done | bytes 131104 | tf_op jit(solution)/shard_map/ppermute | solution.py:31
  34.6 0.6 copy-done.9
  35.2 1.9 %beside.5 = bf16[4,4,16,1024]{3,2,1,0:T(8,128)(2,1)} custom-call(s32[4]{0:T(128)} %pad_add_fusion.at, bf16[4,16,1024]{2,1,0:T(8,128)(2,1)} %beside.4.refs_0_, bf16[4,16,1024]{2,1,0:T(8,128)(2,1)} %copy-done.7, bf16[4,16,1024]{2,1,0:T(8,128)(2,1)} %copy-done.8, bf16[4,16,1024]{2,1,0:T(8,128)(2,1)} %copy-done.9), custom_call_target="tpu_custom_call" | custom-call | tf_op jit(solution)/shard_map/beside/pallas_call | solution.py:90
  37.2 1.2 collective-permute-start.20
  38.4 1.4 %collective-permute-start.21 = (bf16[256,1024]{1,0:T(8,128)(2,1)}, bf16[256,1024]{1,0:T(8,128)(2,1)S(1)}, u32[]{:S(2)}, u32[]{:S(2)}) collective-permute-start(bf16[256,1024]{1,0:T(8,128)(2,1)} %bitcast.9), channel_id=1, source_target_pairs={{0,224},{32,0},{64,32},{96,64},{128,96},{160,128},{192,160},{224,1... | collective-permute-start | bytes 1572872 | tf_op jit(solution)/shard_map/ppermute | solution.py:31
  39.8 0.8 copy-done.4
  40.6 2.1 %split.1 = (bf16[4,8,16,896]{3,2,1,0:T(8,128)(2,1)}, bf16[8,16,768]{2,1,0:T(8,128)(2,1)}) custom-call(bf16[8,16,1664]{2,1,0:T(8,128)(2,1)} %bitcast.12), custom_call_target="tpu_custom_call" | custom-call | tf_op jit(solution)/shard_map/split/pallas_call | solution.py:288
  42.8 4.2 %all-to-all-start.1 = ((bf16[4,8,16,896]{3,2,1,0:T(8,128)(2,1)}), bf16[4,8,16,896]{3,2,1,0:T(8,128)(2,1)}, u32[]{:S(2)}, u32[]{:S(2)}) async-start(bf16[4,8,16,896]{3,2,1,0:T(8,128)(2,1)} %get-tuple-element.11), calls=%async_computation.1 | async-start | bytes 1835008 | tf_op jit(solution)/shard_map/all_to_all | solution.py:67
  47.0 2.8 %collective-permute-start.6 = (bf16[8,16,768]{2,1,0:T(8,128)(2,1)}, bf16[8,16,768]{2,1,0:T(8,128)(2,1)S(1)}, u32[]{:S(2)}, u32[]{:S(2)}) collective-permute-start(bf16[8,16,768]{2,1,0:T(8,128)(2,1)} %get-tuple-element.12.refs_0_), channel_id=1, source_target_pairs={{0,24},{8,0},{16,8},{24,16},{1,25},{9,1},{17,9},{25,17},{2,26},{10... | collective-permute-start | bytes 589832 | tf_op jit(solution)/shard_map/ppermute | solution.py:31
  49.9 2.8 %collective-permute-done.6.refs_2_ = bf16[8,16,768]{2,1,0:T(8,128)(2,1)S(1)} collective-permute-done((bf16[8,16,768]{2,1,0:T(8,128)(2,1)}, bf16[8,16,768]{2,1,0:T(8,128)(2,1)S(1)}, u32[]{:S(2)}, u32[]{:S(2)}) %collective-permute-start.6) | collective-permute-done | bytes 196640 | tf_op jit(solution)/shard_map/ppermute | solution.py:31
  52.7 3.1 %collective-permute-start.8 = (bf16[4,16,768]{2,1,0:T(8,128)(2,1)S(1)}, bf16[4,16,768]{2,1,0:T(8,128)(2,1)S(1)}, u32[]{:S(2)}, u32[]{:S(2)}) collective-permute-start(bf16[4,16,768]{2,1,0:T(8,128)(2,1)S(1)} %slice.35), channel_id=1, source_target_pairs={{0,24},{8,0},{16,8},{24,16},{1,25},{9,1},{17,9},{25,17},{2,26},{10... | collective-permute-start | bytes 294920 | tf_op jit(solution)/shard_map/ppermute | solution.py:31
  55.8 1.6 %collective-permute-done.8.refs_4_ = bf16[4,16,768]{2,1,0:T(8,128)(2,1)S(1)} collective-permute-done((bf16[4,16,768]{2,1,0:T(8,128)(2,1)S(1)}, bf16[4,16,768]{2,1,0:T(8,128)(2,1)S(1)}, u32[]{:S(2)}, u32[]{:S(2)}) %collective-permute-start.8) | collective-permute-done | bytes 98336 | tf_op jit(solution)/shard_map/ppermute | solution.py:31
  57.4 0.6 copy-done.11
  58.1 2.2 %beside.3.refs_5_ = bf16[8,4,16,768]{3,2,1,0:T(8,128)(2,1)} custom-call(s32[4]{0:T(128)} %pad_add_fusion.at, bf16[8,16,768]{2,1,0:T(8,128)(2,1)} %get-tuple-element.12.refs_0_, bf16[8,16,768]{2,1,0:T(8,128)(2,1)} %copy-done.5, bf16[8,16,768]{2,1,0:T(8,128)(2,1)} %copy-done.6, bf16[4,16,768]{2,1,0:T(8,128)(2,1)} %copy-done.10, bf16[4,16,768]{2,1,0:T(8,128)(2,1)} %copy-done.11), custom_call_target="tpu_custom_call" | custom-call | tf_op jit(solution)/shard_map/beside/pallas_call | solution.py:90
  60.2 1.6 %collective-permute-start.9 = (bf16[8,4,16,768]{3,2,1,0:T(8,128)(2,1)}, bf16[8,4,16,768]{3,2,1,0:T(8,128)(2,1)}, u32[]{:S(2)}, u32[]{:S(2)}) collective-permute-start(bf16[8,4,16,768]{3,2,1,0:T(8,128)(2,1)} %beside.3.refs_5_), channel_id=1, source_target_pairs={{0,2},{2,4},{4,6},{6,0},{1,3},{3,5},{5,7},{7,1},{8,10},{10,12},{12... | collective-permute-start | bytes 2359304 | tf_op jit(solution)/shard_map/ppermute | solution.py:31
  61.8 1.4 %collective-permute-start.10 = (bf16[8,4,16,768]{3,2,1,0:T(8,128)(2,1)}, bf16[8,4,16,768]{3,2,1,0:T(8,128)(2,1)}, u32[]{:S(2)}, u32[]{:S(2)}) collective-permute-start(bf16[8,4,16,768]{3,2,1,0:T(8,128)(2,1)} %beside.3.refs_5_), channel_id=1, source_target_pairs={{0,6},{2,0},{4,2},{6,4},{1,7},{3,1},{5,3},{7,5},{8,14},{10,8},{12,... | collective-permute-start | bytes 2359304 | tf_op jit(solution)/shard_map/ppermute | solution.py:31
  63.2 1.1 collective-permute-start.23
  64.9 3.0 %collective-permute-start.2 = (bf16[4,8,16,896]{3,2,1,0:T(8,128)(2,1)}, bf16[4,8,16,896]{3,2,1,0:T(8,128)(2,1)S(1)}, u32[]{:S(2)}, u32[]{:S(2)}) collective-permute-start(bf16[4,8,16,896]{3,2,1,0:T(8,128)(2,1)} %all-to-all-done.1.refs_0_), channel_id=1, source_target_pairs={{0,24},{8,0},{16,8},{24,16},{1,25},{9,1},{17,9},{25,17},{2,26},{10... | collective-permute-start | bytes 2752520 | tf_op jit(solution)/shard_map/ppermute | solution.py:31
  67.9 3.8 %collective-permute-done.23.refs_4_ = bf16[256,1024]{1,0:T(8,128)(2,1)S(1)} collective-permute-done((bf16[256,1024]{1,0:T(8,128)(2,1)S(1)}, bf16[256,1024]{1,0:T(8,128)(2,1)S(1)}, u32[]{:S(2)}, u32[]{:S(2)}) %collective-permute-start.23) | collective-permute-done | bytes 524320 | tf_op jit(solution)/shard_map/ppermute | solution.py:31
  71.6 6.2 %collective-permute-start = (bf16[256,2048]{1,0:T(8,128)(2,1)S(1)}, bf16[256,2048]{1,0:T(8,128)(2,1)S(1)}, u32[]{:S(2)}, u32[]{:S(2)}) collective-permute-start(bf16[256,2048]{1,0:T(8,128)(2,1)S(1)} %copy-done.1), channel_id=1, source_target_pairs={{0,1},{1,0},{2,3},{3,2},{4,5},{5,4},{6,7},{7,6},{8,9},{9,8},{10,11... | collective-permute-start | bytes 3145736 | tf_op jit(solution)/shard_map/ppermute | solution.py:31
  78.2 2.6 %collective-permute-start.25 = (bf16[256,1024]{1,0:T(8,128)(2,1)S(1)}, bf16[256,1024]{1,0:T(8,128)(2,1)S(1)}, u32[]{:S(2)}, u32[]{:S(2)}) collective-permute-start(bf16[256,1024]{1,0:T(8,128)(2,1)S(1)} %collective-permute-done.23.refs_4_), channel_id=1, source_target_pairs={{0,224},{32,0},{64,32},{96,64},{128,96},{160,128},{192,160},{224,1... | collective-permute-start | bytes 1572872 | tf_op jit(solution)/shard_map/ppermute | solution.py:31
  80.8 1.0 slice.36
  81.8 1.1 slice.37
  82.9 0.8 collective-permute-start.11
  83.8 2.1 %collective-permute-start.12 = (bf16[4,4,16,768]{3,2,1,0:T(8,128)(2,1)S(1)}, bf16[4,4,16,768]{3,2,1,0:T(8,128)(2,1)S(1)}, u32[]{:S(2)}, u32[]{:S(2)}) collective-permute-start(bf16[4,4,16,768]{3,2,1,0:T(8,128)(2,1)S(1)} %slice.37), channel_id=1, source_target_pairs={{0,6},{2,0},{4,2},{6,4},{1,7},{3,1},{5,3},{7,5},{8,14},{10,8},{12,... | collective-permute-start | bytes 1179656 | tf_op jit(solution)/shard_map/ppermute | solution.py:31
  85.9 2.9 %collective-permute-done.24.refs_5_ = bf16[256,1024]{1,0:T(8,128)(2,1)S(1)} collective-permute-done((bf16[256,1024]{1,0:T(8,128)(2,1)S(1)}, bf16[256,1024]{1,0:T(8,128)(2,1)S(1)}, u32[]{:S(2)}, u32[]{:S(2)}) %collective-permute-start.24) | collective-permute-done | bytes 524320 | tf_op jit(solution)/shard_map/ppermute | solution.py:31
  89.3 2.7 %collective-permute-start.4 = (bf16[2,8,16,896]{3,2,1,0:T(8,128)(2,1)S(1)}, bf16[2,8,16,896]{3,2,1,0:T(8,128)(2,1)S(1)}, u32[]{:S(2)}, u32[]{:S(2)}) collective-permute-start(bf16[2,8,16,896]{3,2,1,0:T(8,128)(2,1)S(1)} %slice.33), channel_id=1, source_target_pairs={{0,24},{8,0},{16,8},{24,16},{1,25},{9,1},{17,9},{25,17},{2,26},{10... | collective-permute-start | bytes 1376264 | tf_op jit(solution)/shard_map/ppermute | solution.py:31
  92.9 4.0 %collective-permute-start.26 = (bf16[128,1024]{1,0:T(8,128)(2,1)S(1)}, bf16[128,1024]{1,0:T(8,128)(2,1)S(1)}, u32[]{:S(2)}, u32[]{:S(2)}) collective-permute-start(bf16[128,1024]{1,0:T(8,128)(2,1)S(1)} %slice.38), channel_id=1, source_target_pairs={{0,32},{32,64},{64,96},{96,128},{128,160},{160,192},{192,224},{224... | collective-permute-start | bytes 786440 | tf_op jit(solution)/shard_map/ppermute | solution.py:31
  96.9 1.0 collective-permute-done.3.refs_3_
  97.9 15.0 %att.1.ctx = bf16[512,1024]{1,0:T(8,128)(2,1)S(1)} custom-call(s32[4]{0:T(128)S(1)} %copy-done.3, bf16[256,2048]{1,0:T(8,128)(2,1)S(1)} %copy-done.1, bf16[256,2048]{1,0:T(8,128)(2,1)S(1)} %collective-permute-done.other, f32[256,128]{1,0:T(8,128)S(1)} %get-tuple-element.17.cos_ref, f32[256,128]{1,0:T(8,128)S(1)} %get-tuple-element.18.sin_ref, ...), custom_call_target="tpu_custom_call" | custom-call | flops 4000000000 | bytes 10000000 | tf_op jit(solution)/shard_map/att/pallas_call | solution.py:309
  113.0 3.6 %project.3 = f32[256,2048]{1,0:T(8,128)S(1)} custom-call(s32[4]{0:T(128)S(1)} %copy-done.3, bf16[512,1024]{1,0:T(8,128)(2,1)S(1)} %att.1.ctx, bf16[256,1024]{1,0:T(8,128)(2,1)S(1)} %bitcast.10, bf16[256,1024]{1,0:T(8,128)(2,1)S(1)} %collective-permute-done.20.refs_1_, bf16[256,1024]{1,0:T(8,128)(2,1)S(1)} %collective-permute-done.21.refs_2_, ...), custom_call_target="tpu_custom_call" | custom-call | flops 1000000000 | bytes 8000000 | tf_op jit(solution)/shard_map/project/pallas_call | solution.py:331
  116.6 5.8 %collective-permute-start.28 = (f32[256,2048]{1,0:T(8,128)S(1)}, f32[256,2048]{1,0:T(8,128)S(1)}, u32[]{:S(2)}, u32[]{:S(2)}) collective-permute-start(f32[256,2048]{1,0:T(8,128)S(1)} %project.3), channel_id=1, source_target_pairs={{0,1},{1,0},{2,3},{3,2},{4,5},{5,4},{6,7},{7,6},{8,9},{9,8},{10,11... | collective-permute-start | bytes 6291464 | tf_op jit(solution)/shard_map/ppermute | solution.py:31
  122.5 3.6 %project.2 = f32[256,2048]{1,0:T(8,128)S(1)} custom-call(s32[4]{0:T(128)S(1)} %copy-done.3, bf16[512,1024]{1,0:T(8,128)(2,1)S(1)} %att.1.ctx, bf16[256,1024]{1,0:T(8,128)(2,1)S(1)} %bitcast.11, bf16[256,1024]{1,0:T(8,128)(2,1)S(1)} %collective-permute-done.20.refs_1_, bf16[256,1024]{1,0:T(8,128)(2,1)S(1)} %collective-permute-done.21.refs_2_, ...), custom_call_target="tpu_custom_call" | custom-call | flops 1000000000 | bytes 8000000 | tf_op jit(solution)/shard_map/project/pallas_call | solution.py:331
  126.2 1.5 %add_convert_fusion = bf16[256,2048]{1,0:T(8,128)(2,1)} fusion(f32[256,2048]{1,0:T(8,128)S(1)} %project.2, f32[256,2048]{1,0:T(8,128)S(1)} %collective-permute-done.28, bf16[256,2048]{1,0:T(8,128)(2,1)S(1)} %copy-done.1), kind=kLoop, calls=%fused_computation | loop fusion | flops 2097152 | bytes 6291456 | tf_op jit(solution)/shard_map/convert_element_type | solution.py:343
  (68 shorter events, 4.4 us)
Async XLA Ops:
  2.3 37.6 %all-to-all-start = ((bf16[16,8,1664]{2,1,0:T(8,128)(2,1)}), bf16[16,8,1664]{2,1,0:T(8,128)(2,1)S(1)}, u32[]{:S(2)}, u32[]{:S(2)}) async-start(bf16[16,8,1664]{2,1,0:T(8,128)(2,1)} %get-tuple-element.10), calls=%async_computation | async-start | bytes 851968 | tf_op jit(solution)/shard_map/all_to_all | solution.py:67
  12.3 1.4 %collective-permute-start.13 = (bf16[8,1024]{1,0:T(8,128)(2,1)}, bf16[8,1024]{1,0:T(8,128)(2,1)S(1)}, u32[]{:S(2)}, u32[]{:S(2)}) collective-permute-start(bf16[8,1024]{1,0:T(8,128)(2,1)} %get-tuple-element.14), channel_id=1, source_target_pairs={{0,1},{1,0},{2,3},{3,2},{4,5},{5,4},{6,7},{7,6},{8,9},{9,8},{10,11... | collective-permute-start | bytes 49160 | tf_op jit(solution)/shard_map/ppermute | solution.py:31
  13.7 0.6 copy-start.15
  15.6 4.5 %collective-permute-start.14 = (bf16[16,1024]{1,0:T(8,128)(2,1)}, bf16[16,1024]{1,0:T(8,128)(2,1)S(1)}, u32[]{:S(2)}, u32[]{:S(2)}) collective-permute-start(bf16[16,1024]{1,0:T(8,128)(2,1)} %order.1.refs_0_), channel_id=1, source_target_pairs={{0,2},{2,4},{4,6},{6,0},{1,3},{3,5},{5,7},{7,1},{8,10},{10,12},{12... | collective-permute-start | bytes 98312 | tf_op jit(solution)/shard_map/ppermute | solution.py:31
  16.8 3.3 %collective-permute-start.15 = (bf16[16,1024]{1,0:T(8,128)(2,1)}, bf16[16,1024]{1,0:T(8,128)(2,1)S(1)}, u32[]{:S(2)}, u32[]{:S(2)}) collective-permute-start(bf16[16,1024]{1,0:T(8,128)(2,1)} %order.1.refs_0_), channel_id=1, source_target_pairs={{0,6},{2,0},{4,2},{6,4},{1,7},{3,1},{5,3},{7,5},{8,14},{10,8},{12,... | collective-permute-start | bytes 98312 | tf_op jit(solution)/shard_map/ppermute | solution.py:31
  18.3 4.8 %collective-permute-start.16 = (bf16[16,1024]{1,0:T(8,128)(2,1)}, bf16[16,1024]{1,0:T(8,128)(2,1)S(1)}, u32[]{:S(2)}, u32[]{:S(2)}) collective-permute-start(bf16[16,1024]{1,0:T(8,128)(2,1)} %order.1.refs_0_), channel_id=1, source_target_pairs={{0,4},{2,6},{4,0},{6,2},{1,5},{3,7},{5,1},{7,3},{8,12},{10,14},{12... | collective-permute-start | bytes 98312 | tf_op jit(solution)/shard_map/ppermute | solution.py:31
  20.1 3.0 %copy-start.12 = (bf16[16,1024]{1,0:T(8,128)(2,1)}, bf16[16,1024]{1,0:T(8,128)(2,1)S(1)}, u32[]{:S(2)}) copy-start(bf16[16,1024]{1,0:T(8,128)(2,1)S(1)} %collective-permute-done.14.refs_1_) | copy-start | bytes 98308
  20.1 3.0 %copy-start.13 = (bf16[16,1024]{1,0:T(8,128)(2,1)}, bf16[16,1024]{1,0:T(8,128)(2,1)S(1)}, u32[]{:S(2)}) copy-start(bf16[16,1024]{1,0:T(8,128)(2,1)S(1)} %collective-permute-done.15.refs_2_) | copy-start | bytes 98308
  23.1 0.6 copy-start.14
  25.2 5.3 %collective-permute-start.17 = (bf16[4,16,1024]{2,1,0:T(8,128)(2,1)}, bf16[4,16,1024]{2,1,0:T(8,128)(2,1)S(1)}, u32[]{:S(2)}, u32[]{:S(2)}) collective-permute-start(bf16[4,16,1024]{2,1,0:T(8,128)(2,1)} %beside.4.refs_0_), channel_id=1, source_target_pairs={{0,8},{8,16},{16,24},{24,0},{1,9},{9,17},{17,25},{25,1},{2,10},{10... | collective-permute-start | bytes 393224 | tf_op jit(solution)/shard_map/ppermute | solution.py:31
  26.5 4.0 %collective-permute-start.18 = (bf16[4,16,1024]{2,1,0:T(8,128)(2,1)}, bf16[4,16,1024]{2,1,0:T(8,128)(2,1)S(1)}, u32[]{:S(2)}, u32[]{:S(2)}) collective-permute-start(bf16[4,16,1024]{2,1,0:T(8,128)(2,1)} %beside.4.refs_0_), channel_id=1, source_target_pairs={{0,24},{8,0},{16,8},{24,16},{1,25},{9,1},{17,9},{25,17},{2,26},{10... | collective-permute-start | bytes 393224 | tf_op jit(solution)/shard_map/ppermute | solution.py:31
  27.9 6.7 %collective-permute-start.19 = (bf16[4,16,1024]{2,1,0:T(8,128)(2,1)}, bf16[4,16,1024]{2,1,0:T(8,128)(2,1)S(1)}, u32[]{:S(2)}, u32[]{:S(2)}) collective-permute-start(bf16[4,16,1024]{2,1,0:T(8,128)(2,1)} %beside.4.refs_0_), channel_id=1, source_target_pairs={{0,16},{8,24},{16,0},{24,8},{1,17},{9,25},{17,1},{25,9},{2,18},{10... | collective-permute-start | bytes 393224 | tf_op jit(solution)/shard_map/ppermute | solution.py:31
  30.5 4.1 %copy-start.7 = (bf16[4,16,1024]{2,1,0:T(8,128)(2,1)}, bf16[4,16,1024]{2,1,0:T(8,128)(2,1)S(1)}, u32[]{:S(2)}) copy-start(bf16[4,16,1024]{2,1,0:T(8,128)(2,1)S(1)} %collective-permute-done.17.refs_1_) | copy-start | bytes 393220
  30.5 4.1 %copy-start.8 = (bf16[4,16,1024]{2,1,0:T(8,128)(2,1)}, bf16[4,16,1024]{2,1,0:T(8,128)(2,1)S(1)}, u32[]{:S(2)}) copy-start(bf16[4,16,1024]{2,1,0:T(8,128)(2,1)S(1)} %collective-permute-done.18.refs_2_) | copy-start | bytes 393220
  34.6 0.6 copy-start.9
  37.2 12.6 %collective-permute-start.20 = (bf16[256,1024]{1,0:T(8,128)(2,1)}, bf16[256,1024]{1,0:T(8,128)(2,1)S(1)}, u32[]{:S(2)}, u32[]{:S(2)}) collective-permute-start(bf16[256,1024]{1,0:T(8,128)(2,1)} %bitcast.8), channel_id=1, source_target_pairs={{0,32},{32,64},{64,96},{96,128},{128,160},{160,192},{192,224},{224... | collective-permute-start | bytes 1572872 | tf_op jit(solution)/shard_map/ppermute | solution.py:31
  38.4 24.8 %collective-permute-start.21 = (bf16[256,1024]{1,0:T(8,128)(2,1)}, bf16[256,1024]{1,0:T(8,128)(2,1)S(1)}, u32[]{:S(2)}, u32[]{:S(2)}) collective-permute-start(bf16[256,1024]{1,0:T(8,128)(2,1)} %bitcast.9), channel_id=1, source_target_pairs={{0,224},{32,0},{64,32},{96,64},{128,96},{160,128},{192,160},{224,1... | collective-permute-start | bytes 1572872 | tf_op jit(solution)/shard_map/ppermute | solution.py:31
  39.8 0.8 copy-start.4
  40.6 31.0 %copy-start.1 = (bf16[256,2048]{1,0:T(8,128)(2,1)S(1)}, bf16[256,2048]{1,0:T(8,128)(2,1)}, u32[]{:S(2)}) copy-start(bf16[256,2048]{1,0:T(8,128)(2,1)} %own.1) | copy-start | bytes 3145732
  42.8 7.0 %collective-permute-start.5 = (bf16[8,16,768]{2,1,0:T(8,128)(2,1)}, bf16[8,16,768]{2,1,0:T(8,128)(2,1)S(1)}, u32[]{:S(2)}, u32[]{:S(2)}) collective-permute-start(bf16[8,16,768]{2,1,0:T(8,128)(2,1)} %get-tuple-element.12.refs_0_), channel_id=1, source_target_pairs={{0,8},{8,16},{16,24},{24,0},{1,9},{9,17},{17,25},{25,1},{2,10},{10... | collective-permute-start | bytes 589832 | tf_op jit(solution)/shard_map/ppermute | solution.py:31
  42.8 21.5 %all-to-all-start.1 = ((bf16[4,8,16,896]{3,2,1,0:T(8,128)(2,1)}), bf16[4,8,16,896]{3,2,1,0:T(8,128)(2,1)}, u32[]{:S(2)}, u32[]{:S(2)}) async-start(bf16[4,8,16,896]{3,2,1,0:T(8,128)(2,1)} %get-tuple-element.11), calls=%async_computation.1 | async-start | bytes 1835008 | tf_op jit(solution)/shard_map/all_to_all | solution.py:67
  47.0 5.7 %collective-permute-start.6 = (bf16[8,16,768]{2,1,0:T(8,128)(2,1)}, bf16[8,16,768]{2,1,0:T(8,128)(2,1)S(1)}, u32[]{:S(2)}, u32[]{:S(2)}) collective-permute-start(bf16[8,16,768]{2,1,0:T(8,128)(2,1)} %get-tuple-element.12.refs_0_), channel_id=1, source_target_pairs={{0,24},{8,0},{16,8},{24,16},{1,25},{9,1},{17,9},{25,17},{2,26},{10... | collective-permute-start | bytes 589832 | tf_op jit(solution)/shard_map/ppermute | solution.py:31
  49.7 15.1 %collective-permute-start.22 = (bf16[256,1024]{1,0:T(8,128)(2,1)S(1)}, bf16[256,1024]{1,0:T(8,128)(2,1)S(1)}, u32[]{:S(2)}, u32[]{:S(2)}) collective-permute-start(bf16[256,1024]{1,0:T(8,128)(2,1)S(1)} %collective-permute-done.20.refs_1_), channel_id=1, source_target_pairs={{0,32},{32,64},{64,96},{96,128},{128,160},{160,192},{192,224},{224... | collective-permute-start | bytes 1572872 | tf_op jit(solution)/shard_map/ppermute | solution.py:31
  49.8 7.6 %copy-start.5 = (bf16[8,16,768]{2,1,0:T(8,128)(2,1)}, bf16[8,16,768]{2,1,0:T(8,128)(2,1)S(1)}, u32[]{:S(2)}) copy-start(bf16[8,16,768]{2,1,0:T(8,128)(2,1)S(1)} %collective-permute-done.5.refs_1_) | copy-start | bytes 589828
  49.8 6.0 %collective-permute-start.7 = (bf16[4,16,768]{2,1,0:T(8,128)(2,1)S(1)}, bf16[4,16,768]{2,1,0:T(8,128)(2,1)S(1)}, u32[]{:S(2)}, u32[]{:S(2)}) collective-permute-start(bf16[4,16,768]{2,1,0:T(8,128)(2,1)S(1)} %slice.34), channel_id=1, source_target_pairs={{0,8},{8,16},{16,24},{24,0},{1,9},{9,17},{17,25},{25,1},{2,10},{10... | collective-permute-start | bytes 294920 | tf_op jit(solution)/shard_map/ppermute | solution.py:31
  52.7 4.7 %copy-start.6 = (bf16[8,16,768]{2,1,0:T(8,128)(2,1)}, bf16[8,16,768]{2,1,0:T(8,128)(2,1)S(1)}, u32[]{:S(2)}) copy-start(bf16[8,16,768]{2,1,0:T(8,128)(2,1)S(1)} %collective-permute-done.6.refs_2_) | copy-start | bytes 589828
  52.7 4.7 %collective-permute-start.8 = (bf16[4,16,768]{2,1,0:T(8,128)(2,1)S(1)}, bf16[4,16,768]{2,1,0:T(8,128)(2,1)S(1)}, u32[]{:S(2)}, u32[]{:S(2)}) collective-permute-start(bf16[4,16,768]{2,1,0:T(8,128)(2,1)S(1)} %slice.35), channel_id=1, source_target_pairs={{0,24},{8,0},{16,8},{24,16},{1,25},{9,1},{17,9},{25,17},{2,26},{10... | collective-permute-start | bytes 294920 | tf_op jit(solution)/shard_map/ppermute | solution.py:31
  55.8 1.6 %copy-start.10 = (bf16[4,16,768]{2,1,0:T(8,128)(2,1)}, bf16[4,16,768]{2,1,0:T(8,128)(2,1)S(1)}, u32[]{:S(2)}) copy-start(bf16[4,16,768]{2,1,0:T(8,128)(2,1)S(1)} %collective-permute-done.7.refs_3_) | copy-start | bytes 294916
  57.4 0.6 copy-start.11
  60.2 17.6 %collective-permute-start.9 = (bf16[8,4,16,768]{3,2,1,0:T(8,128)(2,1)}, bf16[8,4,16,768]{3,2,1,0:T(8,128)(2,1)}, u32[]{:S(2)}, u32[]{:S(2)}) collective-permute-start(bf16[8,4,16,768]{3,2,1,0:T(8,128)(2,1)} %beside.3.refs_5_), channel_id=1, source_target_pairs={{0,2},{2,4},{4,6},{6,0},{1,3},{3,5},{5,7},{7,1},{8,10},{10,12},{12... | collective-permute-start | bytes 2359304 | tf_op jit(solution)/shard_map/ppermute | solution.py:31
  61.8 16.3 %collective-permute-start.10 = (bf16[8,4,16,768]{3,2,1,0:T(8,128)(2,1)}, bf16[8,4,16,768]{3,2,1,0:T(8,128)(2,1)}, u32[]{:S(2)}, u32[]{:S(2)}) collective-permute-start(bf16[8,4,16,768]{3,2,1,0:T(8,128)(2,1)} %beside.3.refs_5_), channel_id=1, source_target_pairs={{0,6},{2,0},{4,2},{6,4},{1,7},{3,1},{5,3},{7,5},{8,14},{10,8},{12,... | collective-permute-start | bytes 2359304 | tf_op jit(solution)/shard_map/ppermute | solution.py:31
  63.2 8.4 %collective-permute-start.23 = (bf16[256,1024]{1,0:T(8,128)(2,1)S(1)}, bf16[256,1024]{1,0:T(8,128)(2,1)S(1)}, u32[]{:S(2)}, u32[]{:S(2)}) collective-permute-start(bf16[256,1024]{1,0:T(8,128)(2,1)S(1)} %collective-permute-done.21.refs_2_), channel_id=1, source_target_pairs={{0,224},{32,0},{64,32},{96,64},{128,96},{160,128},{192,160},{224,1... | collective-permute-start | bytes 1572872 | tf_op jit(solution)/shard_map/ppermute | solution.py:31
  64.3 18.7 %collective-permute-start.1 = (bf16[4,8,16,896]{3,2,1,0:T(8,128)(2,1)}, bf16[4,8,16,896]{3,2,1,0:T(8,128)(2,1)S(1)}, u32[]{:S(2)}, u32[]{:S(2)}) collective-permute-start(bf16[4,8,16,896]{3,2,1,0:T(8,128)(2,1)} %all-to-all-done.1.refs_0_), channel_id=1, source_target_pairs={{0,8},{8,16},{16,24},{24,0},{1,9},{9,17},{17,25},{25,1},{2,10},{10... | collective-permute-start | bytes 2752520 | tf_op jit(solution)/shard_map/ppermute | solution.py:31
  64.9 18.9 %collective-permute-start.2 = (bf16[4,8,16,896]{3,2,1,0:T(8,128)(2,1)}, bf16[4,8,16,896]{3,2,1,0:T(8,128)(2,1)S(1)}, u32[]{:S(2)}, u32[]{:S(2)}) collective-permute-start(bf16[4,8,16,896]{3,2,1,0:T(8,128)(2,1)} %all-to-all-done.1.refs_0_), channel_id=1, source_target_pairs={{0,24},{8,0},{16,8},{24,16},{1,25},{9,1},{17,9},{25,17},{2,26},{10... | collective-permute-start | bytes 2752520 | tf_op jit(solution)/shard_map/ppermute | solution.py:31
  71.6 21.2 %collective-permute-start = (bf16[256,2048]{1,0:T(8,128)(2,1)S(1)}, bf16[256,2048]{1,0:T(8,128)(2,1)S(1)}, u32[]{:S(2)}, u32[]{:S(2)}) collective-permute-start(bf16[256,2048]{1,0:T(8,128)(2,1)S(1)} %copy-done.1), channel_id=1, source_target_pairs={{0,1},{1,0},{2,3},{3,2},{4,5},{5,4},{6,7},{7,6},{8,9},{9,8},{10,11... | collective-permute-start | bytes 3145736 | tf_op jit(solution)/shard_map/ppermute | solution.py:31
  77.9 10.9 %collective-permute-start.24 = (bf16[256,1024]{1,0:T(8,128)(2,1)S(1)}, bf16[256,1024]{1,0:T(8,128)(2,1)S(1)}, u32[]{:S(2)}, u32[]{:S(2)}) collective-permute-start(bf16[256,1024]{1,0:T(8,128)(2,1)S(1)} %collective-permute-done.22.refs_3_), channel_id=1, source_target_pairs={{0,32},{32,64},{64,96},{96,128},{128,160},{160,192},{192,224},{224... | collective-permute-start | bytes 1572872 | tf_op jit(solution)/shard_map/ppermute | solution.py:31
  78.2 11.1 %collective-permute-start.25 = (bf16[256,1024]{1,0:T(8,128)(2,1)S(1)}, bf16[256,1024]{1,0:T(8,128)(2,1)S(1)}, u32[]{:S(2)}, u32[]{:S(2)}) collective-permute-start(bf16[256,1024]{1,0:T(8,128)(2,1)S(1)} %collective-permute-done.23.refs_4_), channel_id=1, source_target_pairs={{0,224},{32,0},{64,32},{96,64},{128,96},{160,128},{192,160},{224,1... | collective-permute-start | bytes 1572872 | tf_op jit(solution)/shard_map/ppermute | solution.py:31
  81.8 16.1 %copy-start.2 = (bf16[8,4,16,768]{3,2,1,0:T(8,128)(2,1)S(1)}, bf16[8,4,16,768]{3,2,1,0:T(8,128)(2,1)}, u32[]{:S(2)}) copy-start(bf16[8,4,16,768]{3,2,1,0:T(8,128)(2,1)} %beside.3.refs_5_) | copy-start | bytes 2359300
  81.8 16.1 %copy-start.3 = (s32[4]{0:T(128)S(1)}, s32[4]{0:T(128)}, u32[]{:S(2)}) copy-start(s32[4]{0:T(128)} %pad_add_fusion.at) | copy-start | bytes 52
  82.9 13.9 %collective-permute-start.11 = (bf16[4,4,16,768]{3,2,1,0:T(8,128)(2,1)S(1)}, bf16[4,4,16,768]{3,2,1,0:T(8,128)(2,1)S(1)}, u32[]{:S(2)}, u32[]{:S(2)}) collective-permute-start(bf16[4,4,16,768]{3,2,1,0:T(8,128)(2,1)S(1)} %slice.36), channel_id=1, source_target_pairs={{0,2},{2,4},{4,6},{6,0},{1,3},{3,5},{5,7},{7,1},{8,10},{10,12},{12... | collective-permute-start | bytes 1179656 | tf_op jit(solution)/shard_map/ppermute | solution.py:31
  83.8 13.1 %collective-permute-start.12 = (bf16[4,4,16,768]{3,2,1,0:T(8,128)(2,1)S(1)}, bf16[4,4,16,768]{3,2,1,0:T(8,128)(2,1)S(1)}, u32[]{:S(2)}, u32[]{:S(2)}) collective-permute-start(bf16[4,4,16,768]{3,2,1,0:T(8,128)(2,1)S(1)} %slice.37), channel_id=1, source_target_pairs={{0,6},{2,0},{4,2},{6,4},{1,7},{3,1},{5,3},{7,5},{8,14},{10,8},{12,... | collective-permute-start | bytes 1179656 | tf_op jit(solution)/shard_map/ppermute | solution.py:31
  88.8 9.1 %collective-permute-start.3 = (bf16[2,8,16,896]{3,2,1,0:T(8,128)(2,1)S(1)}, bf16[2,8,16,896]{3,2,1,0:T(8,128)(2,1)S(1)}, u32[]{:S(2)}, u32[]{:S(2)}) collective-permute-start(bf16[2,8,16,896]{3,2,1,0:T(8,128)(2,1)S(1)} %slice.32), channel_id=1, source_target_pairs={{0,8},{8,16},{16,24},{24,0},{1,9},{9,17},{17,25},{25,1},{2,10},{10... | collective-permute-start | bytes 1376264 | tf_op jit(solution)/shard_map/ppermute | solution.py:31
  89.3 8.6 %collective-permute-start.4 = (bf16[2,8,16,896]{3,2,1,0:T(8,128)(2,1)S(1)}, bf16[2,8,16,896]{3,2,1,0:T(8,128)(2,1)S(1)}, u32[]{:S(2)}, u32[]{:S(2)}) collective-permute-start(bf16[2,8,16,896]{3,2,1,0:T(8,128)(2,1)S(1)} %slice.33), channel_id=1, source_target_pairs={{0,24},{8,0},{16,8},{24,16},{1,25},{9,1},{17,9},{25,17},{2,26},{10... | collective-permute-start | bytes 1376264 | tf_op jit(solution)/shard_map/ppermute | solution.py:31
  92.9 20.1 %collective-permute-start.26 = (bf16[128,1024]{1,0:T(8,128)(2,1)S(1)}, bf16[128,1024]{1,0:T(8,128)(2,1)S(1)}, u32[]{:S(2)}, u32[]{:S(2)}) collective-permute-start(bf16[128,1024]{1,0:T(8,128)(2,1)S(1)} %slice.38), channel_id=1, source_target_pairs={{0,32},{32,64},{64,96},{96,128},{128,160},{160,192},{192,224},{224... | collective-permute-start | bytes 786440 | tf_op jit(solution)/shard_map/ppermute | solution.py:31
  96.9 16.1 %collective-permute-start.27 = (bf16[128,1024]{1,0:T(8,128)(2,1)S(1)}, bf16[128,1024]{1,0:T(8,128)(2,1)S(1)}, u32[]{:S(2)}, u32[]{:S(2)}) collective-permute-start(bf16[128,1024]{1,0:T(8,128)(2,1)S(1)} %slice.39), channel_id=1, source_target_pairs={{0,224},{32,0},{64,32},{96,64},{128,96},{160,128},{192,160},{224,1... | collective-permute-start | bytes 786440 | tf_op jit(solution)/shard_map/ppermute | solution.py:31
  97.9 15.0 %copy-start = (bf16[4,4,16,1024]{3,2,1,0:T(8,128)(2,1)S(1)}, bf16[4,4,16,1024]{3,2,1,0:T(8,128)(2,1)}, u32[]{:S(2)}) copy-start(bf16[4,4,16,1024]{3,2,1,0:T(8,128)(2,1)} %beside.5) | copy-start | bytes 1572868
  116.6 9.6 %collective-permute-start.28 = (f32[256,2048]{1,0:T(8,128)S(1)}, f32[256,2048]{1,0:T(8,128)S(1)}, u32[]{:S(2)}, u32[]{:S(2)}) collective-permute-start(f32[256,2048]{1,0:T(8,128)S(1)} %project.3), channel_id=1, source_target_pairs={{0,1},{1,0},{2,3},{3,2},{4,5},{5,4},{6,7},{7,6},{8,9},{9,8},{10,11... | collective-permute-start | bytes 6291464 | tf_op jit(solution)/shard_map/ppermute | solution.py:31

commit v4 on v3

--- a/solution.py
+++ b/solution.py
@@ -56,13 +56,6 @@
         out[k * rows : (k + 1) * rows, :] = jnp.where(at[0] == k, mine[...], got[...])
 
 
-def split_kernel(by_z, a, b):
-    n, m = a.shape[3], b.shape[2]
-    for k in range(a.shape[0]):
-        a[k] = by_z[:, :, 0:n]
-    b[...] = by_z[:, :, n : n + m]
-
-
 def to_all(array, axes):
     return lax.all_to_all(array, axes, split_axis=0, concat_axis=0, tiled=True)
 
@@ -125,7 +118,7 @@
 
 def attend_kernel(tokens, at, own, other, cos_ref, sin_ref, *refs):
     a_pieces, b_pieces = refs[0:5], refs[5:10]
-    ctx, w_a, w_b, normed, q_s, k_s, v_s, sems = refs[10:]
+    ctx, w_a, w_b, normed, inv_s, q_s, k_s, v_s, sems = refs[10:]
     width = own.shape[1]
     x_at, y_at = at[1], at[2]
     a_copies, b_copies = [], []
@@ -143,6 +136,17 @@
     for c in a_copies:
         c.start()
     n = k_s.shape[1]
+    step = 32
+
+    def inverse(i, _):
+        for s, ref in enumerate((own, other)):
+            start = pl.multiple_of(i * step, step)
+            x = ref[pl.ds(start, step), :].astype(F32)
+            inv = lax.rsqrt(jnp.sum(x * x, axis=1, keepdims=True) * (1.0 / width) + norm_eps)
+            inv_s[pl.ds(s * tokens + start, step), :] = jnp.broadcast_to(inv, (step, PAD))
+        return 0
+
+    lax.fori_loop(0, tokens // step, inverse, 0)
     for c in a_copies:
         c.wait()
     for c in b_copies:
@@ -152,14 +156,13 @@
     lanes = jnp.concatenate(
         [jnp.sum(jnp.where(eye, gain[i], 0.0), axis=0, keepdims=True) for i in range(width // PAD)], axis=1
     )
-    step = 32
 
     def norm(i, _):
         for s, ref in enumerate((own, other)):
             start = pl.multiple_of(i * step, step)
+            to = pl.ds(s * tokens + start, step)
             x = ref[pl.ds(start, step), :].astype(F32)
-            inv = lax.rsqrt(jnp.sum(x * x, axis=1, keepdims=True) * (1.0 / width) + norm_eps)
-            normed[pl.ds(s * tokens + start, step), :] = (x * inv * lanes).astype(BF16)
+            normed[to, :] = (x * inv_s[to, 0:1] * lanes).astype(BF16)
         return 0
 
     lax.fori_loop(0, tokens // step, norm, 0)
@@ -246,16 +249,13 @@
     for c in copies:
         c.wait()
 
-    def one(z, _):
-        out[:, pl.ds(pl.multiple_of(z * rows, rows), rows)] = lax.dot_general(
+    for z in range(8):
+        out[:, z * rows : (z + 1) * rows] = lax.dot_general(
             ctx[seq * tokens : (seq + 1) * tokens, :],
             w_o[z],
             (((1,), (1,)), ((), ())),
             preferred_element_type=F32,
         )
-        return 0
-
-    lax.fori_loop(0, 8, one, 0)
 
 
 def inner(hidden, attn_gain, w_query, w_key, w_value, w_out):
@@ -285,13 +285,8 @@
         name="order",
     )(at, mine, got)
     other = shift(hidden, "c", 1)
-    side_a, side_b = pl.pallas_call(
-        split_kernel,
-        out_shape=(shape_of((4, 8, 2 * rows, cols_a)), shape_of((8, 2 * rows, cols_b))),
-        in_specs=[VMEM],
-        out_specs=(VMEM,) * 2,
-        name="split",
-    )(by_z)
+    side_a = jnp.broadcast_to(by_z[:, :, :cols_a], (4, 8, 2 * rows, cols_a))
+    side_b = by_z[:, :, cols_a:]
     out_x = direct4(at, 1, out_rows, "x")
     out_xy = direct4(at, 2, out_x, "y").reshape(-1, wq)
     out_pieces = ring8(out_xy, "z")
@@ -315,6 +310,7 @@
             pltpu.VMEM((8, 4, 4, 2 * rows, cols_a), BF16),
             pltpu.VMEM((8, 4, 4, 2 * rows, cols_b), BF16),
             pltpu.VMEM((2 * tokens, width), BF16),
+            pltpu.VMEM((2 * tokens, PAD), F32),
             pltpu.VMEM((2 * tokens, wq), BF16),
             pltpu.VMEM((2 * tokens, wkv), BF16),
             pltpu.VMEM((2 * tokens, wkv), BF16),

time: 130 us -> 126 us (0.969)
  Pallas kernels: 33 us -> 28.1 us
  waiting for transfers between devices: 21.7 us -> 24.3 us
    pallas_call x2, Pallas kernels: 7.28 us -> 4.49 us  [project(): pl.pallas_call(functools.partial(project_kernel, seq, tokens), out_shape=...]
    ppermute x29, waiting for transfers between devices: 21.7 us -> 24.3 us  [shift(): return lax.ppermute(array, axis, [(i, (i + by) % n) for i in range(n)])]
    pallas_call x1 -> x0, Pallas kernels: 2.13 us -> none  [inner(): pl.pallas_call(split_kernel, out_shape=(shape_of((4, 8, 2 * rows, cols_a)...]
  transfers between devices with their start and end apart: 31 -> 31, of which waited for: 11 -> 14; matrix products, arithmetic and copies ran while one was open for 2% -> 3% of each run, Pallas kernels for 22% -> 19%
where the time goes in v4:
time: 126 us; the launch traced here: 125 us
  starting transfers between devices  63.1 us (50%)
  Pallas kernels  28.1 us (22%)
  waiting for transfers between devices  24.3 us (19%)
  local copies, waits for them, and re-layouts  5.78 us (5%)
  other arithmetic  2.95 us (2%)
    ppermute x29, starting transfers between devices, shift(): return lax.ppermute(array, axis, [(i, (i + by) % n) for i in range(n)])  48.8 us
    ppermute x29, waiting for transfers between devices, shift(): return lax.ppermute(array, axis, [(i, (i + by) % n) for i in range(n)])  24.3 us
    pallas_call x1, Pallas kernels, inner(): pl.pallas_call(functools.partial(attend_kernel, tokens), out_shape=shape_...  15 us
    all_to_all x2, starting transfers between devices, to_all(): return lax.all_to_all(array, axes, split_axis=0, concat_axis=0, tiled=True)  14.3 us
    pallas_call x3, Pallas kernels, beside(): pl.pallas_call(functools.partial(beside_kernel, dim, 4, slot), out_shape=...  5.57 us
    pallas_call x2, Pallas kernels, project(): pl.pallas_call(functools.partial(project_kernel, seq, tokens), out_shape=...  4.49 us
  transfers between devices with their start and end apart: 31, of which 14 were waited for; matrix products, arithmetic and copies ran while one was open for 3% of the time, Pallas kernels for 19%

profile of v4, /device:TPU:1, one launch (start us, length us, event | category | flops | bytes accessed | tf_op | source)
XLA Modules:
  0.0 124.5 jit_solution(6379734774380587509)
XLA Ops:
  0.0 0.7 pad_add_fusion.at
  0.7 1.7 %halves.1 = (bf16[16,8,1664]{2,1,0:T(8,128)(2,1)}, bf16[8,1024]{1,0:T(8,128)(2,1)}, bf16[8,1024]{1,0:T(8,128)(2,1)}) custom-call(s32[4]{0:T(128)} %pad_add_fusion.at, bf16[1,8]{1,0:T(2,128)(2,1)} %bitcast.15, bf16[8,512]{1,0:T(8,128)(2,1)} %wk.1, bf16[8,512]{1,0:T(8,128)(2,1)} %wv.1, bf16[8,2048]{1,0:T(8,128)(2,1)} %wq.1, bf16[8,2048]{1,0:T(8,128)(2,1)} %bitcast.14), custom_call_target="tpu_custom_call" | custom-call | tf_op jit(solution)/shard_map/halves/pallas_call | solution.py:271
  2.3 10.0 %all-to-all-start = ((bf16[16,8,1664]{2,1,0:T(8,128)(2,1)}), bf16[16,8,1664]{2,1,0:T(8,128)(2,1)S(1)}, u32[]{:S(2)}, u32[]{:S(2)}) async-start(bf16[16,8,1664]{2,1,0:T(8,128)(2,1)} %get-tuple-element.8), calls=%async_computation | async-start | bytes 851968 | tf_op jit(solution)/shard_map/all_to_all | solution.py:60
  12.5 1.2 collective-permute-done.13.got
  14.3 1.4 %order.1.refs_0_ = bf16[16,1024]{1,0:T(8,128)(2,1)} custom-call(s32[4]{0:T(128)} %pad_add_fusion.at, bf16[8,1024]{1,0:T(8,128)(2,1)} %get-tuple-element.9.mine, bf16[8,1024]{1,0:T(8,128)(2,1)} %copy-done.15), custom_call_target="tpu_custom_call" | custom-call | tf_op jit(solution)/shard_map/order/pallas_call | solution.py:280
  15.7 1.2 collective-permute-start.14
  16.9 1.5 %collective-permute-start.15 = (bf16[16,1024]{1,0:T(8,128)(2,1)}, bf16[16,1024]{1,0:T(8,128)(2,1)S(1)}, u32[]{:S(2)}, u32[]{:S(2)}) collective-permute-start(bf16[16,1024]{1,0:T(8,128)(2,1)} %order.1.refs_0_), channel_id=1, source_target_pairs={{0,6},{2,0},{4,2},{6,4},{1,7},{3,1},{5,3},{7,5},{8,14},{10,8},{12,... | collective-permute-start | bytes 98312 | tf_op jit(solution)/shard_map/ppermute | solution.py:31
  18.3 1.5 %collective-permute-start.16 = (bf16[16,1024]{1,0:T(8,128)(2,1)}, bf16[16,1024]{1,0:T(8,128)(2,1)S(1)}, u32[]{:S(2)}, u32[]{:S(2)}) collective-permute-start(bf16[16,1024]{1,0:T(8,128)(2,1)} %order.1.refs_0_), channel_id=1, source_target_pairs={{0,4},{2,6},{4,0},{6,2},{1,5},{3,7},{5,1},{7,3},{8,12},{10,14},{12... | collective-permute-start | bytes 98312 | tf_op jit(solution)/shard_map/ppermute | solution.py:31
  20.1 3.0 %collective-permute-done.16.refs_3_ = bf16[16,1024]{1,0:T(8,128)(2,1)S(1)} collective-permute-done((bf16[16,1024]{1,0:T(8,128)(2,1)}, bf16[16,1024]{1,0:T(8,128)(2,1)S(1)}, u32[]{:S(2)}, u32[]{:S(2)}) %collective-permute-start.16) | collective-permute-done | bytes 32800 | tf_op jit(solution)/shard_map/ppermute | solution.py:31
  23.7 1.5 %beside.4.refs_0_ = bf16[4,16,1024]{2,1,0:T(8,128)(2,1)} custom-call(s32[4]{0:T(128)} %pad_add_fusion.at, bf16[16,1024]{1,0:T(8,128)(2,1)} %order.1.refs_0_, bf16[16,1024]{1,0:T(8,128)(2,1)} %copy-done.12, bf16[16,1024]{1,0:T(8,128)(2,1)} %copy-done.13, bf16[16,1024]{1,0:T(8,128)(2,1)} %copy-done.14), custom_call_target="tpu_custom_call" | custom-call | tf_op jit(solution)/shard_map/beside/pallas_call | solution.py:83
  25.2 1.3 %collective-permute-start.17 = (bf16[4,16,1024]{2,1,0:T(8,128)(2,1)}, bf16[4,16,1024]{2,1,0:T(8,128)(2,1)S(1)}, u32[]{:S(2)}, u32[]{:S(2)}) collective-permute-start(bf16[4,16,1024]{2,1,0:T(8,128)(2,1)} %beside.4.refs_0_), channel_id=1, source_target_pairs={{0,8},{8,16},{16,24},{24,0},{1,9},{9,17},{17,25},{25,1},{2,10},{10... | collective-permute-start | bytes 393224 | tf_op jit(solution)/shard_map/ppermute | solution.py:31
  26.5 1.4 %collective-permute-start.18 = (bf16[4,16,1024]{2,1,0:T(8,128)(2,1)}, bf16[4,16,1024]{2,1,0:T(8,128)(2,1)S(1)}, u32[]{:S(2)}, u32[]{:S(2)}) collective-permute-start(bf16[4,16,1024]{2,1,0:T(8,128)(2,1)} %beside.4.refs_0_), channel_id=1, source_target_pairs={{0,24},{8,0},{16,8},{24,16},{1,25},{9,1},{17,9},{25,17},{2,26},{10... | collective-permute-start | bytes 393224 | tf_op jit(solution)/shard_map/ppermute | solution.py:31
  27.9 1.6 %collective-permute-start.19 = (bf16[4,16,1024]{2,1,0:T(8,128)(2,1)}, bf16[4,16,1024]{2,1,0:T(8,128)(2,1)S(1)}, u32[]{:S(2)}, u32[]{:S(2)}) collective-permute-start(bf16[4,16,1024]{2,1,0:T(8,128)(2,1)} %beside.4.refs_0_), channel_id=1, source_target_pairs={{0,16},{8,24},{16,0},{24,8},{1,17},{9,25},{17,1},{25,9},{2,18},{10... | collective-permute-start | bytes 393224 | tf_op jit(solution)/shard_map/ppermute | solution.py:31
  29.6 0.9 collective-permute-done.17.refs_1_
  30.5 4.1 %collective-permute-done.19.refs_3_ = bf16[4,16,1024]{2,1,0:T(8,128)(2,1)S(1)} collective-permute-done((bf16[4,16,1024]{2,1,0:T(8,128)(2,1)}, bf16[4,16,1024]{2,1,0:T(8,128)(2,1)S(1)}, u32[]{:S(2)}, u32[]{:S(2)}) %collective-permute-start.19) | collective-permute-done | bytes 131104 | tf_op jit(solution)/shard_map/ppermute | solution.py:31
  34.6 0.6 copy-done.9
  35.2 1.9 %beside.5 = bf16[4,4,16,1024]{3,2,1,0:T(8,128)(2,1)} custom-call(s32[4]{0:T(128)} %pad_add_fusion.at, bf16[4,16,1024]{2,1,0:T(8,128)(2,1)} %beside.4.refs_0_, bf16[4,16,1024]{2,1,0:T(8,128)(2,1)} %copy-done.7, bf16[4,16,1024]{2,1,0:T(8,128)(2,1)} %copy-done.8, bf16[4,16,1024]{2,1,0:T(8,128)(2,1)} %copy-done.9), custom_call_target="tpu_custom_call" | custom-call | tf_op jit(solution)/shard_map/beside/pallas_call | solution.py:83
  37.2 1.2 collective-permute-start.20
  38.4 1.4 %collective-permute-start.21 = (bf16[256,1024]{1,0:T(8,128)(2,1)}, bf16[256,1024]{1,0:T(8,128)(2,1)S(1)}, u32[]{:S(2)}, u32[]{:S(2)}) collective-permute-start(bf16[256,1024]{1,0:T(8,128)(2,1)} %bitcast.9), channel_id=1, source_target_pairs={{0,224},{32,0},{64,32},{96,64},{128,96},{160,128},{192,160},{224,1... | collective-permute-start | bytes 1572872 | tf_op jit(solution)/shard_map/ppermute | solution.py:31
  40.0 1.0 broadcast_in_dim.9
  41.0 4.3 %all-to-all-start.1 = ((bf16[4,8,16,896]{3,2,1,0:T(8,128)(2,1)}), bf16[4,8,16,896]{3,2,1,0:T(8,128)(2,1)}, u32[]{:S(2)}, u32[]{:S(2)}) async-start(bf16[4,8,16,896]{3,2,1,0:T(8,128)(2,1)} %broadcast_in_dim.9), calls=%async_computation.1 | async-start | bytes 1835008 | tf_op jit(solution)/shard_map/all_to_all | solution.py:60
  45.4 2.7 %collective-permute-start.6 = (bf16[8,16,768]{2,1,0:T(8,128)(2,1)S(1)}, bf16[8,16,768]{2,1,0:T(8,128)(2,1)S(1)}, u32[]{:S(2)}, u32[]{:S(2)}) collective-permute-start(bf16[8,16,768]{2,1,0:T(8,128)(2,1)S(1)} %slice.43.refs_0_), channel_id=1, source_target_pairs={{0,24},{8,0},{16,8},{24,16},{1,25},{9,1},{17,9},{25,17},{2,26},{10... | collective-permute-start | bytes 589832 | tf_op jit(solution)/shard_map/ppermute | solution.py:31
  48.1 1.6 %collective-permute-done.20.refs_1_ = bf16[256,1024]{1,0:T(8,128)(2,1)S(1)} collective-permute-done((bf16[256,1024]{1,0:T(8,128)(2,1)}, bf16[256,1024]{1,0:T(8,128)(2,1)S(1)}, u32[]{:S(2)}, u32[]{:S(2)}) %collective-permute-start.20) | collective-permute-done | bytes 524320 | tf_op jit(solution)/shard_map/ppermute | solution.py:31
  49.8 0.9 collective-permute-done.6.refs_2_
  50.7 3.3 %collective-permute-start.8 = (bf16[4,16,768]{2,1,0:T(8,128)(2,1)S(1)}, bf16[4,16,768]{2,1,0:T(8,128)(2,1)S(1)}, u32[]{:S(2)}, u32[]{:S(2)}) collective-permute-start(bf16[4,16,768]{2,1,0:T(8,128)(2,1)S(1)} %slice.45), channel_id=1, source_target_pairs={{0,24},{8,0},{16,8},{24,16},{1,25},{9,1},{17,9},{25,17},{2,26},{10... | collective-permute-start | bytes 294920 | tf_op jit(solution)/shard_map/ppermute | solution.py:31
  54.0 0.9 collective-permute-done.7.refs_3_
  54.9 0.8 collective-permute-done.8.refs_4_
  56.3 2.2 %beside.3.refs_5_ = bf16[8,4,16,768]{3,2,1,0:T(8,128)(2,1)} custom-call(s32[4]{0:T(128)} %pad_add_fusion.at, bf16[8,16,768]{2,1,0:T(8,128)(2,1)} %copy-done.4, bf16[8,16,768]{2,1,0:T(8,128)(2,1)} %copy-done.5, bf16[8,16,768]{2,1,0:T(8,128)(2,1)} %copy-done.6, bf16[4,16,768]{2,1,0:T(8,128)(2,1)} %copy-done.10, bf16[4,16,768]{2,1,0:T(8,128)(2,1)} %copy-done.11), custom_call_target="tpu_custom_call" | custom-call | tf_op jit(solution)/shard_map/beside/pallas_call | solution.py:83
  58.5 1.4 %collective-permute-start.9 = (bf16[8,4,16,768]{3,2,1,0:T(8,128)(2,1)}, bf16[8,4,16,768]{3,2,1,0:T(8,128)(2,1)}, u32[]{:S(2)}, u32[]{:S(2)}) collective-permute-start(bf16[8,4,16,768]{3,2,1,0:T(8,128)(2,1)} %beside.3.refs_5_), channel_id=1, source_target_pairs={{0,2},{2,4},{4,6},{6,0},{1,3},{3,5},{5,7},{7,1},{8,10},{10,12},{12... | collective-permute-start | bytes 2359304 | tf_op jit(solution)/shard_map/ppermute | solution.py:31
  59.9 1.5 %collective-permute-start.10 = (bf16[8,4,16,768]{3,2,1,0:T(8,128)(2,1)}, bf16[8,4,16,768]{3,2,1,0:T(8,128)(2,1)}, u32[]{:S(2)}, u32[]{:S(2)}) collective-permute-start(bf16[8,4,16,768]{3,2,1,0:T(8,128)(2,1)} %beside.3.refs_5_), channel_id=1, source_target_pairs={{0,6},{2,0},{4,2},{6,4},{1,7},{3,1},{5,3},{7,5},{8,14},{10,8},{12,... | collective-permute-start | bytes 2359304 | tf_op jit(solution)/shard_map/ppermute | solution.py:31
  61.3 2.3 %collective-permute-start.23 = (bf16[256,1024]{1,0:T(8,128)(2,1)S(1)}, bf16[256,1024]{1,0:T(8,128)(2,1)S(1)}, u32[]{:S(2)}, u32[]{:S(2)}) collective-permute-start(bf16[256,1024]{1,0:T(8,128)(2,1)S(1)} %collective-permute-done.21.refs_2_), channel_id=1, source_target_pairs={{0,224},{32,0},{64,32},{96,64},{128,96},{160,128},{192,160},{224,1... | collective-permute-start | bytes 1572872 | tf_op jit(solution)/shard_map/ppermute | solution.py:31
  63.7 2.7 %collective-permute-start.2 = (bf16[4,8,16,896]{3,2,1,0:T(8,128)(2,1)}, bf16[4,8,16,896]{3,2,1,0:T(8,128)(2,1)S(1)}, u32[]{:S(2)}, u32[]{:S(2)}) collective-permute-start(bf16[4,8,16,896]{3,2,1,0:T(8,128)(2,1)} %all-to-all-done.1.refs_0_), channel_id=1, source_target_pairs={{0,24},{8,0},{16,8},{24,16},{1,25},{9,1},{17,9},{25,17},{2,26},{10... | collective-permute-start | bytes 2752520 | tf_op jit(solution)/shard_map/ppermute | solution.py:31
  66.4 3.8 %collective-permute-done.23.refs_4_ = bf16[256,1024]{1,0:T(8,128)(2,1)S(1)} collective-permute-done((bf16[256,1024]{1,0:T(8,128)(2,1)S(1)}, bf16[256,1024]{1,0:T(8,128)(2,1)S(1)}, u32[]{:S(2)}, u32[]{:S(2)}) %collective-permute-start.23) | collective-permute-done | bytes 524320 | tf_op jit(solution)/shard_map/ppermute | solution.py:31
  70.1 5.9 %collective-permute-start = (bf16[256,2048]{1,0:T(8,128)(2,1)S(1)}, bf16[256,2048]{1,0:T(8,128)(2,1)S(1)}, u32[]{:S(2)}, u32[]{:S(2)}) collective-permute-start(bf16[256,2048]{1,0:T(8,128)(2,1)S(1)} %copy-done.1), channel_id=1, source_target_pairs={{0,1},{1,0},{2,3},{3,2},{4,5},{5,4},{6,7},{7,6},{8,9},{9,8},{10,11... | collective-permute-start | bytes 3145736 | tf_op jit(solution)/shard_map/ppermute | solution.py:31
  76.5 2.8 %collective-permute-start.25 = (bf16[256,1024]{1,0:T(8,128)(2,1)S(1)}, bf16[256,1024]{1,0:T(8,128)(2,1)S(1)}, u32[]{:S(2)}, u32[]{:S(2)}) collective-permute-start(bf16[256,1024]{1,0:T(8,128)(2,1)S(1)} %collective-permute-done.23.refs_4_), channel_id=1, source_target_pairs={{0,224},{32,0},{64,32},{96,64},{128,96},{160,128},{192,160},{224,1... | collective-permute-start | bytes 1572872 | tf_op jit(solution)/shard_map/ppermute | solution.py:31
  79.3 1.0 slice.46
  80.4 1.1 slice.47
  81.9 2.8 %collective-permute-start.12 = (bf16[4,4,16,768]{3,2,1,0:T(8,128)(2,1)S(1)}, bf16[4,4,16,768]{3,2,1,0:T(8,128)(2,1)S(1)}, u32[]{:S(2)}, u32[]{:S(2)}) collective-permute-start(bf16[4,4,16,768]{3,2,1,0:T(8,128)(2,1)S(1)} %slice.47), channel_id=1, source_target_pairs={{0,6},{2,0},{4,2},{6,4},{1,7},{3,1},{5,3},{7,5},{8,14},{10,8},{12,... | collective-permute-start | bytes 1179656 | tf_op jit(solution)/shard_map/ppermute | solution.py:31
  84.7 3.0 %collective-permute-done.24.refs_5_ = bf16[256,1024]{1,0:T(8,128)(2,1)S(1)} collective-permute-done((bf16[256,1024]{1,0:T(8,128)(2,1)S(1)}, bf16[256,1024]{1,0:T(8,128)(2,1)S(1)}, u32[]{:S(2)}, u32[]{:S(2)}) %collective-permute-start.24) | collective-permute-done | bytes 524320 | tf_op jit(solution)/shard_map/ppermute | solution.py:31
  87.7 2.7 %collective-permute-start.4 = (bf16[2,8,16,896]{3,2,1,0:T(8,128)(2,1)S(1)}, bf16[2,8,16,896]{3,2,1,0:T(8,128)(2,1)S(1)}, u32[]{:S(2)}, u32[]{:S(2)}) collective-permute-start(bf16[2,8,16,896]{3,2,1,0:T(8,128)(2,1)S(1)} %slice.42), channel_id=1, source_target_pairs={{0,24},{8,0},{16,8},{24,16},{1,25},{9,1},{17,9},{25,17},{2,26},{10... | collective-permute-start | bytes 1376264 | tf_op jit(solution)/shard_map/ppermute | solution.py:31
  91.2 3.3 %collective-permute-start.26 = (bf16[128,1024]{1,0:T(8,128)(2,1)S(1)}, bf16[128,1024]{1,0:T(8,128)(2,1)S(1)}, u32[]{:S(2)}, u32[]{:S(2)}) collective-permute-start(bf16[128,1024]{1,0:T(8,128)(2,1)S(1)} %slice.48), channel_id=1, source_target_pairs={{0,32},{32,64},{64,96},{96,128},{128,160},{160,192},{192,224},{224... | collective-permute-start | bytes 786440 | tf_op jit(solution)/shard_map/ppermute | solution.py:31
  94.6 2.0 %collective-permute-done.3.refs_3_ = bf16[2,8,16,896]{3,2,1,0:T(8,128)(2,1)S(1)} collective-permute-done((bf16[2,8,16,896]{3,2,1,0:T(8,128)(2,1)S(1)}, bf16[2,8,16,896]{3,2,1,0:T(8,128)(2,1)S(1)}, u32[]{:S(2)}, u32[]{:S(2)}) %collective-permute-start.3) | collective-permute-done | bytes 458784 | tf_op jit(solution)/shard_map/ppermute | solution.py:31
  96.6 15.0 %att.1.ctx = bf16[512,1024]{1,0:T(8,128)(2,1)S(1)} custom-call(s32[4]{0:T(128)S(1)} %copy-done.3, bf16[256,2048]{1,0:T(8,128)(2,1)S(1)} %copy-done.1, bf16[256,2048]{1,0:T(8,128)(2,1)S(1)} %collective-permute-done.other, f32[256,128]{1,0:T(8,128)S(1)} %get-tuple-element.13.cos_ref, f32[256,128]{1,0:T(8,128)S(1)} %get-tuple-element.14.sin_ref, ...), custom_call_target="tpu_custom_call" | custom-call | flops 4000000000 | bytes 10000000 | tf_op jit(solution)/shard_map/att/pallas_call | solution.py:304
  111.6 2.2 %project.3 = f32[256,2048]{1,0:T(8,128)S(1)} custom-call(s32[4]{0:T(128)S(1)} %copy-done.3, bf16[512,1024]{1,0:T(8,128)(2,1)S(1)} %att.1.ctx, bf16[256,1024]{1,0:T(8,128)(2,1)S(1)} %bitcast.10, bf16[256,1024]{1,0:T(8,128)(2,1)S(1)} %collective-permute-done.20.refs_1_, bf16[256,1024]{1,0:T(8,128)(2,1)S(1)} %collective-permute-done.21.refs_2_, ...), custom_call_target="tpu_custom_call" | custom-call | flops 1000000000 | bytes 8000000 | tf_op jit(solution)/shard_map/project/pallas_call | solution.py:327
  113.9 5.4 %collective-permute-start.28 = (f32[256,2048]{1,0:T(8,128)S(1)}, f32[256,2048]{1,0:T(8,128)S(1)}, u32[]{:S(2)}, u32[]{:S(2)}) collective-permute-start(f32[256,2048]{1,0:T(8,128)S(1)} %project.3), channel_id=1, source_target_pairs={{0,1},{1,0},{2,3},{3,2},{4,5},{5,4},{6,7},{7,6},{8,9},{9,8},{10,11... | collective-permute-start | bytes 6291464 | tf_op jit(solution)/shard_map/ppermute | solution.py:31
  119.2 2.2 %project.2 = f32[256,2048]{1,0:T(8,128)S(1)} custom-call(s32[4]{0:T(128)S(1)} %copy-done.3, bf16[512,1024]{1,0:T(8,128)(2,1)S(1)} %att.1.ctx, bf16[256,1024]{1,0:T(8,128)(2,1)S(1)} %bitcast.11, bf16[256,1024]{1,0:T(8,128)(2,1)S(1)} %collective-permute-done.20.refs_1_, bf16[256,1024]{1,0:T(8,128)(2,1)S(1)} %collective-permute-done.21.refs_2_, ...), custom_call_target="tpu_custom_call" | custom-call | flops 1000000000 | bytes 8000000 | tf_op jit(solution)/shard_map/project/pallas_call | solution.py:327
  121.5 1.5 %collective-permute-done.28 = f32[256,2048]{1,0:T(8,128)S(1)} collective-permute-done((f32[256,2048]{1,0:T(8,128)S(1)}, f32[256,2048]{1,0:T(8,128)S(1)}, u32[]{:S(2)}, u32[]{:S(2)}) %collective-permute-start.28) | collective-permute-done | bytes 2097184 | tf_op jit(solution)/shard_map/ppermute | solution.py:31
  123.0 1.5 %add_convert_fusion = bf16[256,2048]{1,0:T(8,128)(2,1)} fusion(f32[256,2048]{1,0:T(8,128)S(1)} %project.2, f32[256,2048]{1,0:T(8,128)S(1)} %collective-permute-done.28, bf16[256,2048]{1,0:T(8,128)(2,1)S(1)} %copy-done.1), kind=kLoop, calls=%fused_computation | loop fusion | flops 2097152 | bytes 6291456 | tf_op jit(solution)/shard_map/convert_element_type | solution.py:339
  (70 shorter events, 4.4 us)
Async XLA Ops:
  2.3 37.5 %all-to-all-start = ((bf16[16,8,1664]{2,1,0:T(8,128)(2,1)}), bf16[16,8,1664]{2,1,0:T(8,128)(2,1)S(1)}, u32[]{:S(2)}, u32[]{:S(2)}) async-start(bf16[16,8,1664]{2,1,0:T(8,128)(2,1)} %get-tuple-element.8), calls=%async_computation | async-start | bytes 851968 | tf_op jit(solution)/shard_map/all_to_all | solution.py:60
  12.3 1.4 %collective-permute-start.13 = (bf16[8,1024]{1,0:T(8,128)(2,1)}, bf16[8,1024]{1,0:T(8,128)(2,1)S(1)}, u32[]{:S(2)}, u32[]{:S(2)}) collective-permute-start(bf16[8,1024]{1,0:T(8,128)(2,1)} %get-tuple-element.10), channel_id=1, source_target_pairs={{0,1},{1,0},{2,3},{3,2},{4,5},{5,4},{6,7},{7,6},{8,9},{9,8},{10,11... | collective-permute-start | bytes 49160 | tf_op jit(solution)/shard_map/ppermute | solution.py:31
  13.7 0.6 copy-start.15
  15.7 4.5 %collective-permute-start.14 = (bf16[16,1024]{1,0:T(8,128)(2,1)}, bf16[16,1024]{1,0:T(8,128)(2,1)S(1)}, u32[]{:S(2)}, u32[]{:S(2)}) collective-permute-start(bf16[16,1024]{1,0:T(8,128)(2,1)} %order.1.refs_0_), channel_id=1, source_target_pairs={{0,2},{2,4},{4,6},{6,0},{1,3},{3,5},{5,7},{7,1},{8,10},{10,12},{12... | collective-permute-start | bytes 98312 | tf_op jit(solution)/shard_map/ppermute | solution.py:31
  16.9 3.3 %collective-permute-start.15 = (bf16[16,1024]{1,0:T(8,128)(2,1)}, bf16[16,1024]{1,0:T(8,128)(2,1)S(1)}, u32[]{:S(2)}, u32[]{:S(2)}) collective-permute-start(bf16[16,1024]{1,0:T(8,128)(2,1)} %order.1.refs_0_), channel_id=1, source_target_pairs={{0,6},{2,0},{4,2},{6,4},{1,7},{3,1},{5,3},{7,5},{8,14},{10,8},{12,... | collective-permute-start | bytes 98312 | tf_op jit(solution)/shard_map/ppermute | solution.py:31
  18.3 4.8 %collective-permute-start.16 = (bf16[16,1024]{1,0:T(8,128)(2,1)}, bf16[16,1024]{1,0:T(8,128)(2,1)S(1)}, u32[]{:S(2)}, u32[]{:S(2)}) collective-permute-start(bf16[16,1024]{1,0:T(8,128)(2,1)} %order.1.refs_0_), channel_id=1, source_target_pairs={{0,4},{2,6},{4,0},{6,2},{1,5},{3,7},{5,1},{7,3},{8,12},{10,14},{12... | collective-permute-start | bytes 98312 | tf_op jit(solution)/shard_map/ppermute | solution.py:31
  20.1 3.0 %copy-start.12 = (bf16[16,1024]{1,0:T(8,128)(2,1)}, bf16[16,1024]{1,0:T(8,128)(2,1)S(1)}, u32[]{:S(2)}) copy-start(bf16[16,1024]{1,0:T(8,128)(2,1)S(1)} %collective-permute-done.14.refs_1_) | copy-start | bytes 98308
  20.1 3.0 %copy-start.13 = (bf16[16,1024]{1,0:T(8,128)(2,1)}, bf16[16,1024]{1,0:T(8,128)(2,1)S(1)}, u32[]{:S(2)}) copy-start(bf16[16,1024]{1,0:T(8,128)(2,1)S(1)} %collective-permute-done.15.refs_2_) | copy-start | bytes 98308
  23.1 0.6 copy-start.14
  25.2 5.3 %collective-permute-start.17 = (bf16[4,16,1024]{2,1,0:T(8,128)(2,1)}, bf16[4,16,1024]{2,1,0:T(8,128)(2,1)S(1)}, u32[]{:S(2)}, u32[]{:S(2)}) collective-permute-start(bf16[4,16,1024]{2,1,0:T(8,128)(2,1)} %beside.4.refs_0_), channel_id=1, source_target_pairs={{0,8},{8,16},{16,24},{24,0},{1,9},{9,17},{17,25},{25,1},{2,10},{10... | collective-permute-start | bytes 393224 | tf_op jit(solution)/shard_map/ppermute | solution.py:31
  26.5 4.0 %collective-permute-start.18 = (bf16[4,16,1024]{2,1,0:T(8,128)(2,1)}, bf16[4,16,1024]{2,1,0:T(8,128)(2,1)S(1)}, u32[]{:S(2)}, u32[]{:S(2)}) collective-permute-start(bf16[4,16,1024]{2,1,0:T(8,128)(2,1)} %beside.4.refs_0_), channel_id=1, source_target_pairs={{0,24},{8,0},{16,8},{24,16},{1,25},{9,1},{17,9},{25,17},{2,26},{10... | collective-permute-start | bytes 393224 | tf_op jit(solution)/shard_map/ppermute | solution.py:31
  27.9 6.7 %collective-permute-start.19 = (bf16[4,16,1024]{2,1,0:T(8,128)(2,1)}, bf16[4,16,1024]{2,1,0:T(8,128)(2,1)S(1)}, u32[]{:S(2)}, u32[]{:S(2)}) collective-permute-start(bf16[4,16,1024]{2,1,0:T(8,128)(2,1)} %beside.4.refs_0_), channel_id=1, source_target_pairs={{0,16},{8,24},{16,0},{24,8},{1,17},{9,25},{17,1},{25,9},{2,18},{10... | collective-permute-start | bytes 393224 | tf_op jit(solution)/shard_map/ppermute | solution.py:31
  30.5 4.1 %copy-start.7 = (bf16[4,16,1024]{2,1,0:T(8,128)(2,1)}, bf16[4,16,1024]{2,1,0:T(8,128)(2,1)S(1)}, u32[]{:S(2)}) copy-start(bf16[4,16,1024]{2,1,0:T(8,128)(2,1)S(1)} %collective-permute-done.17.refs_1_) | copy-start | bytes 393220
  30.5 4.1 %copy-start.8 = (bf16[4,16,1024]{2,1,0:T(8,128)(2,1)}, bf16[4,16,1024]{2,1,0:T(8,128)(2,1)S(1)}, u32[]{:S(2)}) copy-start(bf16[4,16,1024]{2,1,0:T(8,128)(2,1)S(1)} %collective-permute-done.18.refs_2_) | copy-start | bytes 393220
  34.6 0.6 copy-start.9
  37.2 12.5 %collective-permute-start.20 = (bf16[256,1024]{1,0:T(8,128)(2,1)}, bf16[256,1024]{1,0:T(8,128)(2,1)S(1)}, u32[]{:S(2)}, u32[]{:S(2)}) collective-permute-start(bf16[256,1024]{1,0:T(8,128)(2,1)} %bitcast.8), channel_id=1, source_target_pairs={{0,32},{32,64},{64,96},{96,128},{128,160},{160,192},{192,224},{224... | collective-permute-start | bytes 1572872 | tf_op jit(solution)/shard_map/ppermute | solution.py:31
  38.4 22.9 %collective-permute-start.21 = (bf16[256,1024]{1,0:T(8,128)(2,1)}, bf16[256,1024]{1,0:T(8,128)(2,1)S(1)}, u32[]{:S(2)}, u32[]{:S(2)}) collective-permute-start(bf16[256,1024]{1,0:T(8,128)(2,1)} %bitcast.9), channel_id=1, source_target_pairs={{0,224},{32,0},{64,32},{96,64},{128,96},{160,128},{192,160},{224,1... | collective-permute-start | bytes 1572872 | tf_op jit(solution)/shard_map/ppermute | solution.py:31
  39.9 15.8 %copy-start.4 = (bf16[8,16,768]{2,1,0:T(8,128)(2,1)}, bf16[8,16,768]{2,1,0:T(8,128)(2,1)S(1)}, u32[]{:S(2)}) copy-start(bf16[8,16,768]{2,1,0:T(8,128)(2,1)S(1)} %slice.43.refs_0_) | copy-start | bytes 589828
  39.9 9.8 %collective-permute-start.5 = (bf16[8,16,768]{2,1,0:T(8,128)(2,1)S(1)}, bf16[8,16,768]{2,1,0:T(8,128)(2,1)S(1)}, u32[]{:S(2)}, u32[]{:S(2)}) collective-permute-start(bf16[8,16,768]{2,1,0:T(8,128)(2,1)S(1)} %slice.43.refs_0_), channel_id=1, source_target_pairs={{0,8},{8,16},{16,24},{24,0},{1,9},{9,17},{17,25},{25,1},{2,10},{10... | collective-permute-start | bytes 589832 | tf_op jit(solution)/shard_map/ppermute | solution.py:31
  41.0 29.1 %copy-start.1 = (bf16[256,2048]{1,0:T(8,128)(2,1)S(1)}, bf16[256,2048]{1,0:T(8,128)(2,1)}, u32[]{:S(2)}) copy-start(bf16[256,2048]{1,0:T(8,128)(2,1)} %own.1) | copy-start | bytes 3145732
  41.0 22.7 %all-to-all-start.1 = ((bf16[4,8,16,896]{3,2,1,0:T(8,128)(2,1)}), bf16[4,8,16,896]{3,2,1,0:T(8,128)(2,1)}, u32[]{:S(2)}, u32[]{:S(2)}) async-start(bf16[4,8,16,896]{3,2,1,0:T(8,128)(2,1)} %broadcast_in_dim.9), calls=%async_computation.1 | async-start | bytes 1835008 | tf_op jit(solution)/shard_map/all_to_all | solution.py:60
  45.4 5.4 %collective-permute-start.6 = (bf16[8,16,768]{2,1,0:T(8,128)(2,1)S(1)}, bf16[8,16,768]{2,1,0:T(8,128)(2,1)S(1)}, u32[]{:S(2)}, u32[]{:S(2)}) collective-permute-start(bf16[8,16,768]{2,1,0:T(8,128)(2,1)S(1)} %slice.43.refs_0_), channel_id=1, source_target_pairs={{0,24},{8,0},{16,8},{24,16},{1,25},{9,1},{17,9},{25,17},{2,26},{10... | collective-permute-start | bytes 589832 | tf_op jit(solution)/shard_map/ppermute | solution.py:31
  49.7 14.0 %collective-permute-start.22 = (bf16[256,1024]{1,0:T(8,128)(2,1)S(1)}, bf16[256,1024]{1,0:T(8,128)(2,1)S(1)}, u32[]{:S(2)}, u32[]{:S(2)}) collective-permute-start(bf16[256,1024]{1,0:T(8,128)(2,1)S(1)} %collective-permute-done.20.refs_1_), channel_id=1, source_target_pairs={{0,32},{32,64},{64,96},{96,128},{128,160},{160,192},{192,224},{224... | collective-permute-start | bytes 1572872 | tf_op jit(solution)/shard_map/ppermute | solution.py:31
  49.7 6.0 %copy-start.5 = (bf16[8,16,768]{2,1,0:T(8,128)(2,1)}, bf16[8,16,768]{2,1,0:T(8,128)(2,1)S(1)}, u32[]{:S(2)}) copy-start(bf16[8,16,768]{2,1,0:T(8,128)(2,1)S(1)} %collective-permute-done.5.refs_1_) | copy-start | bytes 589828
  49.7 5.2 %collective-permute-start.7 = (bf16[4,16,768]{2,1,0:T(8,128)(2,1)S(1)}, bf16[4,16,768]{2,1,0:T(8,128)(2,1)S(1)}, u32[]{:S(2)}, u32[]{:S(2)}) collective-permute-start(bf16[4,16,768]{2,1,0:T(8,128)(2,1)S(1)} %slice.44), channel_id=1, source_target_pairs={{0,8},{8,16},{16,24},{24,0},{1,9},{9,17},{17,25},{25,1},{2,10},{10... | collective-permute-start | bytes 294920 | tf_op jit(solution)/shard_map/ppermute | solution.py:31
  50.7 5.0 %copy-start.6 = (bf16[8,16,768]{2,1,0:T(8,128)(2,1)}, bf16[8,16,768]{2,1,0:T(8,128)(2,1)S(1)}, u32[]{:S(2)}) copy-start(bf16[8,16,768]{2,1,0:T(8,128)(2,1)S(1)} %collective-permute-done.6.refs_2_) | copy-start | bytes 589828
  50.7 5.0 %collective-permute-start.8 = (bf16[4,16,768]{2,1,0:T(8,128)(2,1)S(1)}, bf16[4,16,768]{2,1,0:T(8,128)(2,1)S(1)}, u32[]{:S(2)}, u32[]{:S(2)}) collective-permute-start(bf16[4,16,768]{2,1,0:T(8,128)(2,1)S(1)} %slice.45), channel_id=1, source_target_pairs={{0,24},{8,0},{16,8},{24,16},{1,25},{9,1},{17,9},{25,17},{2,26},{10... | collective-permute-start | bytes 294920 | tf_op jit(solution)/shard_map/ppermute | solution.py:31
  54.9 0.8 copy-start.10
  55.7 0.6 copy-start.11
  58.5 17.5 %collective-permute-start.9 = (bf16[8,4,16,768]{3,2,1,0:T(8,128)(2,1)}, bf16[8,4,16,768]{3,2,1,0:T(8,128)(2,1)}, u32[]{:S(2)}, u32[]{:S(2)}) collective-permute-start(bf16[8,4,16,768]{3,2,1,0:T(8,128)(2,1)} %beside.3.refs_5_), channel_id=1, source_target_pairs={{0,2},{2,4},{4,6},{6,0},{1,3},{3,5},{5,7},{7,1},{8,10},{10,12},{12... | collective-permute-start | bytes 2359304 | tf_op jit(solution)/shard_map/ppermute | solution.py:31
  59.9 16.6 %collective-permute-start.10 = (bf16[8,4,16,768]{3,2,1,0:T(8,128)(2,1)}, bf16[8,4,16,768]{3,2,1,0:T(8,128)(2,1)}, u32[]{:S(2)}, u32[]{:S(2)}) collective-permute-start(bf16[8,4,16,768]{3,2,1,0:T(8,128)(2,1)} %beside.3.refs_5_), channel_id=1, source_target_pairs={{0,6},{2,0},{4,2},{6,4},{1,7},{3,1},{5,3},{7,5},{8,14},{10,8},{12,... | collective-permute-start | bytes 2359304 | tf_op jit(solution)/shard_map/ppermute | solution.py:31
  61.3 8.8 %collective-permute-start.23 = (bf16[256,1024]{1,0:T(8,128)(2,1)S(1)}, bf16[256,1024]{1,0:T(8,128)(2,1)S(1)}, u32[]{:S(2)}, u32[]{:S(2)}) collective-permute-start(bf16[256,1024]{1,0:T(8,128)(2,1)S(1)} %collective-permute-done.21.refs_2_), channel_id=1, source_target_pairs={{0,224},{32,0},{64,32},{96,64},{128,96},{160,128},{192,160},{224,1... | collective-permute-start | bytes 1572872 | tf_op jit(solution)/shard_map/ppermute | solution.py:31
  63.7 18.1 %collective-permute-start.1 = (bf16[4,8,16,896]{3,2,1,0:T(8,128)(2,1)}, bf16[4,8,16,896]{3,2,1,0:T(8,128)(2,1)S(1)}, u32[]{:S(2)}, u32[]{:S(2)}) collective-permute-start(bf16[4,8,16,896]{3,2,1,0:T(8,128)(2,1)} %all-to-all-done.1.refs_0_), channel_id=1, source_target_pairs={{0,8},{8,16},{16,24},{24,0},{1,9},{9,17},{17,25},{25,1},{2,10},{10... | collective-permute-start | bytes 2752520 | tf_op jit(solution)/shard_map/ppermute | solution.py:31
  63.7 18.2 %collective-permute-start.2 = (bf16[4,8,16,896]{3,2,1,0:T(8,128)(2,1)}, bf16[4,8,16,896]{3,2,1,0:T(8,128)(2,1)S(1)}, u32[]{:S(2)}, u32[]{:S(2)}) collective-permute-start(bf16[4,8,16,896]{3,2,1,0:T(8,128)(2,1)} %all-to-all-done.1.refs_0_), channel_id=1, source_target_pairs={{0,24},{8,0},{16,8},{24,16},{1,25},{9,1},{17,9},{25,17},{2,26},{10... | collective-permute-start | bytes 2752520 | tf_op jit(solution)/shard_map/ppermute | solution.py:31
  70.1 21.1 %collective-permute-start = (bf16[256,2048]{1,0:T(8,128)(2,1)S(1)}, bf16[256,2048]{1,0:T(8,128)(2,1)S(1)}, u32[]{:S(2)}, u32[]{:S(2)}) collective-permute-start(bf16[256,2048]{1,0:T(8,128)(2,1)S(1)} %copy-done.1), channel_id=1, source_target_pairs={{0,1},{1,0},{2,3},{3,2},{4,5},{5,4},{6,7},{7,6},{8,9},{9,8},{10,11... | collective-permute-start | bytes 3145736 | tf_op jit(solution)/shard_map/ppermute | solution.py:31
  76.0 11.7 %collective-permute-start.24 = (bf16[256,1024]{1,0:T(8,128)(2,1)S(1)}, bf16[256,1024]{1,0:T(8,128)(2,1)S(1)}, u32[]{:S(2)}, u32[]{:S(2)}) collective-permute-start(bf16[256,1024]{1,0:T(8,128)(2,1)S(1)} %collective-permute-done.22.refs_3_), channel_id=1, source_target_pairs={{0,32},{32,64},{64,96},{96,128},{128,160},{160,192},{192,224},{224... | collective-permute-start | bytes 1572872 | tf_op jit(solution)/shard_map/ppermute | solution.py:31
  76.5 11.2 %collective-permute-start.25 = (bf16[256,1024]{1,0:T(8,128)(2,1)S(1)}, bf16[256,1024]{1,0:T(8,128)(2,1)S(1)}, u32[]{:S(2)}, u32[]{:S(2)}) collective-permute-start(bf16[256,1024]{1,0:T(8,128)(2,1)S(1)} %collective-permute-done.23.refs_4_), channel_id=1, source_target_pairs={{0,224},{32,0},{64,32},{96,64},{128,96},{160,128},{192,160},{224,1... | collective-permute-start | bytes 1572872 | tf_op jit(solution)/shard_map/ppermute | solution.py:31
  80.3 16.2 %copy-start.2 = (bf16[8,4,16,768]{3,2,1,0:T(8,128)(2,1)S(1)}, bf16[8,4,16,768]{3,2,1,0:T(8,128)(2,1)}, u32[]{:S(2)}) copy-start(bf16[8,4,16,768]{3,2,1,0:T(8,128)(2,1)} %beside.3.refs_5_) | copy-start | bytes 2359300
  80.3 16.2 %copy-start.3 = (s32[4]{0:T(128)S(1)}, s32[4]{0:T(128)}, u32[]{:S(2)}) copy-start(s32[4]{0:T(128)} %pad_add_fusion.at) | copy-start | bytes 52
  81.8 12.7 %collective-permute-start.11 = (bf16[4,4,16,768]{3,2,1,0:T(8,128)(2,1)S(1)}, bf16[4,4,16,768]{3,2,1,0:T(8,128)(2,1)S(1)}, u32[]{:S(2)}, u32[]{:S(2)}) collective-permute-start(bf16[4,4,16,768]{3,2,1,0:T(8,128)(2,1)S(1)} %slice.46), channel_id=1, source_target_pairs={{0,2},{2,4},{4,6},{6,0},{1,3},{3,5},{5,7},{7,1},{8,10},{10,12},{12... | collective-permute-start | bytes 1179656 | tf_op jit(solution)/shard_map/ppermute | solution.py:31
  81.9 12.7 %collective-permute-start.12 = (bf16[4,4,16,768]{3,2,1,0:T(8,128)(2,1)S(1)}, bf16[4,4,16,768]{3,2,1,0:T(8,128)(2,1)S(1)}, u32[]{:S(2)}, u32[]{:S(2)}) collective-permute-start(bf16[4,4,16,768]{3,2,1,0:T(8,128)(2,1)S(1)} %slice.47), channel_id=1, source_target_pairs={{0,6},{2,0},{4,2},{6,4},{1,7},{3,1},{5,3},{7,5},{8,14},{10,8},{12,... | collective-permute-start | bytes 1179656 | tf_op jit(solution)/shard_map/ppermute | solution.py:31
  87.7 8.9 %collective-permute-start.3 = (bf16[2,8,16,896]{3,2,1,0:T(8,128)(2,1)S(1)}, bf16[2,8,16,896]{3,2,1,0:T(8,128)(2,1)S(1)}, u32[]{:S(2)}, u32[]{:S(2)}) collective-permute-start(bf16[2,8,16,896]{3,2,1,0:T(8,128)(2,1)S(1)} %slice.41), channel_id=1, source_target_pairs={{0,8},{8,16},{16,24},{24,0},{1,9},{9,17},{17,25},{25,1},{2,10},{10... | collective-permute-start | bytes 1376264 | tf_op jit(solution)/shard_map/ppermute | solution.py:31
  87.7 8.9 %collective-permute-start.4 = (bf16[2,8,16,896]{3,2,1,0:T(8,128)(2,1)S(1)}, bf16[2,8,16,896]{3,2,1,0:T(8,128)(2,1)S(1)}, u32[]{:S(2)}, u32[]{:S(2)}) collective-permute-start(bf16[2,8,16,896]{3,2,1,0:T(8,128)(2,1)S(1)} %slice.42), channel_id=1, source_target_pairs={{0,24},{8,0},{16,8},{24,16},{1,25},{9,1},{17,9},{25,17},{2,26},{10... | collective-permute-start | bytes 1376264 | tf_op jit(solution)/shard_map/ppermute | solution.py:31
  91.2 20.4 %collective-permute-start.26 = (bf16[128,1024]{1,0:T(8,128)(2,1)S(1)}, bf16[128,1024]{1,0:T(8,128)(2,1)S(1)}, u32[]{:S(2)}, u32[]{:S(2)}) collective-permute-start(bf16[128,1024]{1,0:T(8,128)(2,1)S(1)} %slice.48), channel_id=1, source_target_pairs={{0,32},{32,64},{64,96},{96,128},{128,160},{160,192},{192,224},{224... | collective-permute-start | bytes 786440 | tf_op jit(solution)/shard_map/ppermute | solution.py:31
  94.6 17.0 %collective-permute-start.27 = (bf16[128,1024]{1,0:T(8,128)(2,1)S(1)}, bf16[128,1024]{1,0:T(8,128)(2,1)S(1)}, u32[]{:S(2)}, u32[]{:S(2)}) collective-permute-start(bf16[128,1024]{1,0:T(8,128)(2,1)S(1)} %slice.49), channel_id=1, source_target_pairs={{0,224},{32,0},{64,32},{96,64},{128,96},{160,128},{192,160},{224,1... | collective-permute-start | bytes 786440 | tf_op jit(solution)/shard_map/ppermute | solution.py:31
  96.6 15.0 %copy-start = (bf16[4,4,16,1024]{3,2,1,0:T(8,128)(2,1)S(1)}, bf16[4,4,16,1024]{3,2,1,0:T(8,128)(2,1)}, u32[]{:S(2)}) copy-start(bf16[4,4,16,1024]{3,2,1,0:T(8,128)(2,1)} %beside.5) | copy-start | bytes 1572868
  113.9 9.2 %collective-permute-start.28 = (f32[256,2048]{1,0:T(8,128)S(1)}, f32[256,2048]{1,0:T(8,128)S(1)}, u32[]{:S(2)}, u32[]{:S(2)}) collective-permute-start(f32[256,2048]{1,0:T(8,128)S(1)} %project.3), channel_id=1, source_target_pairs={{0,1},{1,0},{2,3},{3,2},{4,5},{5,4},{6,7},{7,6},{8,9},{9,8},{10,11... | collective-permute-start | bytes 6291464 | tf_op jit(solution)/shard_map/ppermute | solution.py:31

commit v5 on v4

--- a/solution.py
+++ b/solution.py
@@ -13,7 +13,6 @@
 PAD = 128
 AXES = ("z", "y", "x", "c")
 VMEM = pl.BlockSpec(memory_space=pltpu.VMEM)
-SMEM = pl.BlockSpec(memory_space=pltpu.SMEM)
 ANY = pl.BlockSpec(memory_space=pl.ANY)
 F32 = jnp.float32
 BF16 = jnp.bfloat16
@@ -22,6 +21,10 @@
 norm_eps = 1e-05
 
 
+def position():
+    return [lax.axis_index(a) for a in ("c", "x", "y", "z")]
+
+
 def shape_of(dims, dtype=BF16):
     return jax.ShapeDtypeStruct(tuple(dims), dtype)
 
@@ -31,8 +34,8 @@
     return lax.ppermute(array, axis, [(i, (i + by) % n) for i in range(n)])
 
 
-def halves_kernel(at, gain, wk, wv, wq, wo, copies, mine, theirs):
-    core = at[0]
+def halves_kernel(gain, wk, wv, wq, wo, copies, mine, theirs):
+    core = lax.axis_index("c")
     rows = wq.shape[0]
     eye = lax.broadcasted_iota(jnp.int32, (rows, rows), 0) == lax.broadcasted_iota(jnp.int32, (rows, rows), 1)
     column = jnp.sum(jnp.where(eye, gain[...].astype(F32), 0.0), axis=1, keepdims=True)
@@ -50,7 +53,8 @@
     theirs[...] = wo[:, pl.ds(pl.multiple_of((1 - core) * n, 128), n)]
 
 
-def order_kernel(at, mine, got, out):
+def order_kernel(mine, got, out):
+    at = position()
     rows = mine.shape[0]
     for k in range(2):
         out[k * rows : (k + 1) * rows, :] = jnp.where(at[0] == k, mine[...], got[...])
@@ -60,7 +64,8 @@
     return lax.all_to_all(array, axes, split_axis=0, concat_axis=0, tiled=True)
 
 
-def beside_kernel(dim, n, slot, at, *refs):
+def beside_kernel(dim, n, slot, *refs):
+    at = position()
     *pieces, out = refs
     me = at[slot]
     for by, ref in zip((0, n - 1, 1, 2, 2), pieces):
@@ -77,16 +82,16 @@
         out[half : 2 * half, pl.ds(index, 1)] = high[...][:, None]
 
 
-def beside(at, slot, pieces, dim):
+def beside(slot, pieces, dim):
     dims = list(pieces[0].shape)
     dims.insert(dim, 4)
     return pl.pallas_call(
         functools.partial(beside_kernel, dim, 4, slot),
         out_shape=shape_of(dims),
-        in_specs=[SMEM] + [VMEM] * len(pieces),
+        in_specs=[VMEM] * len(pieces),
         out_specs=VMEM,
         name="beside",
-    )(at, *pieces)
+    )(*pieces)
 
 
 def ring4(block, axis):
@@ -98,11 +103,11 @@
     return block, back, ahead, low, high
 
 
-def direct4(at, slot, block, axis):
+def direct4(slot, block, axis):
     back = shift(block, axis, 1)
     ahead = shift(block, axis, -1)
     far = shift(block, axis, 2)
-    return beside(at, slot, (block, back, ahead, far), 0)
+    return beside(slot, (block, back, ahead, far), 0)
 
 
 def ring8(block, axis):
@@ -116,10 +121,11 @@
     return (*pieces, shift(back[:half], axis, 1), shift(ahead[half:], axis, -1))
 
 
-def attend_kernel(tokens, at, own, other, cos_ref, sin_ref, *refs):
+def attend_kernel(tokens, own, other, cos_ref, sin_ref, *refs):
     a_pieces, b_pieces = refs[0:5], refs[5:10]
     ctx, w_a, w_b, normed, inv_s, q_s, k_s, v_s, sems = refs[10:]
     width = own.shape[1]
+    at = position()
     x_at, y_at = at[1], at[2]
     a_copies, b_copies = [], []
     for i, (by, start, size) in enumerate(((0, 0, 1), (3, 0, 1), (1, 0, 1), (2, 0, 2), (2, 1, 2))):
@@ -229,10 +235,10 @@
     lax.fori_loop(0, 2, attend, 0)
 
 
-def project_kernel(seq, tokens, at, ctx, *refs):
+def project_kernel(seq, tokens, ctx, *refs):
     pieces = refs[0:9]
     out, w_o, sems = refs[9:]
-    z_at = at[3]
+    z_at = position()[3]
     rows = w_o.shape[1]
     half = rows // 2
     copies = []
@@ -265,33 +271,32 @@
     cols = wq + 2 * wkv + PAD
     cols_a = 3 * wkv + PAD
     cols_b = cols - cols_a
-    at = jnp.stack([lax.axis_index(a) for a in ("c", "x", "y", "z")]).astype(jnp.int32)
 
     gain = attn_gain[None]
     copies, mine, theirs = pl.pallas_call(
         halves_kernel,
         out_shape=(shape_of((16, rows, cols)), shape_of((rows, wq)), shape_of((rows, wq))),
-        in_specs=[SMEM] + [VMEM] * 5,
+        in_specs=[VMEM] * 5,
         out_specs=(VMEM,) * 3,
         name="halves",
-    )(at, gain, w_key, w_value, w_query, w_out.T)
+    )(gain, w_key, w_value, w_query, w_out.T)
     by_z = to_all(copies, ("z", "c")).reshape(8, 2 * rows, cols)
     got = shift(theirs, "c", 1)
     out_rows = pl.pallas_call(
         order_kernel,
         out_shape=shape_of((2 * rows, wq)),
-        in_specs=[SMEM, VMEM, VMEM],
+        in_specs=[VMEM, VMEM],
         out_specs=VMEM,
         name="order",
-    )(at, mine, got)
+    )(mine, got)
     other = shift(hidden, "c", 1)
     side_a = jnp.broadcast_to(by_z[:, :, :cols_a], (4, 8, 2 * rows, cols_a))
     side_b = by_z[:, :, cols_a:]
-    out_x = direct4(at, 1, out_rows, "x")
-    out_xy = direct4(at, 2, out_x, "y").reshape(-1, wq)
+    out_x = direct4(1, out_rows, "x")
+    out_xy = direct4(2, out_x, "y").reshape(-1, wq)
     out_pieces = ring8(out_xy, "z")
     block_a = to_all(side_a, "x")
-    block_b = beside(at, 2, ring4(side_b, "y"), 1)
+    block_b = beside(2, ring4(side_b, "y"), 1)
     a_pieces = ring4(block_a, "y")
     b_pieces = ring4(block_b, "x")
 
@@ -304,7 +309,7 @@
     context = pl.pallas_call(
         functools.partial(attend_kernel, tokens),
         out_shape=shape_of((2 * tokens, wq)),
-        in_specs=[SMEM] + [VMEM] * 4 + [ANY] * 10,
+        in_specs=[VMEM] * 4 + [ANY] * 10,
         out_specs=VMEM,
         scratch_shapes=[
             pltpu.VMEM((8, 4, 4, 2 * rows, cols_a), BF16),
@@ -321,19 +326,19 @@
         ),
         compiler_params=pltpu.CompilerParams(vmem_limit_bytes=40 * 1024 * 1024),
         name="att",
-    )(at, hidden, other, cos_table, sin_table, *a_pieces, *b_pieces)
+    )(hidden, other, cos_table, sin_table, *a_pieces, *b_pieces)
 
     def project(seq):
         return pl.pallas_call(
             functools.partial(project_kernel, seq, tokens),
             out_shape=shape_of((tokens, width), F32),
-            in_specs=[SMEM, VMEM] + [ANY] * 9,
+            in_specs=[VMEM] + [ANY] * 9,
             out_specs=VMEM,
             scratch_shapes=[pltpu.VMEM((8, width // 8, wq), BF16), pltpu.SemaphoreType.DMA((9,))],
             cost_estimate=pl.CostEstimate(flops=1_000_000_000, bytes_accessed=8_000_000, transcendentals=0),
             compiler_params=pltpu.CompilerParams(vmem_limit_bytes=24 * 1024 * 1024),
             name="project",
-        )(at, context, *out_pieces)
+        )(context, *out_pieces)
 
     from_them = shift(project(1), "c", 1)
     return (hidden.astype(F32) + (project(0) + from_them)).astype(BF16)

time: 126 us -> 124 us (0.984)
  Pallas kernels: 28.1 us -> 26.4 us
    unnamed x32 -> x30, local copies, waits for them, and re-layouts: 2.51 us -> 2.54 us
where the time goes in v5:
time: 124 us; the launch traced here: 123 us
  starting transfers between devices  63.2 us (51%)
  Pallas kernels  26.4 us (21%)
  waiting for transfers between devices  24.8 us (20%)
  local copies, waits for them, and re-layouts  5.81 us (5%)
  other arithmetic  2.25 us (2%)
    ppermute x29, starting transfers between devices, shift(): return lax.ppermute(array, axis, [(i, (i + by) % n) for i in range(n)])  48.9 us
    ppermute x29, waiting for transfers between devices, shift(): return lax.ppermute(array, axis, [(i, (i + by) % n) for i in range(n)])  24.8 us
    pallas_call x1, Pallas kernels, inner(): pl.pallas_call(functools.partial(attend_kernel, tokens), out_shape=shape_...  14.4 us
    all_to_all x2, starting transfers between devices, to_all(): return lax.all_to_all(array, axes, split_axis=0, concat_axis=0, tiled=True)  14.3 us
    pallas_call x3, Pallas kernels, beside(): pl.pallas_call(functools.partial(beside_kernel, dim, 4, slot), out_shape=...  5.55 us
    pallas_call x2, Pallas kernels, project(): pl.pallas_call(functools.partial(project_kernel, seq, tokens), out_shape=...  3.36 us
    unnamed x30, local copies, waits for them, and re-layouts  2.54 us
  transfers between devices with their start and end apart: 31, of which 14 were waited for; matrix products, arithmetic and copies ran while one was open for 3% of the time, Pallas kernels for 19%

profile of v5, /device:TPU:1, one launch (start us, length us, event | category | flops | bytes accessed | tf_op | source)
XLA Modules:
  0.0 122.7 jit_solution(17484416047294877054)
XLA Ops:
  0.0 1.7 %halves.1 = (bf16[16,8,1664]{2,1,0:T(8,128)(2,1)}, bf16[8,1024]{1,0:T(8,128)(2,1)}, bf16[8,1024]{1,0:T(8,128)(2,1)}) custom-call(bf16[1,8]{1,0:T(2,128)(2,1)} %bitcast.11, bf16[8,512]{1,0:T(8,128)(2,1)} %wk.1, bf16[8,512]{1,0:T(8,128)(2,1)} %wv.1, bf16[8,2048]{1,0:T(8,128)(2,1)} %wq.1, bf16[8,2048]{1,0:T(8,128)(2,1)} %bitcast.10), custom_call_target="tpu_custom_call" | custom-call | tf_op jit(solution)/shard_map/halves/pallas_call | solution.py:276
  1.7 10.0 %all-to-all-start = ((bf16[16,8,1664]{2,1,0:T(8,128)(2,1)}), bf16[16,8,1664]{2,1,0:T(8,128)(2,1)S(1)}, u32[]{:S(2)}, u32[]{:S(2)}) async-start(bf16[16,8,1664]{2,1,0:T(8,128)(2,1)} %get-tuple-element.8), calls=%async_computation | async-start | bytes 851968 | tf_op jit(solution)/shard_map/all_to_all | solution.py:64
  11.8 1.2 collective-permute-done.13.got
  13.6 1.3 %order.1.refs_0_ = bf16[16,1024]{1,0:T(8,128)(2,1)} custom-call(bf16[8,1024]{1,0:T(8,128)(2,1)} %get-tuple-element.9.mine, bf16[8,1024]{1,0:T(8,128)(2,1)} %copy-done.14), custom_call_target="tpu_custom_call" | custom-call | tf_op jit(solution)/shard_map/order/pallas_call | solution.py:285
  15.0 1.2 collective-permute-start.14
  16.2 1.5 %collective-permute-start.15 = (bf16[16,1024]{1,0:T(8,128)(2,1)}, bf16[16,1024]{1,0:T(8,128)(2,1)S(1)}, u32[]{:S(2)}, u32[]{:S(2)}) collective-permute-start(bf16[16,1024]{1,0:T(8,128)(2,1)} %order.1.refs_0_), channel_id=1, source_target_pairs={{0,6},{2,0},{4,2},{6,4},{1,7},{3,1},{5,3},{7,5},{8,14},{10,8},{12,... | collective-permute-start | bytes 98312 | tf_op jit(solution)/shard_map/ppermute | solution.py:34
  17.7 1.5 %collective-permute-start.16 = (bf16[16,1024]{1,0:T(8,128)(2,1)}, bf16[16,1024]{1,0:T(8,128)(2,1)S(1)}, u32[]{:S(2)}, u32[]{:S(2)}) collective-permute-start(bf16[16,1024]{1,0:T(8,128)(2,1)} %order.1.refs_0_), channel_id=1, source_target_pairs={{0,4},{2,6},{4,0},{6,2},{1,5},{3,7},{5,1},{7,3},{8,12},{10,14},{12... | collective-permute-start | bytes 98312 | tf_op jit(solution)/shard_map/ppermute | solution.py:34
  19.5 3.0 %collective-permute-done.16.refs_3_ = bf16[16,1024]{1,0:T(8,128)(2,1)S(1)} collective-permute-done((bf16[16,1024]{1,0:T(8,128)(2,1)}, bf16[16,1024]{1,0:T(8,128)(2,1)S(1)}, u32[]{:S(2)}, u32[]{:S(2)}) %collective-permute-start.16) | collective-permute-done | bytes 32800 | tf_op jit(solution)/shard_map/ppermute | solution.py:34
  23.1 1.5 %beside.4.refs_0_ = bf16[4,16,1024]{2,1,0:T(8,128)(2,1)} custom-call(bf16[16,1024]{1,0:T(8,128)(2,1)} %order.1.refs_0_, bf16[16,1024]{1,0:T(8,128)(2,1)} %copy-done.11, bf16[16,1024]{1,0:T(8,128)(2,1)} %copy-done.12, bf16[16,1024]{1,0:T(8,128)(2,1)} %copy-done.13), custom_call_target="tpu_custom_call" | custom-call | tf_op jit(solution)/shard_map/beside/pallas_call | solution.py:88
  24.5 1.3 %collective-permute-start.17 = (bf16[4,16,1024]{2,1,0:T(8,128)(2,1)}, bf16[4,16,1024]{2,1,0:T(8,128)(2,1)S(1)}, u32[]{:S(2)}, u32[]{:S(2)}) collective-permute-start(bf16[4,16,1024]{2,1,0:T(8,128)(2,1)} %beside.4.refs_0_), channel_id=1, source_target_pairs={{0,8},{8,16},{16,24},{24,0},{1,9},{9,17},{17,25},{25,1},{2,10},{10... | collective-permute-start | bytes 393224 | tf_op jit(solution)/shard_map/ppermute | solution.py:34
  25.8 1.4 %collective-permute-start.18 = (bf16[4,16,1024]{2,1,0:T(8,128)(2,1)}, bf16[4,16,1024]{2,1,0:T(8,128)(2,1)S(1)}, u32[]{:S(2)}, u32[]{:S(2)}) collective-permute-start(bf16[4,16,1024]{2,1,0:T(8,128)(2,1)} %beside.4.refs_0_), channel_id=1, source_target_pairs={{0,24},{8,0},{16,8},{24,16},{1,25},{9,1},{17,9},{25,17},{2,26},{10... | collective-permute-start | bytes 393224 | tf_op jit(solution)/shard_map/ppermute | solution.py:34
  27.3 1.6 %collective-permute-start.19 = (bf16[4,16,1024]{2,1,0:T(8,128)(2,1)}, bf16[4,16,1024]{2,1,0:T(8,128)(2,1)S(1)}, u32[]{:S(2)}, u32[]{:S(2)}) collective-permute-start(bf16[4,16,1024]{2,1,0:T(8,128)(2,1)} %beside.4.refs_0_), channel_id=1, source_target_pairs={{0,16},{8,24},{16,0},{24,8},{1,17},{9,25},{17,1},{25,9},{2,18},{10... | collective-permute-start | bytes 393224 | tf_op jit(solution)/shard_map/ppermute | solution.py:34
  28.9 0.9 collective-permute-done.17.refs_1_
  29.9 4.1 %collective-permute-done.19.refs_3_ = bf16[4,16,1024]{2,1,0:T(8,128)(2,1)S(1)} collective-permute-done((bf16[4,16,1024]{2,1,0:T(8,128)(2,1)}, bf16[4,16,1024]{2,1,0:T(8,128)(2,1)S(1)}, u32[]{:S(2)}, u32[]{:S(2)}) %collective-permute-start.19) | collective-permute-done | bytes 131104 | tf_op jit(solution)/shard_map/ppermute | solution.py:34
  33.9 0.7 copy-done.8
  34.6 1.9 %beside.5 = bf16[4,4,16,1024]{3,2,1,0:T(8,128)(2,1)} custom-call(bf16[4,16,1024]{2,1,0:T(8,128)(2,1)} %beside.4.refs_0_, bf16[4,16,1024]{2,1,0:T(8,128)(2,1)} %copy-done.6, bf16[4,16,1024]{2,1,0:T(8,128)(2,1)} %copy-done.7, bf16[4,16,1024]{2,1,0:T(8,128)(2,1)} %copy-done.8), custom_call_target="tpu_custom_call" | custom-call | tf_op jit(solution)/shard_map/beside/pallas_call | solution.py:88
  36.5 1.2 %collective-permute-start.20 = (bf16[256,1024]{1,0:T(8,128)(2,1)}, bf16[256,1024]{1,0:T(8,128)(2,1)S(1)}, u32[]{:S(2)}, u32[]{:S(2)}) collective-permute-start(bf16[256,1024]{1,0:T(8,128)(2,1)} %bitcast.4), channel_id=1, source_target_pairs={{0,32},{32,64},{64,96},{96,128},{128,160},{160,192},{192,224},{224... | collective-permute-start | bytes 1572872 | tf_op jit(solution)/shard_map/ppermute | solution.py:34
  37.7 1.4 %collective-permute-start.21 = (bf16[256,1024]{1,0:T(8,128)(2,1)}, bf16[256,1024]{1,0:T(8,128)(2,1)S(1)}, u32[]{:S(2)}, u32[]{:S(2)}) collective-permute-start(bf16[256,1024]{1,0:T(8,128)(2,1)} %bitcast.5), channel_id=1, source_target_pairs={{0,224},{32,0},{64,32},{96,64},{128,96},{160,128},{192,160},{224,1... | collective-permute-start | bytes 1572872 | tf_op jit(solution)/shard_map/ppermute | solution.py:34
  39.3 1.0 broadcast_in_dim.9
  40.3 4.4 %all-to-all-start.1 = ((bf16[4,8,16,896]{3,2,1,0:T(8,128)(2,1)}), bf16[4,8,16,896]{3,2,1,0:T(8,128)(2,1)}, u32[]{:S(2)}, u32[]{:S(2)}) async-start(bf16[4,8,16,896]{3,2,1,0:T(8,128)(2,1)} %broadcast_in_dim.9), calls=%async_computation.1 | async-start | bytes 1835008 | tf_op jit(solution)/shard_map/all_to_all | solution.py:64
  44.7 2.7 %collective-permute-start.6 = (bf16[8,16,768]{2,1,0:T(8,128)(2,1)S(1)}, bf16[8,16,768]{2,1,0:T(8,128)(2,1)S(1)}, u32[]{:S(2)}, u32[]{:S(2)}) collective-permute-start(bf16[8,16,768]{2,1,0:T(8,128)(2,1)S(1)} %slice.43.refs_0_), channel_id=1, source_target_pairs={{0,24},{8,0},{16,8},{24,16},{1,25},{9,1},{17,9},{25,17},{2,26},{10... | collective-permute-start | bytes 589832 | tf_op jit(solution)/shard_map/ppermute | solution.py:34
  47.4 1.6 %collective-permute-done.20.refs_1_ = bf16[256,1024]{1,0:T(8,128)(2,1)S(1)} collective-permute-done((bf16[256,1024]{1,0:T(8,128)(2,1)}, bf16[256,1024]{1,0:T(8,128)(2,1)S(1)}, u32[]{:S(2)}, u32[]{:S(2)}) %collective-permute-start.20) | collective-permute-done | bytes 524320 | tf_op jit(solution)/shard_map/ppermute | solution.py:34
  49.2 0.9 collective-permute-done.6.refs_2_
  50.1 3.3 %collective-permute-start.8 = (bf16[4,16,768]{2,1,0:T(8,128)(2,1)S(1)}, bf16[4,16,768]{2,1,0:T(8,128)(2,1)S(1)}, u32[]{:S(2)}, u32[]{:S(2)}) collective-permute-start(bf16[4,16,768]{2,1,0:T(8,128)(2,1)S(1)} %slice.45), channel_id=1, source_target_pairs={{0,24},{8,0},{16,8},{24,16},{1,25},{9,1},{17,9},{25,17},{2,26},{10... | collective-permute-start | bytes 294920 | tf_op jit(solution)/shard_map/ppermute | solution.py:34
  53.4 0.9 collective-permute-done.7.refs_3_
  54.2 0.8 collective-permute-done.8.refs_4_
  55.0 0.6 copy-done.10
  55.7 2.2 %beside.3.refs_5_ = bf16[8,4,16,768]{3,2,1,0:T(8,128)(2,1)} custom-call(bf16[8,16,768]{2,1,0:T(8,128)(2,1)} %copy-done.3, bf16[8,16,768]{2,1,0:T(8,128)(2,1)} %copy-done.4, bf16[8,16,768]{2,1,0:T(8,128)(2,1)} %copy-done.5, bf16[4,16,768]{2,1,0:T(8,128)(2,1)} %copy-done.9, bf16[4,16,768]{2,1,0:T(8,128)(2,1)} %copy-done.10), custom_call_target="tpu_custom_call" | custom-call | tf_op jit(solution)/shard_map/beside/pallas_call | solution.py:88
  57.8 1.4 %collective-permute-start.9 = (bf16[8,4,16,768]{3,2,1,0:T(8,128)(2,1)}, bf16[8,4,16,768]{3,2,1,0:T(8,128)(2,1)}, u32[]{:S(2)}, u32[]{:S(2)}) collective-permute-start(bf16[8,4,16,768]{3,2,1,0:T(8,128)(2,1)} %beside.3.refs_5_), channel_id=1, source_target_pairs={{0,2},{2,4},{4,6},{6,0},{1,3},{3,5},{5,7},{7,1},{8,10},{10,12},{12... | collective-permute-start | bytes 2359304 | tf_op jit(solution)/shard_map/ppermute | solution.py:34
  59.2 1.5 %collective-permute-start.10 = (bf16[8,4,16,768]{3,2,1,0:T(8,128)(2,1)}, bf16[8,4,16,768]{3,2,1,0:T(8,128)(2,1)}, u32[]{:S(2)}, u32[]{:S(2)}) collective-permute-start(bf16[8,4,16,768]{3,2,1,0:T(8,128)(2,1)} %beside.3.refs_5_), channel_id=1, source_target_pairs={{0,6},{2,0},{4,2},{6,4},{1,7},{3,1},{5,3},{7,5},{8,14},{10,8},{12,... | collective-permute-start | bytes 2359304 | tf_op jit(solution)/shard_map/ppermute | solution.py:34
  60.7 2.3 %collective-permute-start.23 = (bf16[256,1024]{1,0:T(8,128)(2,1)S(1)}, bf16[256,1024]{1,0:T(8,128)(2,1)S(1)}, u32[]{:S(2)}, u32[]{:S(2)}) collective-permute-start(bf16[256,1024]{1,0:T(8,128)(2,1)S(1)} %collective-permute-done.21.refs_2_), channel_id=1, source_target_pairs={{0,224},{32,0},{64,32},{96,64},{128,96},{160,128},{192,160},{224,1... | collective-permute-start | bytes 1572872 | tf_op jit(solution)/shard_map/ppermute | solution.py:34
  63.0 2.7 %collective-permute-start.2 = (bf16[4,8,16,896]{3,2,1,0:T(8,128)(2,1)}, bf16[4,8,16,896]{3,2,1,0:T(8,128)(2,1)S(1)}, u32[]{:S(2)}, u32[]{:S(2)}) collective-permute-start(bf16[4,8,16,896]{3,2,1,0:T(8,128)(2,1)} %all-to-all-done.1.refs_0_), channel_id=1, source_target_pairs={{0,24},{8,0},{16,8},{24,16},{1,25},{9,1},{17,9},{25,17},{2,26},{10... | collective-permute-start | bytes 2752520 | tf_op jit(solution)/shard_map/ppermute | solution.py:34
  65.7 3.8 %collective-permute-done.23.refs_4_ = bf16[256,1024]{1,0:T(8,128)(2,1)S(1)} collective-permute-done((bf16[256,1024]{1,0:T(8,128)(2,1)S(1)}, bf16[256,1024]{1,0:T(8,128)(2,1)S(1)}, u32[]{:S(2)}, u32[]{:S(2)}) %collective-permute-start.23) | collective-permute-done | bytes 524320 | tf_op jit(solution)/shard_map/ppermute | solution.py:34
  69.5 5.9 %collective-permute-start = (bf16[256,2048]{1,0:T(8,128)(2,1)S(1)}, bf16[256,2048]{1,0:T(8,128)(2,1)S(1)}, u32[]{:S(2)}, u32[]{:S(2)}) collective-permute-start(bf16[256,2048]{1,0:T(8,128)(2,1)S(1)} %copy-done.1), channel_id=1, source_target_pairs={{0,1},{1,0},{2,3},{3,2},{4,5},{5,4},{6,7},{7,6},{8,9},{9,8},{10,11... | collective-permute-start | bytes 3145736 | tf_op jit(solution)/shard_map/ppermute | solution.py:34
  75.8 2.8 %collective-permute-start.25 = (bf16[256,1024]{1,0:T(8,128)(2,1)S(1)}, bf16[256,1024]{1,0:T(8,128)(2,1)S(1)}, u32[]{:S(2)}, u32[]{:S(2)}) collective-permute-start(bf16[256,1024]{1,0:T(8,128)(2,1)S(1)} %collective-permute-done.23.refs_4_), channel_id=1, source_target_pairs={{0,224},{32,0},{64,32},{96,64},{128,96},{160,128},{192,160},{224,1... | collective-permute-start | bytes 1572872 | tf_op jit(solution)/shard_map/ppermute | solution.py:34
  78.7 1.0 slice.46
  79.7 1.1 slice.47
  81.2 2.8 %collective-permute-start.12 = (bf16[4,4,16,768]{3,2,1,0:T(8,128)(2,1)S(1)}, bf16[4,4,16,768]{3,2,1,0:T(8,128)(2,1)S(1)}, u32[]{:S(2)}, u32[]{:S(2)}) collective-permute-start(bf16[4,4,16,768]{3,2,1,0:T(8,128)(2,1)S(1)} %slice.47), channel_id=1, source_target_pairs={{0,6},{2,0},{4,2},{6,4},{1,7},{3,1},{5,3},{7,5},{8,14},{10,8},{12,... | collective-permute-start | bytes 1179656 | tf_op jit(solution)/shard_map/ppermute | solution.py:34
  84.0 3.0 %collective-permute-done.24.refs_5_ = bf16[256,1024]{1,0:T(8,128)(2,1)S(1)} collective-permute-done((bf16[256,1024]{1,0:T(8,128)(2,1)S(1)}, bf16[256,1024]{1,0:T(8,128)(2,1)S(1)}, u32[]{:S(2)}, u32[]{:S(2)}) %collective-permute-start.24) | collective-permute-done | bytes 524320 | tf_op jit(solution)/shard_map/ppermute | solution.py:34
  87.0 2.7 %collective-permute-start.4 = (bf16[2,8,16,896]{3,2,1,0:T(8,128)(2,1)S(1)}, bf16[2,8,16,896]{3,2,1,0:T(8,128)(2,1)S(1)}, u32[]{:S(2)}, u32[]{:S(2)}) collective-permute-start(bf16[2,8,16,896]{3,2,1,0:T(8,128)(2,1)S(1)} %slice.42), channel_id=1, source_target_pairs={{0,24},{8,0},{16,8},{24,16},{1,25},{9,1},{17,9},{25,17},{2,26},{10... | collective-permute-start | bytes 1376264 | tf_op jit(solution)/shard_map/ppermute | solution.py:34
  90.6 3.4 %collective-permute-start.26 = (bf16[128,1024]{1,0:T(8,128)(2,1)S(1)}, bf16[128,1024]{1,0:T(8,128)(2,1)S(1)}, u32[]{:S(2)}, u32[]{:S(2)}) collective-permute-start(bf16[128,1024]{1,0:T(8,128)(2,1)S(1)} %slice.48), channel_id=1, source_target_pairs={{0,32},{32,64},{64,96},{96,128},{128,160},{160,192},{192,224},{224... | collective-permute-start | bytes 786440 | tf_op jit(solution)/shard_map/ppermute | solution.py:34
  94.0 1.9 %collective-permute-done.3.refs_3_ = bf16[2,8,16,896]{3,2,1,0:T(8,128)(2,1)S(1)} collective-permute-done((bf16[2,8,16,896]{3,2,1,0:T(8,128)(2,1)S(1)}, bf16[2,8,16,896]{3,2,1,0:T(8,128)(2,1)S(1)}, u32[]{:S(2)}, u32[]{:S(2)}) %collective-permute-start.3) | collective-permute-done | bytes 458784 | tf_op jit(solution)/shard_map/ppermute | solution.py:34
  95.9 14.4 %att.1.ctx = bf16[512,1024]{1,0:T(8,128)(2,1)S(1)} custom-call(bf16[256,2048]{1,0:T(8,128)(2,1)S(1)} %copy-done.1, bf16[256,2048]{1,0:T(8,128)(2,1)S(1)} %collective-permute-done.other, f32[256,128]{1,0:T(8,128)S(1)} %get-tuple-element.13.cos_ref, f32[256,128]{1,0:T(8,128)S(1)} %get-tuple-element.14.sin_ref, bf16[4,8,16,896]{3,2,1,0:T(8,128)(2,1)} %all-to-all-done.1.refs_0_, ...), custom_call_target="tpu_custom_call" | custom-call | flops 4000000000 | bytes 10000000 | tf_op jit(solution)/shard_map/att/pallas_call | solution.py:309
  110.4 1.7 %project.3 = f32[256,2048]{1,0:T(8,128)S(1)} custom-call(bf16[512,1024]{1,0:T(8,128)(2,1)S(1)} %att.1.ctx, bf16[256,1024]{1,0:T(8,128)(2,1)S(1)} %bitcast.6, bf16[256,1024]{1,0:T(8,128)(2,1)S(1)} %collective-permute-done.20.refs_1_, bf16[256,1024]{1,0:T(8,128)(2,1)S(1)} %collective-permute-done.21.refs_2_, ...), custom_call_target="tpu_custom_call" | custom-call | flops 1000000000 | bytes 8000000 | tf_op jit(solution)/shard_map/project/pallas_call | solution.py:332
  112.1 5.4 %collective-permute-start.28 = (f32[256,2048]{1,0:T(8,128)S(1)}, f32[256,2048]{1,0:T(8,128)S(1)}, u32[]{:S(2)}, u32[]{:S(2)}) collective-permute-start(f32[256,2048]{1,0:T(8,128)S(1)} %project.3), channel_id=1, source_target_pairs={{0,1},{1,0},{2,3},{3,2},{4,5},{5,4},{6,7},{7,6},{8,9},{9,8},{10,11... | collective-permute-start | bytes 6291464 | tf_op jit(solution)/shard_map/ppermute | solution.py:34
  117.5 1.7 %project.2 = f32[256,2048]{1,0:T(8,128)S(1)} custom-call(bf16[512,1024]{1,0:T(8,128)(2,1)S(1)} %att.1.ctx, bf16[256,1024]{1,0:T(8,128)(2,1)S(1)} %bitcast.7, bf16[256,1024]{1,0:T(8,128)(2,1)S(1)} %collective-permute-done.20.refs_1_, bf16[256,1024]{1,0:T(8,128)(2,1)S(1)} %collective-permute-done.21.refs_2_, ...), custom_call_target="tpu_custom_call" | custom-call | flops 1000000000 | bytes 8000000 | tf_op jit(solution)/shard_map/project/pallas_call | solution.py:332
  119.1 2.1 %collective-permute-done.28 = f32[256,2048]{1,0:T(8,128)S(1)} collective-permute-done((f32[256,2048]{1,0:T(8,128)S(1)}, f32[256,2048]{1,0:T(8,128)S(1)}, u32[]{:S(2)}, u32[]{:S(2)}) %collective-permute-start.28) | collective-permute-done | bytes 2097184 | tf_op jit(solution)/shard_map/ppermute | solution.py:34
  121.2 1.5 %add_convert_fusion = bf16[256,2048]{1,0:T(8,128)(2,1)} fusion(f32[256,2048]{1,0:T(8,128)S(1)} %project.2, f32[256,2048]{1,0:T(8,128)S(1)} %collective-permute-done.28, bf16[256,2048]{1,0:T(8,128)(2,1)S(1)} %copy-done.1), kind=kLoop, calls=%fused_computation | loop fusion | flops 2097152 | bytes 6291456 | tf_op jit(solution)/shard_map/convert_element_type | solution.py:344
  (67 shorter events, 3.8 us)
Async XLA Ops:
  1.7 37.5 %all-to-all-start = ((bf16[16,8,1664]{2,1,0:T(8,128)(2,1)}), bf16[16,8,1664]{2,1,0:T(8,128)(2,1)S(1)}, u32[]{:S(2)}, u32[]{:S(2)}) async-start(bf16[16,8,1664]{2,1,0:T(8,128)(2,1)} %get-tuple-element.8), calls=%async_computation | async-start | bytes 851968 | tf_op jit(solution)/shard_map/all_to_all | solution.py:64
  11.6 1.4 %collective-permute-start.13 = (bf16[8,1024]{1,0:T(8,128)(2,1)}, bf16[8,1024]{1,0:T(8,128)(2,1)S(1)}, u32[]{:S(2)}, u32[]{:S(2)}) collective-permute-start(bf16[8,1024]{1,0:T(8,128)(2,1)} %get-tuple-element.10), channel_id=1, source_target_pairs={{0,1},{1,0},{2,3},{3,2},{4,5},{5,4},{6,7},{7,6},{8,9},{9,8},{10,11... | collective-permute-start | bytes 49160 | tf_op jit(solution)/shard_map/ppermute | solution.py:34
  13.0 0.6 copy-start.14
  15.0 4.5 %collective-permute-start.14 = (bf16[16,1024]{1,0:T(8,128)(2,1)}, bf16[16,1024]{1,0:T(8,128)(2,1)S(1)}, u32[]{:S(2)}, u32[]{:S(2)}) collective-permute-start(bf16[16,1024]{1,0:T(8,128)(2,1)} %order.1.refs_0_), channel_id=1, source_target_pairs={{0,2},{2,4},{4,6},{6,0},{1,3},{3,5},{5,7},{7,1},{8,10},{10,12},{12... | collective-permute-start | bytes 98312 | tf_op jit(solution)/shard_map/ppermute | solution.py:34
  16.2 3.3 %collective-permute-start.15 = (bf16[16,1024]{1,0:T(8,128)(2,1)}, bf16[16,1024]{1,0:T(8,128)(2,1)S(1)}, u32[]{:S(2)}, u32[]{:S(2)}) collective-permute-start(bf16[16,1024]{1,0:T(8,128)(2,1)} %order.1.refs_0_), channel_id=1, source_target_pairs={{0,6},{2,0},{4,2},{6,4},{1,7},{3,1},{5,3},{7,5},{8,14},{10,8},{12,... | collective-permute-start | bytes 98312 | tf_op jit(solution)/shard_map/ppermute | solution.py:34
  17.7 4.8 %collective-permute-start.16 = (bf16[16,1024]{1,0:T(8,128)(2,1)}, bf16[16,1024]{1,0:T(8,128)(2,1)S(1)}, u32[]{:S(2)}, u32[]{:S(2)}) collective-permute-start(bf16[16,1024]{1,0:T(8,128)(2,1)} %order.1.refs_0_), channel_id=1, source_target_pairs={{0,4},{2,6},{4,0},{6,2},{1,5},{3,7},{5,1},{7,3},{8,12},{10,14},{12... | collective-permute-start | bytes 98312 | tf_op jit(solution)/shard_map/ppermute | solution.py:34
  19.5 3.0 %copy-start.11 = (bf16[16,1024]{1,0:T(8,128)(2,1)}, bf16[16,1024]{1,0:T(8,128)(2,1)S(1)}, u32[]{:S(2)}) copy-start(bf16[16,1024]{1,0:T(8,128)(2,1)S(1)} %collective-permute-done.14.refs_1_) | copy-start | bytes 98308
  19.5 3.0 %copy-start.12 = (bf16[16,1024]{1,0:T(8,128)(2,1)}, bf16[16,1024]{1,0:T(8,128)(2,1)S(1)}, u32[]{:S(2)}) copy-start(bf16[16,1024]{1,0:T(8,128)(2,1)S(1)} %collective-permute-done.15.refs_2_) | copy-start | bytes 98308
  22.4 0.6 copy-start.13
  24.5 5.3 %collective-permute-start.17 = (bf16[4,16,1024]{2,1,0:T(8,128)(2,1)}, bf16[4,16,1024]{2,1,0:T(8,128)(2,1)S(1)}, u32[]{:S(2)}, u32[]{:S(2)}) collective-permute-start(bf16[4,16,1024]{2,1,0:T(8,128)(2,1)} %beside.4.refs_0_), channel_id=1, source_target_pairs={{0,8},{8,16},{16,24},{24,0},{1,9},{9,17},{17,25},{25,1},{2,10},{10... | collective-permute-start | bytes 393224 | tf_op jit(solution)/shard_map/ppermute | solution.py:34
  25.8 4.0 %collective-permute-start.18 = (bf16[4,16,1024]{2,1,0:T(8,128)(2,1)}, bf16[4,16,1024]{2,1,0:T(8,128)(2,1)S(1)}, u32[]{:S(2)}, u32[]{:S(2)}) collective-permute-start(bf16[4,16,1024]{2,1,0:T(8,128)(2,1)} %beside.4.refs_0_), channel_id=1, source_target_pairs={{0,24},{8,0},{16,8},{24,16},{1,25},{9,1},{17,9},{25,17},{2,26},{10... | collective-permute-start | bytes 393224 | tf_op jit(solution)/shard_map/ppermute | solution.py:34
  27.3 6.7 %collective-permute-start.19 = (bf16[4,16,1024]{2,1,0:T(8,128)(2,1)}, bf16[4,16,1024]{2,1,0:T(8,128)(2,1)S(1)}, u32[]{:S(2)}, u32[]{:S(2)}) collective-permute-start(bf16[4,16,1024]{2,1,0:T(8,128)(2,1)} %beside.4.refs_0_), channel_id=1, source_target_pairs={{0,16},{8,24},{16,0},{24,8},{1,17},{9,25},{17,1},{25,9},{2,18},{10... | collective-permute-start | bytes 393224 | tf_op jit(solution)/shard_map/ppermute | solution.py:34
  29.8 4.1 %copy-start.6 = (bf16[4,16,1024]{2,1,0:T(8,128)(2,1)}, bf16[4,16,1024]{2,1,0:T(8,128)(2,1)S(1)}, u32[]{:S(2)}) copy-start(bf16[4,16,1024]{2,1,0:T(8,128)(2,1)S(1)} %collective-permute-done.17.refs_1_) | copy-start | bytes 393220
  29.8 4.1 %copy-start.7 = (bf16[4,16,1024]{2,1,0:T(8,128)(2,1)}, bf16[4,16,1024]{2,1,0:T(8,128)(2,1)S(1)}, u32[]{:S(2)}) copy-start(bf16[4,16,1024]{2,1,0:T(8,128)(2,1)S(1)} %collective-permute-done.18.refs_2_) | copy-start | bytes 393220
  33.9 0.7 copy-start.8
  36.5 12.5 %collective-permute-start.20 = (bf16[256,1024]{1,0:T(8,128)(2,1)}, bf16[256,1024]{1,0:T(8,128)(2,1)S(1)}, u32[]{:S(2)}, u32[]{:S(2)}) collective-permute-start(bf16[256,1024]{1,0:T(8,128)(2,1)} %bitcast.4), channel_id=1, source_target_pairs={{0,32},{32,64},{64,96},{96,128},{128,160},{160,192},{192,224},{224... | collective-permute-start | bytes 1572872 | tf_op jit(solution)/shard_map/ppermute | solution.py:34
  37.7 22.9 %collective-permute-start.21 = (bf16[256,1024]{1,0:T(8,128)(2,1)}, bf16[256,1024]{1,0:T(8,128)(2,1)S(1)}, u32[]{:S(2)}, u32[]{:S(2)}) collective-permute-start(bf16[256,1024]{1,0:T(8,128)(2,1)} %bitcast.5), channel_id=1, source_target_pairs={{0,224},{32,0},{64,32},{96,64},{128,96},{160,128},{192,160},{224,1... | collective-permute-start | bytes 1572872 | tf_op jit(solution)/shard_map/ppermute | solution.py:34
  39.2 15.8 %copy-start.3 = (bf16[8,16,768]{2,1,0:T(8,128)(2,1)}, bf16[8,16,768]{2,1,0:T(8,128)(2,1)S(1)}, u32[]{:S(2)}) copy-start(bf16[8,16,768]{2,1,0:T(8,128)(2,1)S(1)} %slice.43.refs_0_) | copy-start | bytes 589828
  39.2 9.8 %collective-permute-start.5 = (bf16[8,16,768]{2,1,0:T(8,128)(2,1)S(1)}, bf16[8,16,768]{2,1,0:T(8,128)(2,1)S(1)}, u32[]{:S(2)}, u32[]{:S(2)}) collective-permute-start(bf16[8,16,768]{2,1,0:T(8,128)(2,1)S(1)} %slice.43.refs_0_), channel_id=1, source_target_pairs={{0,8},{8,16},{16,24},{24,0},{1,9},{9,17},{17,25},{25,1},{2,10},{10... | collective-permute-start | bytes 589832 | tf_op jit(solution)/shard_map/ppermute | solution.py:34
  40.3 29.2 %copy-start.1 = (bf16[256,2048]{1,0:T(8,128)(2,1)S(1)}, bf16[256,2048]{1,0:T(8,128)(2,1)}, u32[]{:S(2)}) copy-start(bf16[256,2048]{1,0:T(8,128)(2,1)} %own.1) | copy-start | bytes 3145732
  40.3 22.7 %all-to-all-start.1 = ((bf16[4,8,16,896]{3,2,1,0:T(8,128)(2,1)}), bf16[4,8,16,896]{3,2,1,0:T(8,128)(2,1)}, u32[]{:S(2)}, u32[]{:S(2)}) async-start(bf16[4,8,16,896]{3,2,1,0:T(8,128)(2,1)} %broadcast_in_dim.9), calls=%async_computation.1 | async-start | bytes 1835008 | tf_op jit(solution)/shard_map/all_to_all | solution.py:64
  44.7 5.4 %collective-permute-start.6 = (bf16[8,16,768]{2,1,0:T(8,128)(2,1)S(1)}, bf16[8,16,768]{2,1,0:T(8,128)(2,1)S(1)}, u32[]{:S(2)}, u32[]{:S(2)}) collective-permute-start(bf16[8,16,768]{2,1,0:T(8,128)(2,1)S(1)} %slice.43.refs_0_), channel_id=1, source_target_pairs={{0,24},{8,0},{16,8},{24,16},{1,25},{9,1},{17,9},{25,17},{2,26},{10... | collective-permute-start | bytes 589832 | tf_op jit(solution)/shard_map/ppermute | solution.py:34
  49.0 14.0 %collective-permute-start.22 = (bf16[256,1024]{1,0:T(8,128)(2,1)S(1)}, bf16[256,1024]{1,0:T(8,128)(2,1)S(1)}, u32[]{:S(2)}, u32[]{:S(2)}) collective-permute-start(bf16[256,1024]{1,0:T(8,128)(2,1)S(1)} %collective-permute-done.20.refs_1_), channel_id=1, source_target_pairs={{0,32},{32,64},{64,96},{96,128},{128,160},{160,192},{192,224},{224... | collective-permute-start | bytes 1572872 | tf_op jit(solution)/shard_map/ppermute | solution.py:34
  49.0 6.0 %copy-start.4 = (bf16[8,16,768]{2,1,0:T(8,128)(2,1)}, bf16[8,16,768]{2,1,0:T(8,128)(2,1)S(1)}, u32[]{:S(2)}) copy-start(bf16[8,16,768]{2,1,0:T(8,128)(2,1)S(1)} %collective-permute-done.5.refs_1_) | copy-start | bytes 589828
  49.1 5.2 %collective-permute-start.7 = (bf16[4,16,768]{2,1,0:T(8,128)(2,1)S(1)}, bf16[4,16,768]{2,1,0:T(8,128)(2,1)S(1)}, u32[]{:S(2)}, u32[]{:S(2)}) collective-permute-start(bf16[4,16,768]{2,1,0:T(8,128)(2,1)S(1)} %slice.44), channel_id=1, source_target_pairs={{0,8},{8,16},{16,24},{24,0},{1,9},{9,17},{17,25},{25,1},{2,10},{10... | collective-permute-start | bytes 294920 | tf_op jit(solution)/shard_map/ppermute | solution.py:34
  50.1 5.0 %copy-start.5 = (bf16[8,16,768]{2,1,0:T(8,128)(2,1)}, bf16[8,16,768]{2,1,0:T(8,128)(2,1)S(1)}, u32[]{:S(2)}) copy-start(bf16[8,16,768]{2,1,0:T(8,128)(2,1)S(1)} %collective-permute-done.6.refs_2_) | copy-start | bytes 589828
  50.1 4.9 %collective-permute-start.8 = (bf16[4,16,768]{2,1,0:T(8,128)(2,1)S(1)}, bf16[4,16,768]{2,1,0:T(8,128)(2,1)S(1)}, u32[]{:S(2)}, u32[]{:S(2)}) collective-permute-start(bf16[4,16,768]{2,1,0:T(8,128)(2,1)S(1)} %slice.45), channel_id=1, source_target_pairs={{0,24},{8,0},{16,8},{24,16},{1,25},{9,1},{17,9},{25,17},{2,26},{10... | collective-permute-start | bytes 294920 | tf_op jit(solution)/shard_map/ppermute | solution.py:34
  54.2 0.8 copy-start.9
  55.0 0.6 copy-start.10
  57.8 17.5 %collective-permute-start.9 = (bf16[8,4,16,768]{3,2,1,0:T(8,128)(2,1)}, bf16[8,4,16,768]{3,2,1,0:T(8,128)(2,1)}, u32[]{:S(2)}, u32[]{:S(2)}) collective-permute-start(bf16[8,4,16,768]{3,2,1,0:T(8,128)(2,1)} %beside.3.refs_5_), channel_id=1, source_target_pairs={{0,2},{2,4},{4,6},{6,0},{1,3},{3,5},{5,7},{7,1},{8,10},{10,12},{12... | collective-permute-start | bytes 2359304 | tf_op jit(solution)/shard_map/ppermute | solution.py:34
  59.2 16.6 %collective-permute-start.10 = (bf16[8,4,16,768]{3,2,1,0:T(8,128)(2,1)}, bf16[8,4,16,768]{3,2,1,0:T(8,128)(2,1)}, u32[]{:S(2)}, u32[]{:S(2)}) collective-permute-start(bf16[8,4,16,768]{3,2,1,0:T(8,128)(2,1)} %beside.3.refs_5_), channel_id=1, source_target_pairs={{0,6},{2,0},{4,2},{6,4},{1,7},{3,1},{5,3},{7,5},{8,14},{10,8},{12,... | collective-permute-start | bytes 2359304 | tf_op jit(solution)/shard_map/ppermute | solution.py:34
  60.7 8.8 %collective-permute-start.23 = (bf16[256,1024]{1,0:T(8,128)(2,1)S(1)}, bf16[256,1024]{1,0:T(8,128)(2,1)S(1)}, u32[]{:S(2)}, u32[]{:S(2)}) collective-permute-start(bf16[256,1024]{1,0:T(8,128)(2,1)S(1)} %collective-permute-done.21.refs_2_), channel_id=1, source_target_pairs={{0,224},{32,0},{64,32},{96,64},{128,96},{160,128},{192,160},{224,1... | collective-permute-start | bytes 1572872 | tf_op jit(solution)/shard_map/ppermute | solution.py:34
  63.0 18.1 %collective-permute-start.1 = (bf16[4,8,16,896]{3,2,1,0:T(8,128)(2,1)}, bf16[4,8,16,896]{3,2,1,0:T(8,128)(2,1)S(1)}, u32[]{:S(2)}, u32[]{:S(2)}) collective-permute-start(bf16[4,8,16,896]{3,2,1,0:T(8,128)(2,1)} %all-to-all-done.1.refs_0_), channel_id=1, source_target_pairs={{0,8},{8,16},{16,24},{24,0},{1,9},{9,17},{17,25},{25,1},{2,10},{10... | collective-permute-start | bytes 2752520 | tf_op jit(solution)/shard_map/ppermute | solution.py:34
  63.0 18.2 %collective-permute-start.2 = (bf16[4,8,16,896]{3,2,1,0:T(8,128)(2,1)}, bf16[4,8,16,896]{3,2,1,0:T(8,128)(2,1)S(1)}, u32[]{:S(2)}, u32[]{:S(2)}) collective-permute-start(bf16[4,8,16,896]{3,2,1,0:T(8,128)(2,1)} %all-to-all-done.1.refs_0_), channel_id=1, source_target_pairs={{0,24},{8,0},{16,8},{24,16},{1,25},{9,1},{17,9},{25,17},{2,26},{10... | collective-permute-start | bytes 2752520 | tf_op jit(solution)/shard_map/ppermute | solution.py:34
  69.5 21.1 %collective-permute-start = (bf16[256,2048]{1,0:T(8,128)(2,1)S(1)}, bf16[256,2048]{1,0:T(8,128)(2,1)S(1)}, u32[]{:S(2)}, u32[]{:S(2)}) collective-permute-start(bf16[256,2048]{1,0:T(8,128)(2,1)S(1)} %copy-done.1), channel_id=1, source_target_pairs={{0,1},{1,0},{2,3},{3,2},{4,5},{5,4},{6,7},{7,6},{8,9},{9,8},{10,11... | collective-permute-start | bytes 3145736 | tf_op jit(solution)/shard_map/ppermute | solution.py:34
  75.4 11.7 %collective-permute-start.24 = (bf16[256,1024]{1,0:T(8,128)(2,1)S(1)}, bf16[256,1024]{1,0:T(8,128)(2,1)S(1)}, u32[]{:S(2)}, u32[]{:S(2)}) collective-permute-start(bf16[256,1024]{1,0:T(8,128)(2,1)S(1)} %collective-permute-done.22.refs_3_), channel_id=1, source_target_pairs={{0,32},{32,64},{64,96},{96,128},{128,160},{160,192},{192,224},{224... | collective-permute-start | bytes 1572872 | tf_op jit(solution)/shard_map/ppermute | solution.py:34
  75.8 11.2 %collective-permute-start.25 = (bf16[256,1024]{1,0:T(8,128)(2,1)S(1)}, bf16[256,1024]{1,0:T(8,128)(2,1)S(1)}, u32[]{:S(2)}, u32[]{:S(2)}) collective-permute-start(bf16[256,1024]{1,0:T(8,128)(2,1)S(1)} %collective-permute-done.23.refs_4_), channel_id=1, source_target_pairs={{0,224},{32,0},{64,32},{96,64},{128,96},{160,128},{192,160},{224,1... | collective-permute-start | bytes 1572872 | tf_op jit(solution)/shard_map/ppermute | solution.py:34
  79.7 16.2 %copy-start.2 = (bf16[8,4,16,768]{3,2,1,0:T(8,128)(2,1)S(1)}, bf16[8,4,16,768]{3,2,1,0:T(8,128)(2,1)}, u32[]{:S(2)}) copy-start(bf16[8,4,16,768]{3,2,1,0:T(8,128)(2,1)} %beside.3.refs_5_) | copy-start | bytes 2359300
  81.2 12.8 %collective-permute-start.11 = (bf16[4,4,16,768]{3,2,1,0:T(8,128)(2,1)S(1)}, bf16[4,4,16,768]{3,2,1,0:T(8,128)(2,1)S(1)}, u32[]{:S(2)}, u32[]{:S(2)}) collective-permute-start(bf16[4,4,16,768]{3,2,1,0:T(8,128)(2,1)S(1)} %slice.46), channel_id=1, source_target_pairs={{0,2},{2,4},{4,6},{6,0},{1,3},{3,5},{5,7},{7,1},{8,10},{10,12},{12... | collective-permute-start | bytes 1179656 | tf_op jit(solution)/shard_map/ppermute | solution.py:34
  81.2 12.7 %collective-permute-start.12 = (bf16[4,4,16,768]{3,2,1,0:T(8,128)(2,1)S(1)}, bf16[4,4,16,768]{3,2,1,0:T(8,128)(2,1)S(1)}, u32[]{:S(2)}, u32[]{:S(2)}) collective-permute-start(bf16[4,4,16,768]{3,2,1,0:T(8,128)(2,1)S(1)} %slice.47), channel_id=1, source_target_pairs={{0,6},{2,0},{4,2},{6,4},{1,7},{3,1},{5,3},{7,5},{8,14},{10,8},{12,... | collective-permute-start | bytes 1179656 | tf_op jit(solution)/shard_map/ppermute | solution.py:34
  87.0 8.9 %collective-permute-start.3 = (bf16[2,8,16,896]{3,2,1,0:T(8,128)(2,1)S(1)}, bf16[2,8,16,896]{3,2,1,0:T(8,128)(2,1)S(1)}, u32[]{:S(2)}, u32[]{:S(2)}) collective-permute-start(bf16[2,8,16,896]{3,2,1,0:T(8,128)(2,1)S(1)} %slice.41), channel_id=1, source_target_pairs={{0,8},{8,16},{16,24},{24,0},{1,9},{9,17},{17,25},{25,1},{2,10},{10... | collective-permute-start | bytes 1376264 | tf_op jit(solution)/shard_map/ppermute | solution.py:34
  87.0 8.9 %collective-permute-start.4 = (bf16[2,8,16,896]{3,2,1,0:T(8,128)(2,1)S(1)}, bf16[2,8,16,896]{3,2,1,0:T(8,128)(2,1)S(1)}, u32[]{:S(2)}, u32[]{:S(2)}) collective-permute-start(bf16[2,8,16,896]{3,2,1,0:T(8,128)(2,1)S(1)} %slice.42), channel_id=1, source_target_pairs={{0,24},{8,0},{16,8},{24,16},{1,25},{9,1},{17,9},{25,17},{2,26},{10... | collective-permute-start | bytes 1376264 | tf_op jit(solution)/shard_map/ppermute | solution.py:34
  90.6 19.8 %collective-permute-start.26 = (bf16[128,1024]{1,0:T(8,128)(2,1)S(1)}, bf16[128,1024]{1,0:T(8,128)(2,1)S(1)}, u32[]{:S(2)}, u32[]{:S(2)}) collective-permute-start(bf16[128,1024]{1,0:T(8,128)(2,1)S(1)} %slice.48), channel_id=1, source_target_pairs={{0,32},{32,64},{64,96},{96,128},{128,160},{160,192},{192,224},{224... | collective-permute-start | bytes 786440 | tf_op jit(solution)/shard_map/ppermute | solution.py:34
  93.9 16.4 %collective-permute-start.27 = (bf16[128,1024]{1,0:T(8,128)(2,1)S(1)}, bf16[128,1024]{1,0:T(8,128)(2,1)S(1)}, u32[]{:S(2)}, u32[]{:S(2)}) collective-permute-start(bf16[128,1024]{1,0:T(8,128)(2,1)S(1)} %slice.49), channel_id=1, source_target_pairs={{0,224},{32,0},{64,32},{96,64},{128,96},{160,128},{192,160},{224,1... | collective-permute-start | bytes 786440 | tf_op jit(solution)/shard_map/ppermute | solution.py:34
  95.9 14.5 %copy-start = (bf16[4,4,16,1024]{3,2,1,0:T(8,128)(2,1)S(1)}, bf16[4,4,16,1024]{3,2,1,0:T(8,128)(2,1)}, u32[]{:S(2)}) copy-start(bf16[4,4,16,1024]{3,2,1,0:T(8,128)(2,1)} %beside.5) | copy-start | bytes 1572868
  112.1 9.2 %collective-permute-start.28 = (f32[256,2048]{1,0:T(8,128)S(1)}, f32[256,2048]{1,0:T(8,128)S(1)}, u32[]{:S(2)}, u32[]{:S(2)}) collective-permute-start(f32[256,2048]{1,0:T(8,128)S(1)} %project.3), channel_id=1, source_target_pairs={{0,1},{1,0},{2,3},{3,2},{4,5},{5,4},{6,7},{7,6},{8,9},{9,8},{10,11... | collective-permute-start | bytes 6291464 | tf_op jit(solution)/shard_map/ppermute | solution.py:34
